TPU v7x, 32 devices: a whole 2x2x4 slice. The times are simulated.
32 devices in a mesh: site: 8 (over z, x), dom: 4 (over y, core).
Axes of the slice: x: 2, y: 2, z: 4, core: 2. Of those that a mesh axis runs over, the one named last changes fastest.
Arguments:
- top_partial: float32 [16, 61, 4, 8192], P(None, None, 'dom', 'site'), may hold values from 0.001 to 1
- bottom_partial: float32 [16, 61, 4, 8192], P(None, None, 'dom', 'site'), may hold values from 0.001 to 1
- left_vectors: float32 [256, 61, 61], P('dom'), may hold values from 0.05 to 1
- right_vectors: float32 [256, 61, 61], P('dom'), may hold values from 0.05 to 1
- decay_rates: float32 [256, 61], P('dom'), may hold values from 0.05 to 8
- state_weights: float32 [256, 61], P('dom'), may hold values from 0.002 to 0.05
- part_rates: float32 [256], P('dom'), may hold values from 0.3 to 3
- branch_lengths: float32 [1997], replicated, may hold values from 0.02 to 0.5
- pattern_weights: int32 [4, 8192], P('dom', 'site'), may hold values from 0 to 9
- block_partition: int32 [4, 64], P('dom', 'site'), may hold values from 0 to 255
- chosen_branches: int32 [16], replicated, may hold values from 0 to 1996, as said below
Outputs:
- site_loglik: float32 [16, 4, 8192], P(None, 'dom', 'site')
- part_derivs: float32 [2, 16, 256], P(None, None, 'dom')
- new_lengths: float32 [1997], replicated
Inputs may be any that keep to these rules, and one draw needn't show every extreme that they name: `chosen_branches`: distinct branch numbers.
All inputs are finite; a program needn't handle non-finite values.
Results may differ from a plain program's by a relative error of at most 0.0003.
Values sent between devices are 32-bit elements; how exact they have to be, the bound alone decides.
No kernel may reach another device: no remote copies, remote signals or barrier semaphores. Data moves between devices by JAX's collectives and lax.ppermute only.
A program may use at most 64 MiB of HBM per device.

v0:
```python
import jax
import jax.numpy as jnp
from jax import lax
from jax.sharding import PartitionSpec as P

BLK = 128


def project(upper, lower, vec_left, vec_right, state_w):
    scaled = upper * jnp.transpose(state_w)[None, :, :, None]
    lefts = jnp.einsum("binl,nik->bknl", scaled, vec_left, precision=lax.Precision.HIGHEST)
    rights = jnp.einsum("nkj,bjnl->bknl", vec_right, lower, precision=lax.Precision.HIGHEST)
    return (lefts, rights)


def finish(lefts, rights, exponent, times, weight_f):
    joint = lefts * rights
    expo = jnp.transpose(exponent)[None, :, :, None]
    decayed = joint * jnp.exp(expo * times[:, None, None, None])
    like_zero = jnp.sum(decayed, axis=1)
    like_one = jnp.sum(decayed * expo, axis=1)
    like_two = jnp.sum(decayed * expo * expo, axis=1)
    first = like_one / like_zero
    second = like_two / like_zero - first * first
    loglik = weight_f[None] * jnp.log(like_zero)
    sums = jnp.stack(
        [jnp.sum(weight_f[None] * first, axis=-1), jnp.sum(weight_f[None] * second, axis=-1)]
    )
    return (loglik, sums)


def on_device(
    top_partial,
    bottom_partial,
    left_vectors,
    right_vectors,
    decay_rates,
    state_weights,
    part_rates,
    branch_lengths,
    pattern_weights,
    block_partition,
    chosen_branches,
):
    times = branch_lengths[chosen_branches]
    branches = top_partial.shape[0]
    states = top_partial.shape[1]
    sites_here = top_partial.shape[3]
    nblocks = sites_here // BLK
    upper = top_partial.reshape(branches, states, nblocks, BLK)
    lower = bottom_partial.reshape(branches, states, nblocks, BLK)
    blocks = block_partition[0]
    owned = left_vectors.shape[0]
    groups = lax.axis_size("dom")
    parts_all = owned * groups
    wanted = lax.all_gather(block_partition, "dom", axis=0, tiled=True)
    relative = wanted - lax.axis_index("dom") * owned
    inside = jnp.logical_and(relative >= 0, relative < owned).astype(jnp.float32)
    clipped = jnp.clip(relative, 0, owned - 1)
    send_left = left_vectors[clipped] * inside[:, :, None, None]
    send_right = right_vectors[clipped] * inside[:, :, None, None]
    send_decay = decay_rates[clipped] * inside[:, :, None]
    send_weight = state_weights[clipped] * inside[:, :, None]
    send_rate = part_rates[clipped] * inside
    received = (
        lax.all_to_all(send_left, "dom", split_axis=0, concat_axis=0, tiled=True),
        lax.all_to_all(send_right, "dom", split_axis=0, concat_axis=0, tiled=True),
        lax.all_to_all(send_decay, "dom", split_axis=0, concat_axis=0, tiled=True),
        lax.all_to_all(send_weight, "dom", split_axis=0, concat_axis=0, tiled=True),
        lax.all_to_all(send_rate, "dom", split_axis=0, concat_axis=0, tiled=True),
    )
    vec_left = jnp.sum(received[0], axis=0)
    vec_right = jnp.sum(received[1], axis=0)
    decay_b = jnp.sum(received[2], axis=0)
    weight_b = jnp.sum(received[3], axis=0)
    rate_b = jnp.sum(received[4], axis=0)
    exponent = -decay_b * rate_b[:, None]
    lefts, rights = project(upper, lower, vec_left, vec_right, weight_b)
    weight_f = pattern_weights[0].astype(jnp.float32).reshape(nblocks, BLK)
    loglik, sums = finish(lefts, rights, exponent, times, weight_f)
    onehot = (blocks[:, None] == jnp.arange(parts_all, dtype=jnp.int32)[None, :]).astype(
        jnp.float32
    )
    part_local = jnp.einsum("abn,np->abp", sums, onehot, precision=lax.Precision.HIGHEST)
    everything = lax.psum(part_local, ("site", "dom"))
    share = lax.dynamic_slice_in_dim(everything, lax.axis_index("dom") * owned, owned, 2)
    totals = jnp.sum(everything, axis=2)
    updated = times - totals[0] / totals[1]
    new_lengths = branch_lengths.at[chosen_branches].set(updated)
    return (loglik.reshape(branches, 1, sites_here), share, new_lengths)


def solution(mesh):
    return jax.shard_map(
        on_device,
        mesh=mesh,
        in_specs=(
            P(None, None, "dom", "site"),
            P(None, None, "dom", "site"),
            P("dom", None, None),
            P("dom", None, None),
            P("dom", None),
            P("dom", None),
            P("dom"),
            P(),
            P("dom", "site"),
            P("dom", "site"),
            P(),
        ),
        out_specs=(P(None, "dom", "site"), P(None, None, "dom"), P()),
        check_vma=False,
    )
```

profile of v0, /device:TPU:0, one launch (start us, length us, event | category | flops | bytes accessed | tf_op | source)
XLA Modules:
  0.0 122.0 jit_solution(4191838396032848199)
XLA Ops:
  0.6 0.8 copy.76
  1.5 6.2 %all-gather = s32[4,1,8]{2,1,0:T(1,128)S(1)} all-gather(s32[1,1,8]{2,1,0:T(1,128)} %bitcast.55), channel_id=1, replica_groups=mesh['site'=8,'dom'=4] {'dom'}, dimensions={0}, use_global_device_ids=true | all-gather | bytes 160 | tf_op jit(solution)/shard_map/all_gather | solution.py:56
  7.7 0.1 reshape.73
  7.8 1.4 %gather_fusion.4 = f32[32]{0:T(128)S(1)} fusion(f32[64]{0:T(128)} %param.17, s32[1024]{0:T(1024)S(1)} %pad_clamp_fusion.1), kind=kCustom, calls=%fused_computation.4 | custom fusion | bytes 384 | tf_op jit(solution)/shard_map/gather | solution.py:64
  9.2 0.1 reshape.104
  9.3 0.6 bitcast_select_fusion
  9.9 3.2 %all-to-all-start.4 = ((f32[4,1,8]{2,1,0:T(1,128)}), f32[4,1,8]{2,1,0:T(1,128)S(1)}, u32[]{:S(2)}, u32[]{:S(2)}) async-start(f32[4,1,8]{2,1,0:T(1,128)} %bitcast.14), calls=%async_computation.4 | async-start | bytes 4096 | tf_op jit(solution)/shard_map/all_to_all | solution.py:70
  13.1 1.3 %gather_fusion.3 = f32[32,61]{1,0:T(8,128)S(1)} fusion(f32[64,61]{1,0:T(8,128)} %param.15, s32[1024]{0:T(1024)S(1)} %pad_clamp_fusion.1), kind=kCustom, calls=%fused_computation.3 | custom fusion | bytes 15744 | tf_op jit(solution)/shard_map/gather | solution.py:62
  14.4 1.3 %gather_fusion.1 = f32[32,61]{1,0:T(8,128)S(1)} fusion(f32[64,61]{1,0:T(8,128)} %param.16, s32[1024]{0:T(1024)S(1)} %pad_clamp_fusion.1), kind=kCustom, calls=%fused_computation.1 | custom fusion | bytes 15744 | tf_op jit(solution)/shard_map/gather | solution.py:63
  15.8 0.1 bitcast_multiply_fusion.2
  15.8 0.7 reshape.156
  16.5 0.3 all-to-all-done.4
  16.8 3.2 %all-to-all-start.3 = ((f32[4,1,488]{2,1,0:T(1,128)}), f32[4,1,488]{2,1,0:T(1,128)S(1)}, u32[]{:S(2)}, u32[]{:S(2)}) async-start(f32[4,1,488]{2,1,0:T(1,128)} %reshape.156), calls=%async_computation.3 | async-start | bytes 16384 | tf_op jit(solution)/shard_map/all_to_all | solution.py:68
  20.1 0.7 reshape.158
  20.7 2.7 %gather_fusion.2 = f32[32,61,61]{2,0,1:T(8,128)S(1)} fusion(f32[64,61,61]{2,0,1:T(8,128)S(1)} %copy-done, s32[1024]{0:T(1024)S(1)} %pad_clamp_fusion.1), kind=kCustom, calls=%fused_computation.2 | custom fusion | bytes 952704 | tf_op jit(solution)/shard_map/gather | solution.py:61
  23.5 5.0 %gather_fusion = f32[32,61,61]{2,0,1:T(8,128)} fusion(f32[64,61,61]{2,0,1:T(8,128)} %param.13, s32[1024]{0:T(1024)S(1)} %pad_clamp_fusion.1), kind=kCustom, calls=%fused_computation | custom fusion | bytes 952704 | tf_op jit(solution)/shard_map/gather | solution.py:60
  28.5 3.4 %all-to-all-start.1 = ((f32[4,1,488]{2,1,0:T(1,128)}), f32[4,1,488]{2,1,0:T(1,128)S(1)}, u32[]{:S(2)}, u32[]{:S(2)}) async-start(f32[4,1,488]{2,1,0:T(1,128)} %reshape.158), calls=%async_computation.1 | async-start | bytes 16384 | tf_op jit(solution)/shard_map/all_to_all | solution.py:69
  31.9 2.8 %copy_multiply_fusion.5 = (f32[4,8,61,61]{3,1,2,0:T(8,128)}, f32[4,8,61,61]{3,1,2,0:T(8,128)}) fusion(f32[4,8]{1,0:T(4,128)S(1)} %bitcast_convert_fusion, f32[32,61,61]{2,0,1:T(8,128)S(1)} %gather_fusion.2, f32[32,61,61]{2,0,1:T(8,128)} %gather_fusion), kind=kLoop, calls=%fused_computation.16 | loop fusion | flops 238144 | bytes 1905280 | tf_op jit(solution)/shard_map/mul | solution.py:60
  34.7 3.2 %reshape.160 = f32[4,1,29768]{2,1,0:T(1,128)} reshape(f32[4,61,8,61]{3,2,1,0:T(8,128)} %bitcast.46) | data formatting | bytes 952576
  37.8 3.5 %all-to-all-start = ((f32[4,1,29768]{2,1,0:T(1,128)}), f32[4,1,29768]{2,1,0:T(1,128)S(1)}, u32[]{:S(2)}, u32[]{:S(2)}) async-start(f32[4,1,29768]{2,1,0:T(1,128)} %reshape.160), calls=%async_computation | async-start | bytes 954368 | tf_op jit(solution)/shard_map/all_to_all | solution.py:66
  41.4 3.1 %reshape.154 = f32[4,1,29768]{2,1,0:T(1,128)} reshape(f32[4,61,8,61]{3,2,1,0:T(8,128)} %bitcast.45) | data formatting | bytes 952576
  44.5 0.7 gather_fusion.5
  45.2 0.5 broadcast.86
  45.7 0.7 reduce.1
  46.4 0.1 reshape.157
  46.5 0.7 reduce.3
  47.2 0.1 reshape.159
  47.3 0.6 reduce_sum.100
  47.9 0.1 multiply_bitcast_fusion
  47.9 1.7 %all-to-all-done = f32[4,1,29768]{2,1,0:T(1,128)S(1)} async-done(((f32[4,1,29768]{2,1,0:T(1,128)}), f32[4,1,29768]{2,1,0:T(1,128)S(1)}, u32[]{:S(2)}, u32[]{:S(2)}) %all-to-all-start) | async-done | bytes 476320 | tf_op jit(solution)/shard_map/all_to_all | solution.py:66
  49.6 4.3 %all-to-all-start.2 = ((f32[4,1,29768]{2,1,0:T(1,128)}), f32[4,1,29768]{2,1,0:T(1,128)}, u32[]{:S(2)}, u32[]{:S(2)}) async-start(f32[4,1,29768]{2,1,0:T(1,128)} %reshape.154), calls=%async_computation.2 | async-start | bytes 954368 | tf_op jit(solution)/shard_map/all_to_all | solution.py:67
  53.9 0.1 multiply_exponential_fusion
  54.0 2.1 %reduce.4 = f32[4,29768]{1,0:T(4,128)S(1)} reduce(f32[4,1,29768]{2,1,0:T(1,128)S(1)} %all-to-all-done, f32[]{:T(128)} %broadcast.86), dimensions={1}, to_apply=%all_to_all.18.reduce_sub_computation | reduce | bytes 952580 | tf_op jit(solution)/shard_map/all_to_all | solution.py:66
  56.1 0.6 reshape.161
  56.7 0.8 bitcast_reduce_fusion
  57.4 4.7 %all-to-all-done.2 = f32[4,1,29768]{2,1,0:T(1,128)} async-done(((f32[4,1,29768]{2,1,0:T(1,128)}), f32[4,1,29768]{2,1,0:T(1,128)}, u32[]{:S(2)}, u32[]{:S(2)}) %all-to-all-start.2) | async-done | bytes 476320 | tf_op jit(solution)/shard_map/all_to_all | solution.py:67
  62.1 2.9 %reduce.2 = f32[4,29768]{1,0:T(4,128)S(1)} reduce(f32[4,1,29768]{2,1,0:T(1,128)} %all-to-all-done.2, f32[]{:T(128)} %broadcast.86), dimensions={1}, to_apply=%all_to_all.20.reduce_sub_computation | reduce | bytes 952580 | tf_op jit(solution)/shard_map/all_to_all | solution.py:67
  65.0 0.6 reshape.155
  65.6 0.1 bitcast_reduce_fusion.1
  65.7 6.8 %fusion = f32[8,61,16,128]{3,1,2,0:T(8,128)S(1)} fusion(f32[16,61,8,128]{3,2,1,0:T(8,128)} %bitcast.44, f32[8,61,61,1]{2,0,1,3:T(8,128)S(1)} %bitcast.47), kind=kOutput, calls=%fused_computation.8 | convolution fusion | flops 731578368 | bytes 8114464 | tf_op jit(solution)/shard_map/nkj,bjnl->bknl/dot_general | solution.py:12
  72.6 6.4 %multiply_reduce_fusion.1 = (f32[16,8,128]{2,0,1:T(8,128)S(1)}, f32[16,8,128]{2,0,1:T(8,128)S(1)}, f32[16,8,128]{2,0,1:T(8,128)S(1)}) fusion(f32[61,8]{0,1:T(8,128)S(1)} %copy-done.4, f32[16,61,8]{1,0,2:T(8,128)S(1)} %multiply_exponential_fusion, f32[8,61,16,128]{3,1,2,0:T(8,128)S(1)} %fusion, f32[16,61,8,128]{3,2,1,0:T(8,128)S(1)} %bitcast.57, ...), kind=kOutput, calls=%fused_computation.13 | convolution fusion | flops 739524608 | bytes 8346208 | tf_op jit(solution)/shard_map/binl,nik->bknl/dot_general | solution.py:11
  79.0 0.1 multiply_reduce_fusion.3
  79.2 0.2 fusion.6
  79.4 40.4 %psum.7 = f32[2,16,256]{2,1,0:T(8,128)S(1)} all-reduce(f32[2,16,256]{2,1,0:T(8,128)S(1)} %fusion.6), channel_id=1, replica_groups=mesh['site'=8,'dom'=4] {'site','dom'}, use_global_device_ids=true, to_apply=%region_10.11 | all-reduce | flops 8192 | bytes 65536 | tf_op jit(solution)/shard_map/psum | solution.py:85
  119.8 0.1 reduce_sum.109
  119.9 0.7 constant_dynamic-slice_fusion
  120.6 0.6 scatter_fusion
  121.3 0.7 copy.45
  (44 shorter events, 0.2 us)
Async XLA Ops:
  0.6 20.1 %copy-start = (f32[64,61,61]{2,0,1:T(8,128)S(1)}, f32[64,61,61]{2,0,1:T(8,128)}, u32[]{:S(2)}) copy-start(f32[64,61,61]{2,0,1:T(8,128)} %param.14) | copy-start | bytes 2857732
  9.9 6.9 %all-to-all-start.4 = ((f32[4,1,8]{2,1,0:T(1,128)}), f32[4,1,8]{2,1,0:T(1,128)S(1)}, u32[]{:S(2)}, u32[]{:S(2)}) async-start(f32[4,1,8]{2,1,0:T(1,128)} %bitcast.14), calls=%async_computation.4 | async-start | bytes 4096 | tf_op jit(solution)/shard_map/all_to_all | solution.py:70
  16.8 11.7 %all-to-all-start.3 = ((f32[4,1,488]{2,1,0:T(1,128)}), f32[4,1,488]{2,1,0:T(1,128)S(1)}, u32[]{:S(2)}, u32[]{:S(2)}) async-start(f32[4,1,488]{2,1,0:T(1,128)} %reshape.156), calls=%async_computation.3 | async-start | bytes 16384 | tf_op jit(solution)/shard_map/all_to_all | solution.py:68
  28.4 12.9 %copy-start.13 = (s32[16]{0:T(128)S(1)}, s32[16]{0:T(128)}, u32[]{:S(2)}) copy-start(s32[16]{0:T(128)} %param.21) | copy-start | bytes 196
  28.4 12.9 %copy-start.7 = (s32[1,1024]{1,0:T(1,128)S(1)}, s32[1,1024]{1,0:T(1,128)}, u32[]{:S(2)}) copy-start(s32[1,1024]{1,0:T(1,128)} %param.19) | copy-start | bytes 12292
  28.5 9.4 %all-to-all-start.1 = ((f32[4,1,488]{2,1,0:T(1,128)}), f32[4,1,488]{2,1,0:T(1,128)S(1)}, u32[]{:S(2)}, u32[]{:S(2)}) async-start(f32[4,1,488]{2,1,0:T(1,128)} %reshape.158), calls=%async_computation.1 | async-start | bytes 16384 | tf_op jit(solution)/shard_map/all_to_all | solution.py:69
  37.8 11.8 %all-to-all-start = ((f32[4,1,29768]{2,1,0:T(1,128)}), f32[4,1,29768]{2,1,0:T(1,128)S(1)}, u32[]{:S(2)}, u32[]{:S(2)}) async-start(f32[4,1,29768]{2,1,0:T(1,128)} %reshape.160), calls=%async_computation | async-start | bytes 954368 | tf_op jit(solution)/shard_map/all_to_all | solution.py:66
  41.3 3.2 %copy-start.9 = (s32[16]{0:T(128)}, s32[16]{0:T(128)S(1)}, u32[]{:S(2)}) copy-start(s32[16]{0:T(128)S(1)} %compare_select_fusion.1) | copy-start | bytes 196
  45.2 8.7 %copy-start.5 = (f32[16]{0:T(128)}, f32[16]{0:T(128)S(1)}, u32[]{:S(2)}) copy-start(f32[16]{0:T(128)S(1)} %gather_fusion.5) | copy-start | bytes 196
  47.9 6.1 %copy-start.3 = (f32[61,8]{0,1:T(8,128)}, f32[61,8]{0,1:T(8,128)S(1)}, u32[]{:S(2)}) copy-start(f32[61,8]{0,1:T(8,128)S(1)} %multiply_bitcast_fusion) | copy-start | bytes 5860
  49.6 12.5 %all-to-all-start.2 = ((f32[4,1,29768]{2,1,0:T(1,128)}), f32[4,1,29768]{2,1,0:T(1,128)}, u32[]{:S(2)}, u32[]{:S(2)}) async-start(f32[4,1,29768]{2,1,0:T(1,128)} %reshape.154), calls=%async_computation.2 | async-start | bytes 954368 | tf_op jit(solution)/shard_map/all_to_all | solution.py:67
  65.7 6.9 %copy-start.2 = (f32[8,61,61]{2,0,1:T(8,128)S(1)}, f32[8,61,61]{2,0,1:T(8,128)}, u32[]{:S(2)}) copy-start(f32[8,61,61]{2,0,1:T(8,128)} %bitcast_reduce_fusion) | copy-start | bytes 357220
  65.7 6.9 %copy-start.4 = (f32[61,8]{0,1:T(8,128)S(1)}, f32[61,8]{0,1:T(8,128)}, u32[]{:S(2)}) copy-start(f32[61,8]{0,1:T(8,128)} %copy-done.3) | copy-start | bytes 5860
  65.7 6.9 %copy-start.8 = (f32[8,61]{1,0:T(8,128)S(1)}, f32[8,61]{1,0:T(8,128)}, u32[]{:S(2)}) copy-start(f32[8,61]{1,0:T(8,128)} %reduce_sum.100) | copy-start | bytes 5860
  65.7 6.9 %copy-start.12 = (f32[16,61,1,1024]{3,2,1,0:T(1,128)S(1)}, f32[16,61,1,1024]{3,2,1,0:T(1,128)}, u32[]{:S(2)}) copy-start(f32[16,61,1,1024]{3,2,1,0:T(1,128)} %param.11) | copy-start | bytes 11993092
  72.6 6.6 %copy-start.11 = (s32[1,8]{1,0:T(1,128)S(1)}, s32[1,8]{1,0:T(1,128)}, u32[]{:S(2)}) copy-start(s32[1,8]{1,0:T(1,128)} %param.20) | copy-start | bytes 100
  72.6 48.0 %copy-start.6 = (f32[16]{0:T(128)S(1)}, f32[16]{0:T(128)}, u32[]{:S(2)}) copy-start(f32[16]{0:T(128)} %copy-done.5) | copy-start | bytes 196
  72.6 48.0 %copy-start.10 = (s32[16]{0:T(128)S(1)}, s32[16]{0:T(128)}, u32[]{:S(2)}) copy-start(s32[16]{0:T(128)} %copy-done.9) | copy-start | bytes 196
  121.2 0.8 copy-start.1
where the time goes:
time: 123 us; the launch traced here: 122 us
  blocking collectives  46.6 us (38%)
  local copies, waits for them, and re-layouts  25 us (20%)
  starting transfers between devices  17.6 us (14%)
  matrix products  13.5 us (11%)
  other arithmetic  11.7 us (10%)
  waiting for transfers between devices  6.6 us (5%)
    psum x1, blocking collectives, on_device(): everything = lax.psum(part_local, ('site', 'dom'))  40.4 us
    unnamed x38, local copies, waits for them, and re-layouts  10.6 us
    dot_general x1, matrix products, project(): jnp.einsum('nkj,bjnl->bknl', vec_right, lower, precision=lax.Precision.HI...  6.82 us
    dot_general x1, matrix products, project(): jnp.einsum('binl,nik->bknl', scaled, vec_left, precision=lax.Precision.HI...  6.42 us
    all_gather x1, blocking collectives, on_device(): wanted = lax.all_gather(block_partition, 'dom', axis=0, tiled=True)  6.22 us
    gather x1, local copies, waits for them, and re-layouts, on_device(): send_left = left_vectors[clipped] * inside[:, :, None, None]  4.97 us
    all_to_all x1, waiting for transfers between devices, on_device(): lax.all_to_all(send_right, 'dom', split_axis=0, concat_axis=0, tiled=True)  4.67 us
    all_to_all x1, starting transfers between devices, on_device(): lax.all_to_all(send_right, 'dom', split_axis=0, concat_axis=0, tiled=True)  4.3 us
  transfers between devices with their start and end apart: 5, of which 3 were waited for; matrix products, arithmetic and copies ran while one was open for 23% of the time, Pallas kernels for 0%

commit v1 on v0

v1 whole, which is shorter than its diff:
```python
import functools

import jax
import jax.numpy as jnp
from jax import lax
from jax.experimental import pallas as pl
from jax.experimental.pallas import tpu as pltpu
from jax.sharding import PartitionSpec as P

BLK = 128
HALF = 64
F32 = jnp.float32
BF16 = jnp.bfloat16


def pack_kernel(rate_ref, left_ref, right_ref, decay_ref, weight_ref, out_ref):
    states, group, _ = left_ref.shape
    left = left_ref.reshape(states * group, states)
    right = right_ref.reshape(states * group, states)
    base = pl.program_id(0) * group
    for q in range(group):
        table = left[pl.ds(q, states, stride=group), :]
        decay = decay_ref[pl.ds(q, 1), :]
        rows = jnp.concatenate([table, decay, jnp.zeros((HALF - states - 1, states), F32)], axis=0)
        scale = jnp.concatenate(
            [
                weight_ref[pl.ds(q, 1), :],
                jnp.full((1, 1), -rate_ref[base + q], F32),
                jnp.zeros((1, HALF - states - 1), F32),
            ],
            axis=1,
        )
        scaled = rows.T * scale
        other = right[pl.ds(q, states, stride=group), :]
        tile = jnp.concatenate([scaled, other, jnp.zeros((states, HALF - states), F32)], axis=1)
        out_ref[q] = jnp.concatenate([tile, jnp.zeros((HALF - states, 2 * HALF), F32)], axis=0)


def pack_tables(left, right, decay, weight, rate):
    parts, states, _ = left.shape
    group = 8
    table = pl.BlockSpec((states, group, states), lambda g: (0, g, 0))
    row = pl.BlockSpec((group, states), lambda g: (g, 0))
    return pl.pallas_call(
        pack_kernel,
        grid=(parts // group,),
        in_specs=[pl.BlockSpec(memory_space=pltpu.SMEM), table, table, row, row],
        out_specs=pl.BlockSpec((group, HALF, 2 * HALF), lambda g: (g, 0, 0)),
        out_shape=jax.ShapeDtypeStruct((parts, HALF, 2 * HALF), F32),
        name="pack",
    )(rate, jnp.transpose(left, (1, 0, 2)), jnp.transpose(right, (1, 0, 2)), decay, weight)


def split_kernel(top_ref, bottom_ref, out_ref):
    nblocks = out_ref.shape[0]
    fused = out_ref.shape[2] // BLK
    states = top_ref.shape[0] // (nblocks * fused)
    pad = jnp.zeros((HALF - states, BLK), F32)
    for b in range(fused):
        for n in range(nblocks):
            for side, ref in enumerate((top_ref, bottom_ref)):
                rows = ref[pl.ds(b * states * nblocks + n, states, stride=nblocks), :]
                full = jnp.concatenate([rows, pad], axis=0)
                high = full.astype(BF16)
                low = (full - high.astype(F32)).astype(BF16)
                lanes = pl.ds(b * BLK, BLK)
                out_ref[n, pl.ds(side * HALF, HALF), lanes] = high
                out_ref[n, pl.ds((2 + side) * HALF, HALF), lanes] = low


def split_partials(top, bottom, branches, states, nblocks):
    fused = 2
    source = pl.BlockSpec((fused * states * nblocks, BLK), lambda b: (b, 0))
    return pl.pallas_call(
        split_kernel,
        grid=(branches // fused,),
        in_specs=[source, source],
        out_specs=pl.BlockSpec((nblocks, 4 * HALF, fused * BLK), lambda b: (0, 0, b)),
        out_shape=jax.ShapeDtypeStruct((nblocks, 4 * HALF, branches * BLK), BF16),
        name="split",
    )(top, bottom)


def pick_kernel(wanted_ref, where_ref, own_ref, partner_ref, out_ref, sems):
    owned = own_ref.shape[0]
    group = where_ref[0]
    me = where_ref[1]
    count = out_ref.shape[0]
    for n in range(count):
        part = wanted_ref[n]
        owner = part // owned
        row = part - owner * owned
        mine = owner == group + me

        @pl.when(mine)
        def _():
            pltpu.make_async_copy(own_ref.at[row], out_ref.at[n], sems.at[n]).start()

        @pl.when(jnp.logical_not(mine))
        def _():
            pltpu.make_async_copy(partner_ref.at[row], out_ref.at[n], sems.at[n]).start()

    for n in range(count):
        pltpu.make_async_copy(own_ref.at[0], out_ref.at[n], sems.at[n]).wait()


def pick_tiles(wanted, where, own, partner):
    count = wanted.shape[0]
    smem = pl.BlockSpec(memory_space=pltpu.SMEM)
    hbm = pl.BlockSpec(memory_space=pl.ANY)
    return pl.pallas_call(
        pick_kernel,
        in_specs=[smem, smem, hbm, hbm],
        out_specs=pl.BlockSpec(memory_space=pltpu.VMEM),
        out_shape=jax.ShapeDtypeStruct((count,) + own.shape[1:], F32),
        scratch_shapes=[pltpu.SemaphoreType.DMA((count,))],
        name="pick",
    )(wanted, where, own, partner)


def block_kernel(
    rounds, owned, pair, times_ref, blocks_ref, where_ref, weight_ref, operand_ref, *refs
):
    tiles = refs[: rounds]
    loglik_ref, share_ref = refs[rounds : rounds + 2]
    like_refs = refs[rounds + 2 :]
    states_lane = tiles[0].shape[2]
    n = pl.program_id(0)
    last = pl.num_programs(0) - 1
    branches = loglik_ref.shape[0]
    nblocks = loglik_ref.shape[1]
    distance = lax.rem(blocks_ref[n] // (owned * pair) - where_ref[2] + rounds, rounds)
    tile = tiles[0][0]
    for r in range(1, rounds):
        tile = jnp.where(distance == r, tiles[r][0], tile)
    lane = lax.broadcasted_iota(jnp.int32, tile.shape, 1)
    high = tile.astype(BF16)
    low = (tile - high.astype(F32)).astype(BF16)
    zero = jnp.zeros_like(high)
    is_left = lane < HALF
    left_high = jnp.where(is_left, high, zero)
    right_high = jnp.where(is_left, zero, high)
    left_low = jnp.where(is_left, low, zero)
    right_low = jnp.where(is_left, zero, low)
    first_rows = jnp.concatenate([left_high, right_high], axis=0)
    second_rows = jnp.concatenate([left_low, right_low], axis=0)
    lhs = jnp.concatenate(
        [
            jnp.concatenate([first_rows, first_rows], axis=1),
            jnp.concatenate([second_rows, jnp.zeros_like(second_rows)], axis=1),
        ],
        axis=0,
    )
    where_exponent = where_ref[3]
    column = jnp.sum(jnp.where(lane == where_exponent, tile, 0.0), axis=1, keepdims=True)
    expo = jnp.broadcast_to(column, (HALF, BLK))
    wide = 2 * BLK
    for c in range(branches * BLK // wide):
        prod = jnp.dot(
            lhs, operand_ref[0, :, c * wide : (c + 1) * wide], preferred_element_type=F32
        )
        lefts = prod[:HALF] + prod[2 * HALF : 3 * HALF]
        rights = prod[HALF : 2 * HALF] + prod[3 * HALF :]
        joint = lefts * rights
        for h in range(wide // BLK):
            b = c * (wide // BLK) + h
            zeroth = joint[:, h * BLK : (h + 1) * BLK] * jnp.exp(expo * times_ref[b])
            first = zeroth * expo
            second = first * expo
            for ref, term in zip(like_refs, (zeroth, first, second)):
                ref[b, pl.ds(n, 1), :] = jnp.sum(term, axis=0, keepdims=True)

    @pl.when(n == last)
    def _():
        weight = weight_ref[...].astype(F32)
        lanes = lax.broadcasted_iota(jnp.int32, (nblocks, BLK), 1)
        rows = lax.broadcasted_iota(jnp.int32, (nblocks, BLK), 0)
        ident = jnp.zeros((nblocks, BLK), F32)
        for m in range(nblocks):
            ident = jnp.where(rows == m, blocks_ref[m].astype(F32), ident)
        share = jnp.where(lanes == 2 * branches, ident, 0.0)
        for b in range(branches):
            like = like_refs[0][b]
            first = like_refs[1][b] / like
            second = like_refs[2][b] / like - first * first
            loglik_ref[b] = weight * jnp.log(like)
            one = jnp.sum(weight * first, axis=1, keepdims=True)
            two = jnp.sum(weight * second, axis=1, keepdims=True)
            share = jnp.where(lanes == b, one, share)
            share = jnp.where(lanes == branches + b, two, share)
        for d in range(share_ref.shape[0]):
            share_ref[d] = share


def block_likelihoods(times, blocks, where, weight, operand, tiles, owned, pair, devices):
    nblocks, depth, columns = operand.shape
    branches = times.shape[0]
    smem = pl.BlockSpec(memory_space=pltpu.SMEM)
    tile = pl.BlockSpec((1, HALF, 2 * HALF), lambda n: (n, 0, 0))
    whole = lambda shape: pl.BlockSpec(shape, lambda n: (0,) * len(shape))
    return pl.pallas_call(
        functools.partial(block_kernel, len(tiles), owned, pair),
        grid=(nblocks,),
        in_specs=[
            smem,
            smem,
            smem,
            whole((nblocks, BLK)),
            pl.BlockSpec((1, depth, columns), lambda n: (n, 0, 0)),
        ]
        + [tile] * len(tiles),
        out_specs=[whole((branches, nblocks, BLK)), whole((devices, nblocks, BLK))],
        out_shape=[
            jax.ShapeDtypeStruct((branches, nblocks, BLK), F32),
            jax.ShapeDtypeStruct((devices, nblocks, BLK), F32),
        ],
        scratch_shapes=[pltpu.VMEM((branches, nblocks, BLK), F32)] * 3,
        name="blocks",
    )(times, blocks, where, weight, operand, *tiles)


def sum_kernel(where_ref, share_ref, part_ref, total_ref):
    owned = part_ref.shape[1]
    terms = part_ref.shape[0]
    share = share_ref[...]
    rows = share.shape[0]
    lanes = lax.broadcasted_iota(jnp.int32, (rows, owned), 1) + where_ref[4]
    ident = share[:, terms : terms + 1].astype(jnp.int32)
    onehot = (ident == lanes).astype(F32)
    sums = lax.dot_general(
        share,
        onehot,
        (((0,), (0,)), ((), ())),
        precision=lax.Precision.HIGHEST,
        preferred_element_type=F32,
    )
    part_ref[...] = sums[:terms]
    total_ref[...] = jnp.sum(share, axis=0, keepdims=True)


def add_up(where, share, terms, owned):
    return pl.pallas_call(
        sum_kernel,
        in_specs=[
            pl.BlockSpec(memory_space=pltpu.SMEM),
            pl.BlockSpec(memory_space=pltpu.VMEM),
        ],
        out_specs=[pl.BlockSpec(memory_space=pltpu.VMEM)] * 2,
        out_shape=[
            jax.ShapeDtypeStruct((terms, owned), F32),
            jax.ShapeDtypeStruct((1, BLK), F32),
        ],
        name="sums",
    )(where, share)


def on_device(
    top_partial,
    bottom_partial,
    left_vectors,
    right_vectors,
    decay_rates,
    state_weights,
    part_rates,
    branch_lengths,
    pattern_weights,
    block_partition,
    chosen_branches,
):
    branches, states, _, sites_here = top_partial.shape
    nblocks = sites_here // BLK
    owned = left_vectors.shape[0]
    groups = lax.axis_size("dom")
    pair = 2 if groups % 2 == 0 else 1
    rounds = groups // pair
    me = lax.axis_index("dom")
    mine = me // pair
    where = jnp.stack(
        [mine * pair, me - mine * pair, mine, jnp.int32(states), me * owned]
    ).astype(jnp.int32)

    def shifted(value, r):
        step = [
            (d, ((d // pair + r) % rounds) * pair + d % pair) for d in range(groups)
        ]
        return lax.ppermute(value, "dom", step)

    blocks = block_partition[0]
    requests = [shifted(blocks, rounds - r) for r in range(1, rounds)]
    own = pack_tables(left_vectors, right_vectors, decay_rates, state_weights, part_rates)
    if pair == 2:
        partner = lax.ppermute(own, "dom", [(d, d ^ 1) for d in range(groups)])
    else:
        partner = own
    operand = split_partials(
        top_partial.reshape(branches * states * nblocks, BLK),
        bottom_partial.reshape(branches * states * nblocks, BLK),
        branches,
        states,
        nblocks,
    )
    answers = [
        shifted(pick_tiles(request, where, own, partner), r)
        for r, request in zip(range(1, rounds), requests)
    ]
    tiles = [pick_tiles(blocks, where, own, partner)]
    tiles += answers[::-1]
    times = branch_lengths[chosen_branches]
    devices = lax.axis_size("site") * groups
    loglik, share = block_likelihoods(
        times,
        blocks,
        where,
        pattern_weights.reshape(nblocks, BLK),
        operand,
        tiles,
        owned,
        pair,
        devices,
    )
    everything = lax.all_to_all(
        share, ("site", "dom"), split_axis=0, concat_axis=0, tiled=True
    )
    terms = 2 * branches
    parts, totals = add_up(
        where, everything.reshape(devices * nblocks, BLK), terms, owned
    )
    updated = times - totals[0, :branches] / totals[0, branches:terms]
    new_lengths = branch_lengths.at[chosen_branches].set(updated)
    return (
        loglik.reshape(branches, 1, sites_here),
        parts.reshape(2, branches, owned),
        new_lengths,
    )


def solution(mesh):
    return jax.shard_map(
        on_device,
        mesh=mesh,
        in_specs=(
            P(None, None, "dom", "site"),
            P(None, None, "dom", "site"),
            P("dom", None, None),
            P("dom", None, None),
            P("dom", None),
            P("dom", None),
            P("dom"),
            P(),
            P("dom", "site"),
            P("dom", "site"),
            P(),
        ),
        out_specs=(P(None, "dom", "site"), P(None, None, "dom"), P()),
        check_vma=False,
    )
```

time: 123 us -> 60 us (0.49)
  blocking collectives: 46.6 us -> 13.4 us
  Pallas kernels: 0 us -> 31.8 us
  local copies, waits for them, and re-layouts: 25 us -> 6.3 us
  matrix products: 13.5 us -> 0 us
  starting transfers between devices: 17.6 us -> 5.37 us
  other arithmetic: 11.7 us -> 0.84 us
  waiting for transfers between devices: 6.6 us -> 0.94 us
    psum x1 -> x0, blocking collectives: 40.4 us -> none  [on_device(): everything = lax.psum(part_local, ('site', 'dom'))]
    pallas_call x0 -> x6, Pallas kernels: none -> 31.8 us  [the longest x1 9.55 us: split_partials(): pl.pallas_call(split_kernel, grid=(branches // fused,), in_specs=[source,...]
    all_to_all x5 -> x0, starting transfers between devices: 17.6 us -> none  [the longest x1 4.3 us: on_device(): lax.all_to_all(send_right, 'dom', split_axis=0, concat_axis=0, tiled=True)]
    dot_general x3 -> x0, matrix products: 13.5 us -> none  [the longest x1 6.82 us: project(): jnp.einsum('nkj,bjnl->bknl', vec_right, lower, precision=lax.Precision.HI...]
    all_to_all x0 -> x1, blocking collectives: none -> 13.4 us  [on_device(): lax.all_to_all(share, ('site', 'dom'), split_axis=0, concat_axis=0, tiled...]
    gather x6 -> x0, local copies, waits for them, and re-layouts: 11.8 us -> none  [the longest x1 4.97 us: on_device(): send_left = left_vectors[clipped] * inside[:, :, None, None]]
    unnamed x38 -> x15, local copies, waits for them, and re-layouts: 10.6 us -> 3.89 us
    all_to_all x5 -> x0, waiting for transfers between devices: 6.6 us -> none  [the longest x1 4.67 us: on_device(): lax.all_to_all(send_right, 'dom', split_axis=0, concat_axis=0, tiled=True)]
  transfers between devices with their start and end apart: 5 -> 3, of which waited for: 3 -> 1; matrix products, arithmetic and copies ran while one was open for 23% -> 3% of each run, Pallas kernels for 0% -> 20%
where the time goes in v1:
time: 60 us; the launch traced here: 59.3 us
  Pallas kernels  31.8 us (53%)
  blocking collectives  13.4 us (22%)
  local copies, waits for them, and re-layouts  6.3 us (10%)
  starting transfers between devices  5.37 us (9%)
  waiting for transfers between devices  0.94 us (2%)
  other arithmetic  0.84 us (1%)
  between operations  0.69 us (1%)
    all_to_all x1, blocking collectives, on_device(): lax.all_to_all(share, ('site', 'dom'), split_axis=0, concat_axis=0, tiled...  13.4 us
    pallas_call x1, Pallas kernels, split_partials(): pl.pallas_call(split_kernel, grid=(branches // fused,), in_specs=[source,...  9.55 us
    pallas_call x1, Pallas kernels, block_likelihoods(): pl.pallas_call(functools.partial(block_kernel, len(tiles), owned, pair),...  8.52 us
    pallas_call x1, Pallas kernels, pack_tables(): pl.pallas_call(pack_kernel, grid=(parts // group,), in_specs=[pl.BlockSpe...  7.15 us
    ppermute x2, starting transfers between devices, shifted(): return lax.ppermute(value, 'dom', step)  4.88 us
    pallas_call x2, Pallas kernels, pick_tiles(): pl.pallas_call(pick_kernel, in_specs=[smem, smem, hbm, hbm], out_specs=pl...  4.67 us
    unnamed x15, local copies, waits for them, and re-layouts  3.89 us
    pallas_call x1, Pallas kernels, add_up(): pl.pallas_call(sum_kernel, in_specs=[pl.BlockSpec(memory_space=pltpu.SMEM...  1.87 us
  transfers between devices with their start and end apart: 3, of which 1 were waited for; matrix products, arithmetic and copies ran while one was open for 3% of the time, Pallas kernels for 20%

profile of v1, /device:TPU:0, one launch (start us, length us, event | category | flops | bytes accessed | tf_op | source)
XLA Modules:
  0.0 59.3 jit_solution(12107093019291221498)
XLA Ops:
  0.6 0.7 %copy.18 = f32[1997]{0:T(1024)S(1)} copy(f32[1997]{0:T(1024)} %param.18) | data formatting | bytes 15976
  1.3 0.0 copy-start.4
  1.3 7.2 %pack.1.own_ref = f32[64,64,128]{2,1,0:T(8,128)} custom-call(f32[64]{0:T(128)} %rate_ref.1, f32[61,64,61]{2,1,0:T(8,128)} %bitcast.18, f32[61,64,61]{2,1,0:T(8,128)} %bitcast.19, f32[64,61]{1,0:T(8,128)} %decay_ref.1, f32[64,61]{1,0:T(8,128)} %weight_ref.1), custom_call_target="tpu_custom_call" | custom-call | tf_op jit(solution)/shard_map/pack/pallas_call | solution.py:44
  8.5 0.5 collective-permute-start
  9.0 0.0 copy-done.4
  9.0 2.6 %collective-permute-start.1 = (s32[8]{0:T(128)S(1)}, s32[8]{0:T(128)S(1)}, u32[]{:S(2)}, u32[]{:S(2)}) collective-permute-start(s32[8]{0:T(128)S(1)} %bitcast.24), channel_id=1, source_target_pairs={{0,2},{1,3},{2,0},{3,1},{4,6},{5,7},{6,4},{7,5},{8,10},{9,11},{10,... | collective-permute-start | bytes 104 | tf_op jit(solution)/shard_map/ppermute | solution.py:286
  11.6 0.6 %stack.19.where_ref = s32[5]{0:T(128)} concatenate(s32[1]{0:T(128)} %bitcast.1, s32[1]{0:T(128)} %bitcast.2, s32[1]{0:T(128)} %bitcast.3, s32[1]{0:T(128)} %constant.24.clone.1, s32[1]{0:T(128)} %bitcast.4), dimensions={0} | concatenate | bytes 40 | tf_op jit(solution)/shard_map/stack | solution.py:278
  12.2 0.0 copy-start.6
  12.2 0.9 %collective-permute-done.1.wanted_ref = s32[8]{0:T(128)S(1)} collective-permute-done((s32[8]{0:T(128)S(1)}, s32[8]{0:T(128)S(1)}, u32[]{:S(2)}, u32[]{:S(2)}) %collective-permute-start.1) | collective-permute-done | bytes 64 | tf_op jit(solution)/shard_map/ppermute | solution.py:286
  13.1 0.0 copy-start.5
  13.1 0.0 collective-permute-done.partner_ref
  13.1 0.5 copy-done.5
  13.6 0.0 copy-start.1
  13.6 1.3 %copy-done.1 = f32[64,64,128]{2,1,0:T(8,128)} copy-done((f32[64,64,128]{2,1,0:T(8,128)}, f32[64,64,128]{2,1,0:T(8,128)S(1)}, u32[]{:S(2)}) %copy-start.1) | copy-done | bytes 2097176
  14.9 2.3 %pick.3 = f32[8,64,128]{2,1,0:T(8,128)} custom-call(s32[8]{0:T(128)} %copy-done.5, s32[5]{0:T(128)} %stack.19.where_ref, f32[64,64,128]{2,1,0:T(8,128)} %pack.1.own_ref, f32[64,64,128]{2,1,0:T(8,128)} %copy-done.1), custom_call_target="tpu_custom_call" | custom-call | tf_op jit(solution)/shard_map/pick/pallas_call | solution.py:111
  17.3 2.3 %collective-permute-start.2 = (f32[8,64,128]{2,1,0:T(8,128)}, f32[8,64,128]{2,1,0:T(8,128)S(1)}, u32[]{:S(2)}, u32[]{:S(2)}) collective-permute-start(f32[8,64,128]{2,1,0:T(8,128)} %pick.3), channel_id=1, source_target_pairs={{0,2},{1,3},{2,0},{3,1},{4,6},{5,7},{6,4},{7,5},{8,10},{9,11},{10,... | collective-permute-start | bytes 786440 | tf_op jit(solution)/shard_map/ppermute | solution.py:286
  19.6 0.0 copy-done.6
  19.6 1.2 %gather_fusion = f32[16]{0:T(128)} fusion(f32[1997]{0:T(1024)S(1)} %copy.18, s32[1024]{0:T(1024)S(1)} %pad_clamp_fusion), kind=kCustom, calls=%fused_computation | custom fusion | bytes 192 | tf_op jit(solution)/shard_map/gather | solution.py:308
  20.8 9.6 %split.1.operand_ref = bf16[8,256,2048]{2,1,0:T(8,128)(2,1)} custom-call(f32[7808,128]{1,0:T(8,128)} %bitcast.16, f32[7808,128]{1,0:T(8,128)} %bitcast.17), custom_call_target="tpu_custom_call" | custom-call | tf_op jit(solution)/shard_map/split/pallas_call | solution.py:74
  30.3 2.3 %pick.2.refs_0_ = f32[8,64,128]{2,1,0:T(8,128)} custom-call(s32[8]{0:T(128)} %bitcast.22, s32[5]{0:T(128)} %stack.19.where_ref, f32[64,64,128]{2,1,0:T(8,128)} %pack.1.own_ref, f32[64,64,128]{2,1,0:T(8,128)} %copy-done.1), custom_call_target="tpu_custom_call" | custom-call | tf_op jit(solution)/shard_map/pick/pallas_call | solution.py:111
  32.7 0.0 collective-permute-done.2.refs_1_
  32.7 0.0 copy-start.2
  32.7 0.7 %copy-done.2 = f32[8,64,128]{2,1,0:T(8,128)} copy-done((f32[8,64,128]{2,1,0:T(8,128)}, f32[8,64,128]{2,1,0:T(8,128)S(1)}, u32[]{:S(2)}) %copy-start.2) | copy-done | bytes 262168
  33.4 0.0 copy-start.3
  33.4 8.5 %blocks.1 = (f32[16,8,128]{2,1,0:T(8,128)}, f32[32,8,128]{2,1,0:T(8,128)}) custom-call(f32[16]{0:T(128)} %gather_fusion, s32[8]{0:T(128)} %bitcast.23, s32[5]{0:T(128)} %stack.19.where_ref, s32[8,128]{1,0:T(8,128)} %bitcast.21, bf16[8,256,2048]{2,1,0:T(8,128)(2,1)} %split.1.operand_ref, f32[8,64,128]{2,1,0:T(8,128)} %pick.2.refs_0_, f32[8,64,128]{2,1,0:T(8,128)} %copy-done.2), custom_call_target="tpu_custom_call" | custom-call | tf_op jit(solution)/shard_map/blocks/pallas_call | solution.py:201
  42.0 13.4 %all_to_all.5 = f32[32,8,128]{2,1,0:T(8,128)} all-to-all(f32[32,8,128]{2,1,0:T(8,128)} %get-tuple-element.8), channel_id=1, replica_groups=mesh['site'=8,'dom'=4] {'site','dom'}, dimensions={0} | all-to-all | bytes 262144 | tf_op jit(solution)/shard_map/all_to_all | solution.py:321
  55.4 1.9 %sums.1 = (f32[32,64]{1,0:T(8,128)}, f32[1,128]{1,0:T(1,128)}) custom-call(s32[5]{0:T(128)} %stack.19.where_ref, f32[256,128]{1,0:T(8,128)} %bitcast.20), custom_call_target="tpu_custom_call" | custom-call | tf_op jit(solution)/shard_map/sums/pallas_call | solution.py:242
  57.2 0.0 copy-done.3
  57.2 0.8 %bitcast_subtract_fusion = f32[16]{0:T(128)S(1)} fusion(f32[16]{0:T(128)S(1)} %copy-done.3, f32[1,128]{1,0:T(1,128)} %get-tuple-element.10), kind=kLoop, calls=%fused_computation.4 | loop fusion | flops 32 | bytes 256 | tf_op jit(solution)/shard_map/sub | solution.py:328
  58.1 0.6 %scatter_fusion = f32[1997]{0:T(1024)S(1)} fusion(f32[1997]{0:T(1024)S(1)} %copy.18, s32[16]{0:T(128)S(1)} %compare_select_fusion, f32[16]{0:T(128)S(1)} %bitcast_subtract_fusion), kind=kCustom, calls=%fused_computation.1 | custom fusion | bytes 256 | tf_op jit(solution)/shard_map/scatter | solution.py:329
  58.7 0.0 copy-start
  58.7 0.6 copy-done
  (2 shorter events, 0.0 us)
Async XLA Ops:
  1.3 7.6 %copy-start.4 = (s32[1,8]{1,0:T(1,128)S(1)}, s32[1,8]{1,0:T(1,128)}, u32[]{:S(2)}) copy-start(s32[1,8]{1,0:T(1,128)} %param.20) | copy-start | bytes 100
  8.5 4.6 %collective-permute-start = (f32[64,64,128]{2,1,0:T(8,128)}, f32[64,64,128]{2,1,0:T(8,128)S(1)}, u32[]{:S(2)}, u32[]{:S(2)}) collective-permute-start(f32[64,64,128]{2,1,0:T(8,128)} %pack.1.own_ref), channel_id=1, source_target_pairs={{0,1},{1,0},{2,3},{3,2},{4,5},{5,4},{6,7},{7,6},{8,9},{9,8},{10,11... | collective-permute-start | bytes 6291464 | tf_op jit(solution)/shard_map/ppermute | solution.py:292
  9.0 4.1 %collective-permute-start.1 = (s32[8]{0:T(128)S(1)}, s32[8]{0:T(128)S(1)}, u32[]{:S(2)}, u32[]{:S(2)}) collective-permute-start(s32[8]{0:T(128)S(1)} %bitcast.24), channel_id=1, source_target_pairs={{0,2},{1,3},{2,0},{3,1},{4,6},{5,7},{6,4},{7,5},{8,10},{9,11},{10,... | collective-permute-start | bytes 104 | tf_op jit(solution)/shard_map/ppermute | solution.py:286
  12.2 7.4 %copy-start.6 = (s32[16]{0:T(128)S(1)}, s32[16]{0:T(128)}, u32[]{:S(2)}) copy-start(s32[16]{0:T(128)} %param.21) | copy-start | bytes 196
  13.1 0.5 copy-start.5
  13.6 1.3 %copy-start.1 = (f32[64,64,128]{2,1,0:T(8,128)}, f32[64,64,128]{2,1,0:T(8,128)S(1)}, u32[]{:S(2)}) copy-start(f32[64,64,128]{2,1,0:T(8,128)S(1)} %collective-permute-done.partner_ref) | copy-start | bytes 6291460
  17.3 15.4 %collective-permute-start.2 = (f32[8,64,128]{2,1,0:T(8,128)}, f32[8,64,128]{2,1,0:T(8,128)S(1)}, u32[]{:S(2)}, u32[]{:S(2)}) collective-permute-start(f32[8,64,128]{2,1,0:T(8,128)} %pick.3), channel_id=1, source_target_pairs={{0,2},{1,3},{2,0},{3,1},{4,6},{5,7},{6,4},{7,5},{8,10},{9,11},{10,... | collective-permute-start | bytes 786440 | tf_op jit(solution)/shard_map/ppermute | solution.py:286
  32.7 0.8 %copy-start.2 = (f32[8,64,128]{2,1,0:T(8,128)}, f32[8,64,128]{2,1,0:T(8,128)S(1)}, u32[]{:S(2)}) copy-start(f32[8,64,128]{2,1,0:T(8,128)S(1)} %collective-permute-done.2.refs_1_) | copy-start | bytes 786436
  33.4 23.8 %copy-start.3 = (f32[16]{0:T(128)S(1)}, f32[16]{0:T(128)}, u32[]{:S(2)}) copy-start(f32[16]{0:T(128)} %gather_fusion) | copy-start | bytes 196
  58.7 0.6 %copy-start = (f32[1997]{0:T(1024)}, f32[1997]{0:T(1024)S(1)}, u32[]{:S(2)}) copy-start(f32[1997]{0:T(1024)S(1)} %scatter_fusion) | copy-start | bytes 23968

commit v2 on v0

v2 whole, which is shorter than its diff:
```python
import functools

import jax
import jax.numpy as jnp
from jax import lax
from jax.experimental import pallas as pl
from jax.experimental.pallas import tpu as pltpu
from jax.sharding import PartitionSpec as P

BLK = 128
HALF = 64
F32 = jnp.float32
BF16 = jnp.bfloat16
LIMITS = pltpu.CompilerParams(vmem_limit_bytes=24 * 1024 * 1024)


def in_hbm(x):
    return pltpu.with_memory_space_constraint(x, pltpu.HBM)


def pack_kernel(
    rate_hbm,
    left_hbm,
    right_hbm,
    decay_hbm,
    weight_hbm,
    out_ref,
    rate_ref,
    left_ref,
    right_ref,
    decay_ref,
    weight_ref,
    small_sems,
    sems,
):
    states, parts, _ = left_ref.shape
    chunks = sems.shape[1]
    group = parts // chunks
    small = [
        pltpu.make_async_copy(src, dst, small_sems.at[i])
        for i, (src, dst) in enumerate(
            ((rate_hbm, rate_ref), (decay_hbm, decay_ref), (weight_hbm, weight_ref))
        )
    ]
    for copy in small:
        copy.start()

    def copies(g):
        rows = pl.ds(g * group, group)
        return [
            pltpu.make_async_copy(src.at[:, rows, :], dst.at[:, rows, :], sems.at[i, g])
            for i, (src, dst) in enumerate(((left_hbm, left_ref), (right_hbm, right_ref)))
        ]

    for g in range(chunks):
        for copy in copies(g):
            copy.start()
    for copy in small:
        copy.wait()
    left = left_ref.reshape(states * parts, states)
    right = right_ref.reshape(states * parts, states)
    for g in range(chunks):
        for copy in copies(g):
            copy.wait()
        for q in range(g * group, (g + 1) * group):
            table = left[pl.ds(q, states, stride=parts), :]
            decay = decay_ref[pl.ds(q, 1), :]
            rows = jnp.concatenate(
                [table, decay, jnp.zeros((HALF - states - 1, states), F32)], axis=0
            )
            scale = jnp.concatenate(
                [
                    weight_ref[pl.ds(q, 1), :],
                    jnp.full((1, 1), -rate_ref[q], F32),
                    jnp.zeros((1, HALF - states - 1), F32),
                ],
                axis=1,
            )
            scaled = rows.T * scale
            other = right[pl.ds(q, states, stride=parts), :]
            tile = jnp.concatenate(
                [scaled, other, jnp.zeros((states, HALF - states), F32)], axis=1
            )
            out_ref[q] = jnp.concatenate(
                [tile, jnp.zeros((HALF - states, 2 * HALF), F32)], axis=0
            )


def pack_tables(left, right, decay, weight, rate):
    parts, states, _ = left.shape
    chunks = parts // 8
    hbm = pl.BlockSpec(memory_space=pltpu.HBM)
    table = pltpu.VMEM((states, parts, states), F32)
    row = pltpu.VMEM((parts, states), F32)
    return pl.pallas_call(
        pack_kernel,
        in_specs=[hbm] * 5,
        out_specs=pl.BlockSpec(memory_space=pltpu.VMEM),
        out_shape=jax.ShapeDtypeStruct((parts, HALF, 2 * HALF), F32),
        scratch_shapes=[
            pltpu.SMEM((parts,), F32),
            table,
            table,
            row,
            row,
            pltpu.SemaphoreType.DMA((3,)),
            pltpu.SemaphoreType.DMA((2, chunks)),
        ],
        name="pack",
        compiler_params=LIMITS,
    )(
        in_hbm(rate),
        in_hbm(jnp.transpose(left, (1, 0, 2))),
        in_hbm(jnp.transpose(right, (1, 0, 2))),
        in_hbm(decay),
        in_hbm(weight),
    )


def start_tiles(wanted_ref, pair, own_ref, partner_ref, out_ref, sems):
    owned = own_ref.shape[0]
    me = lax.axis_index("dom")
    for n in range(out_ref.shape[0]):
        part = wanted_ref[n]
        owner = part // owned
        row = part - owner * owned
        mine = owner == me

        @pl.when(mine)
        def _():
            pltpu.make_async_copy(own_ref.at[row], out_ref.at[n], sems.at[n]).start()

        @pl.when(jnp.logical_not(mine))
        def _():
            pltpu.make_async_copy(partner_ref.at[row], out_ref.at[n], sems.at[n]).start()


def wait_tiles(own_ref, out_ref, sems):
    for n in range(out_ref.shape[0]):
        pltpu.make_async_copy(own_ref.at[0], out_ref.at[n], sems.at[n]).wait()


def pick_kernel(pair, wanted_ref, own_ref, partner_ref, out_ref, sems):
    start_tiles(wanted_ref, pair, own_ref, partner_ref, out_ref, sems)
    wait_tiles(own_ref, out_ref, sems)


def pick_tiles(wanted, own, partner, pair):
    count = wanted.shape[0]
    hbm = pl.BlockSpec(memory_space=pl.ANY)
    return pl.pallas_call(
        functools.partial(pick_kernel, pair),
        in_specs=[pl.BlockSpec(memory_space=pltpu.SMEM), hbm, hbm],
        out_specs=pl.BlockSpec(memory_space=pltpu.VMEM),
        out_shape=jax.ShapeDtypeStruct((count,) + own.shape[1:], F32),
        scratch_shapes=[pltpu.SemaphoreType.DMA((count,))],
        name="pick",
        compiler_params=LIMITS,
    )(wanted, own, partner)


def prepare_kernel(
    pair,
    rounds,
    blocks_ref,
    chosen_ref,
    lengths_ref,
    top_hbm,
    bottom_hbm,
    own_ref,
    partner_ref,
    out_ref,
    tiles_ref,
    aux_ref,
    map_ref,
    top_ref,
    bottom_ref,
    tile_sems,
    sems,
):
    nblocks = out_ref.shape[0]
    chunks = sems.shape[1]
    chunk = top_ref.shape[0] // chunks
    columns = out_ref.shape[3] // chunks
    fused = columns // BLK
    states = chunk // (fused * nblocks)
    branches = chosen_ref.shape[0]

    def copies(g):
        rows = pl.ds(g * chunk, chunk)
        return [
            pltpu.make_async_copy(src.at[rows], dst.at[rows], sems.at[i, g])
            for i, (src, dst) in enumerate(((top_hbm, top_ref), (bottom_hbm, bottom_ref)))
        ]

    for g in range(chunks):
        for copy in copies(g):
            copy.start()
    start_tiles(blocks_ref, pair, own_ref, partner_ref, tiles_ref, tile_sems)
    owned = own_ref.shape[0]
    my_pair = lax.axis_index("dom") // pair
    lane = lax.broadcasted_iota(jnp.int32, (1, BLK), 1)
    flat = lax.broadcasted_iota(jnp.int32, map_ref.shape, 0) * BLK
    flat = flat + lax.broadcasted_iota(jnp.int32, map_ref.shape, 1)
    for n in range(nblocks):
        part = blocks_ref[n]
        distance = lax.rem(part // (owned * pair) - my_pair + rounds, rounds)
        aux_ref[pl.ds(n, 1), :] = jnp.full((1, BLK), distance.astype(F32), F32)
        aux_ref[pl.ds(nblocks + n, 1), :] = jnp.full((1, BLK), part.astype(F32), F32)
    along = jnp.zeros((1, BLK), F32)
    update = jnp.zeros(map_ref.shape, jnp.int32)
    for b in range(branches):
        place = chosen_ref[b]
        time = lengths_ref[place]
        aux_ref[pl.ds(2 * nblocks + b, 1), :] = jnp.full((1, BLK), time, F32)
        along = jnp.where(lane == b, time, along)
        update = jnp.where(flat == place, b + 1, update)
    aux_ref[pl.ds(2 * nblocks + branches, 1), :] = along
    map_ref[...] = update
    pad = jnp.zeros((HALF - states, BLK), F32)

    def step(g, carry):
        for copy in copies(g):
            copy.wait()
        for b in range(fused):
            for n in range(nblocks):
                for side, ref in enumerate((top_ref, bottom_ref)):
                    first = g * chunk + b * states * nblocks + n
                    rows = ref[pl.ds(first, states, stride=nblocks), :]
                    full = jnp.concatenate([rows, pad], axis=0)
                    high = full.astype(BF16)
                    low = (full - high.astype(F32)).astype(BF16)
                    lanes = pl.ds(pl.multiple_of(g * columns + b * BLK, BLK), BLK)
                    out_ref[n, side, pl.ds(0, HALF), lanes] = high
                    out_ref[n, side, pl.ds(HALF, HALF), lanes] = low
        return carry

    lax.fori_loop(0, chunks, step, 0)
    wait_tiles(own_ref, tiles_ref, tile_sems)


def prepare(blocks, chosen, lengths, top, bottom, own, partner, states, pair, rounds):
    nblocks = blocks.shape[0]
    branches = chosen.shape[0]
    chunks = branches // 2
    smem = pl.BlockSpec(memory_space=pltpu.SMEM)
    hbm = pl.BlockSpec(memory_space=pltpu.HBM)
    anywhere = pl.BlockSpec(memory_space=pl.ANY)
    vmem = pl.BlockSpec(memory_space=pltpu.VMEM)
    rows = -(-lengths.shape[0] // BLK)
    return pl.pallas_call(
        functools.partial(prepare_kernel, pair, rounds),
        in_specs=[smem, smem, smem, hbm, hbm, anywhere, anywhere],
        out_specs=[vmem] * 4,
        out_shape=[
            jax.ShapeDtypeStruct((nblocks, 2, 2 * HALF, branches * BLK), BF16),
            jax.ShapeDtypeStruct((nblocks,) + own.shape[1:], F32),
            jax.ShapeDtypeStruct((2 * nblocks + branches + 8, BLK), F32),
            jax.ShapeDtypeStruct((rows, BLK), jnp.int32),
        ],
        scratch_shapes=[
            pltpu.VMEM(top.shape, F32),
            pltpu.VMEM(top.shape, F32),
            pltpu.SemaphoreType.DMA((nblocks,)),
            pltpu.SemaphoreType.DMA((2, chunks)),
        ],
        name="prepare",
        compiler_params=LIMITS,
    )(blocks, chosen, lengths, in_hbm(top), in_hbm(bottom), own, partner)


def block_kernel(rounds, states, aux_ref, weight_ref, operand_ref, *refs):
    tiles = refs[:rounds]
    loglik_ref, share_ref = refs[rounds : rounds + 2]
    like_refs = refs[rounds + 2 :]
    branches, nblocks, _ = loglik_ref.shape
    wide = 2 * BLK
    lane = lax.broadcasted_iota(jnp.int32, (HALF, 2 * HALF), 1)
    is_left = lane < HALF
    for n in range(nblocks):
        distance = aux_ref[pl.ds(n, 1), :]
        tile = tiles[0][n]
        for r in range(1, rounds):
            tile = jnp.where(distance == float(r), tiles[r][n], tile)
        turned = pltpu.roll(tile, HALF, 1)
        sides = []
        for double in (jnp.where(is_left, tile, turned), jnp.where(is_left, turned, tile)):
            high = double.astype(BF16)
            low = (double - high.astype(F32)).astype(BF16)
            sides.append(jnp.concatenate([high, low[:, :HALF]], axis=1))
        expo = jnp.broadcast_to(tile[:, states : states + 1], (HALF, BLK))
        for c in range(branches * BLK // wide):
            columns = pl.ds(c * wide, wide)
            prods = []
            for side, lhs in enumerate(sides):
                part = operand_ref[n, side, :, columns]
                rhs = jnp.concatenate([part, part[:HALF]], axis=0)
                prods.append(jnp.dot(lhs, rhs, preferred_element_type=F32))
            joint = prods[0] * prods[1]
            for h in range(wide // BLK):
                b = c * (wide // BLK) + h
                time = aux_ref[pl.ds(2 * nblocks + b, 1), :]
                zeroth = joint[:, h * BLK : (h + 1) * BLK] * jnp.exp(expo * time)
                first = zeroth * expo
                second = first * expo
                for ref, term in zip(like_refs, (zeroth, first, second)):
                    ref[b, pl.ds(n, 1), :] = jnp.sum(term, axis=0, keepdims=True)

    weight = weight_ref[...].astype(F32)
    lanes = lax.broadcasted_iota(jnp.int32, (nblocks, BLK), 1)
    share = jnp.where(lanes == 2 * branches, aux_ref[pl.ds(nblocks, nblocks), :], 0.0)
    for b in range(branches):
        like = like_refs[0][b]
        first = like_refs[1][b] / like
        second = like_refs[2][b] / like - first * first
        loglik_ref[b] = weight * jnp.log(like)
        one = jnp.sum(weight * first, axis=1, keepdims=True)
        two = jnp.sum(weight * second, axis=1, keepdims=True)
        share = jnp.where(lanes == b, one, share)
        share = jnp.where(lanes == branches + b, two, share)
    for d in range(share_ref.shape[0]):
        share_ref[d] = share


def block_likelihoods(aux, weight, operand, tiles, branches, states, devices):
    nblocks = operand.shape[0]
    vmem = pl.BlockSpec(memory_space=pltpu.VMEM)
    return pl.pallas_call(
        functools.partial(block_kernel, len(tiles), states),
        in_specs=[vmem] * (3 + len(tiles)),
        out_specs=[vmem] * 2,
        out_shape=[
            jax.ShapeDtypeStruct((branches, nblocks, BLK), F32),
            jax.ShapeDtypeStruct((devices, nblocks, BLK), F32),
        ],
        scratch_shapes=[pltpu.VMEM((branches, nblocks, BLK), F32)] * 3,
        name="blocks",
        compiler_params=LIMITS,
    )(aux, weight, operand, *tiles)


def sum_kernel(nblocks, branches, aux_ref, map_ref, lengths_ref, share_ref, part_ref, new_ref):
    owned = part_ref.shape[1]
    terms = part_ref.shape[0]
    share = share_ref[...]
    rows = share.shape[0]
    parts = lax.broadcasted_iota(jnp.int32, (rows, owned), 1) + lax.axis_index("dom") * owned
    ident = share[:, terms : terms + 1].astype(jnp.int32)
    onehot = (ident == parts).astype(F32)
    sums = lax.dot_general(
        share,
        onehot,
        (((0,), (0,)), ((), ())),
        precision=lax.Precision.HIGHEST,
        preferred_element_type=F32,
    )
    part_ref[...] = sums[:terms]
    total = jnp.sum(share, axis=0, keepdims=True)
    second = pltpu.roll(total, BLK - branches, 1)
    updated = aux_ref[pl.ds(2 * nblocks + branches, 1), :] - total / second
    lane = lax.broadcasted_iota(jnp.int32, (1, BLK), 1)
    place = map_ref[...]
    new = lengths_ref[...]
    for b in range(branches):
        value = jnp.sum(jnp.where(lane == b, updated, 0.0), axis=1, keepdims=True)
        new = jnp.where(place == b + 1, value, new)
    new_ref[...] = new


def add_up(aux, places, lengths, share, nblocks, branches, owned):
    vmem = pl.BlockSpec(memory_space=pltpu.VMEM)
    return pl.pallas_call(
        functools.partial(sum_kernel, nblocks, branches),
        in_specs=[vmem] * 4,
        out_specs=[vmem] * 2,
        out_shape=[
            jax.ShapeDtypeStruct((2 * branches, owned), F32),
            jax.ShapeDtypeStruct(lengths.shape, F32),
        ],
        name="sums",
        compiler_params=LIMITS,
    )(aux, places, lengths, share)


def on_device(
    top_partial,
    bottom_partial,
    left_vectors,
    right_vectors,
    decay_rates,
    state_weights,
    part_rates,
    branch_lengths,
    pattern_weights,
    block_partition,
    chosen_branches,
):
    branches, states, _, sites_here = top_partial.shape
    nblocks = sites_here // BLK
    owned = left_vectors.shape[0]
    groups = lax.axis_size("dom")
    pair = 2 if groups % 2 == 0 else 1
    rounds = groups // pair

    def shifted(value, r):
        step = [
            (d, ((d // pair + r) % rounds) * pair + d % pair) for d in range(groups)
        ]
        return lax.ppermute(value, "dom", step)

    blocks = block_partition[0]
    requests = [shifted(blocks, rounds - r) for r in range(1, rounds)]
    own = pack_tables(left_vectors, right_vectors, decay_rates, state_weights, part_rates)
    if pair == 2:
        partner = lax.ppermute(own, "dom", [(d, d ^ 1) for d in range(groups)])
    else:
        partner = own
    answers = [
        shifted(pick_tiles(request, own, partner, pair), r)
        for r, request in zip(range(1, rounds), requests)
    ]
    operand, tiles, aux, places = prepare(
        blocks,
        chosen_branches,
        branch_lengths,
        top_partial.reshape(branches * states * nblocks, BLK),
        bottom_partial.reshape(branches * states * nblocks, BLK),
        own,
        partner,
        states,
        pair,
        rounds,
    )
    tiles = [tiles] + answers[::-1]
    devices = lax.axis_size("site") * groups
    loglik, share = block_likelihoods(
        aux,
        pattern_weights.reshape(nblocks, BLK),
        operand,
        tiles,
        branches,
        states,
        devices,
    )
    everything = lax.all_to_all(
        share, ("site", "dom"), split_axis=0, concat_axis=0, tiled=True
    )
    count = branch_lengths.shape[0]
    rows = places.shape[0]
    padded = jnp.pad(branch_lengths, (0, rows * BLK - count)).reshape(rows, BLK)
    parts, new_lengths = add_up(
        aux,
        places,
        padded,
        everything.reshape(devices * nblocks, BLK),
        nblocks,
        branches,
        owned,
    )
    new_lengths = new_lengths.reshape(rows * BLK)[:count]
    return (
        loglik.reshape(branches, 1, sites_here),
        parts.reshape(2, branches, owned),
        new_lengths,
    )


def solution(mesh):
    return jax.shard_map(
        on_device,
        mesh=mesh,
        in_specs=(
            P(None, None, "dom", "site"),
            P(None, None, "dom", "site"),
            P("dom", None, None),
            P("dom", None, None),
            P("dom", None),
            P("dom", None),
            P("dom"),
            P(),
            P("dom", "site"),
            P("dom", "site"),
            P(),
        ),
        out_specs=(P(None, "dom", "site"), P(None, None, "dom"), P()),
        check_vma=False,
    )
```

time: 123 us -> 41 us (0.33)
  blocking collectives: 46.6 us -> 0 us
  local copies, waits for them, and re-layouts: 25 us -> 0.02 us
  Pallas kernels: 0 us -> 16.7 us
  matrix products: 13.5 us -> 0 us
  other arithmetic: 11.7 us -> 0 us
  starting transfers between devices: 17.6 us -> 11.8 us
  waiting for transfers between devices: 6.6 us -> 11.6 us
    psum x1 -> x0, blocking collectives: 40.4 us -> none  [on_device(): everything = lax.psum(part_local, ('site', 'dom'))]
    pallas_call x0 -> x5, Pallas kernels: none -> 16.7 us  [the longest x1 6.23 us: pack_tables(): pl.pallas_call(pack_kernel, in_specs=[hbm] * 5, out_specs=pl.BlockSpec(me...]
    dot_general x3 -> x0, matrix products: 13.5 us -> none  [the longest x1 6.82 us: project(): jnp.einsum('nkj,bjnl->bknl', vec_right, lower, precision=lax.Precision.HI...]
    gather x7 -> x0, local copies, waits for them, and re-layouts: 12.5 us -> none  [the longest x1 4.97 us: on_device(): send_left = left_vectors[clipped] * inside[:, :, None, None]]
    all_to_all x5 -> x1, starting transfers between devices: 17.6 us -> 6.08 us  [on_device(): lax.all_to_all(share, ('site', 'dom'), split_axis=0, concat_axis=0, tiled...]
    unnamed x38 -> x8, local copies, waits for them, and re-layouts: 10.6 us -> 0.02 us
    all_to_all x4 -> x0, other arithmetic: 6.36 us -> none  [the longest x1 2.92 us: on_device(): lax.all_to_all(send_right, 'dom', split_axis=0, concat_axis=0, tiled=True)]
    all_gather x1 -> x0, blocking collectives: 6.22 us -> none  [on_device(): wanted = lax.all_gather(block_partition, 'dom', axis=0, tiled=True)]
  transfers between devices with their start and end apart: 5 -> 4, of which waited for: 3 -> 3; matrix products, arithmetic and copies ran while one was open for 23% -> 0% of each run, Pallas kernels for 0% -> 12%
where the time goes in v2:
time: 41 us; the launch traced here: 40.8 us
  Pallas kernels  16.7 us (41%)
  starting transfers between devices  11.8 us (29%)
  waiting for transfers between devices  11.6 us (28%)
  between operations  0.69 us (2%)
    all_to_all x1, waiting for transfers between devices, on_device(): lax.all_to_all(share, ('site', 'dom'), split_axis=0, concat_axis=0, tiled...  8.19 us
    pallas_call x1, Pallas kernels, pack_tables(): pl.pallas_call(pack_kernel, in_specs=[hbm] * 5, out_specs=pl.BlockSpec(me...  6.23 us
    all_to_all x1, starting transfers between devices, on_device(): lax.all_to_all(share, ('site', 'dom'), split_axis=0, concat_axis=0, tiled...  6.08 us
    ppermute x2, starting transfers between devices, shifted(): return lax.ppermute(value, 'dom', step)  5.17 us
    pallas_call x1, Pallas kernels, prepare(): pl.pallas_call(functools.partial(prepare_kernel, pair, rounds), in_specs=...  4.76 us
    pallas_call x1, Pallas kernels, block_likelihoods(): pl.pallas_call(functools.partial(block_kernel, len(tiles), states), in_sp...  3.67 us
    ppermute x2, waiting for transfers between devices, shifted(): return lax.ppermute(value, 'dom', step)  3.38 us
    pallas_call x1, Pallas kernels, pick_tiles(): pl.pallas_call(functools.partial(pick_kernel, pair), in_specs=[pl.BlockSp...  1.1 us
  transfers between devices with their start and end apart: 4, of which 3 were waited for; matrix products, arithmetic and copies ran while one was open for 0% of the time, Pallas kernels for 12%

profile of v2, /device:TPU:0, one launch (start us, length us, event | category | flops | bytes accessed | tf_op | source)
XLA Modules:
  0.0 40.8 jit_solution(9210047604746336706)
XLA Ops:
  0.6 0.0 copy-start.2
  0.6 6.2 %pack.1.own_ref = f32[64,64,128]{2,1,0:T(8,128)S(1)} custom-call(f32[64]{0:T(128)} %rate_hbm.1, f32[61,64,61]{2,1,0:T(8,128)} %bitcast.19, f32[61,64,61]{2,1,0:T(8,128)} %bitcast.20, f32[64,61]{1,0:T(8,128)} %decay_hbm.1, f32[64,61]{1,0:T(8,128)} %weight_hbm.1), custom_call_target="tpu_custom_call" | custom-call | tf_op jit(solution)/shard_map/pack/pallas_call | solution.py:95
  6.9 0.6 %collective-permute-start = (f32[64,64,128]{2,1,0:T(8,128)S(1)}, f32[64,64,128]{2,1,0:T(8,128)S(1)}, u32[]{:S(2)}, u32[]{:S(2)}) collective-permute-start(f32[64,64,128]{2,1,0:T(8,128)S(1)} %pack.1.own_ref), channel_id=1, source_target_pairs={{0,1},{1,0},{2,3},{3,2},{4,5},{5,4},{6,7},{7,6},{8,9},{9,8},{10,11... | collective-permute-start | bytes 6291464 | tf_op jit(solution)/shard_map/ppermute | solution.py:415
  7.4 0.0 copy-done.2
  7.4 0.0 copy-start
  7.4 0.0 copy-start.3
  7.4 2.6 %collective-permute-start.1 = (s32[8]{0:T(128)S(1)}, s32[8]{0:T(128)S(1)}, u32[]{:S(2)}, u32[]{:S(2)}) collective-permute-start(s32[8]{0:T(128)S(1)} %bitcast.15), channel_id=1, source_target_pairs={{0,2},{1,3},{2,0},{3,1},{4,6},{5,7},{6,4},{7,5},{8,10},{9,11},{10,... | collective-permute-start | bytes 104 | tf_op jit(solution)/shard_map/ppermute | solution.py:409
  10.1 1.5 %collective-permute-done.1.wanted_ref = s32[8]{0:T(128)S(1)} collective-permute-done((s32[8]{0:T(128)S(1)}, s32[8]{0:T(128)S(1)}, u32[]{:S(2)}, u32[]{:S(2)}) %collective-permute-start.1) | collective-permute-done | bytes 64 | tf_op jit(solution)/shard_map/ppermute | solution.py:409
  11.6 0.0 collective-permute-done.partner_ref
  11.6 1.1 %pick.1 = f32[8,64,128]{2,1,0:T(8,128)S(1)} custom-call(s32[8]{0:T(128)S(1)} %collective-permute-done.1.wanted_ref, f32[64,64,128]{2,1,0:T(8,128)S(1)} %pack.1.own_ref, f32[64,64,128]{2,1,0:T(8,128)S(1)} %collective-permute-done.partner_ref), custom_call_target="tpu_custom_call" | custom-call | tf_op jit(solution)/shard_map/pick/pallas_call | solution.py:151
  12.7 2.6 %collective-permute-start.2 = (f32[8,64,128]{2,1,0:T(8,128)S(1)}, f32[8,64,128]{2,1,0:T(8,128)S(1)}, u32[]{:S(2)}, u32[]{:S(2)}) collective-permute-start(f32[8,64,128]{2,1,0:T(8,128)S(1)} %pick.1), channel_id=1, source_target_pairs={{0,2},{1,3},{2,0},{3,1},{4,6},{5,7},{6,4},{7,5},{8,10},{9,11},{10,... | collective-permute-start | bytes 786440 | tf_op jit(solution)/shard_map/ppermute | solution.py:409
  15.3 0.0 copy-done
  15.3 0.0 copy-done.3
  15.3 0.0 copy-start.1
  15.3 4.8 %prepare.1 = (bf16[8,2,128,2048]{3,2,1,0:T(8,128)(2,1)S(1)}, f32[8,64,128]{2,1,0:T(8,128)S(1)}, f32[40,128]{1,0:T(8,128)S(1)}, s32[16,128]{1,0:T(8,128)S(1)}) custom-call(s32[8]{0:T(128)S(1)} %bitcast.16, s32[16]{0:T(128)S(1)} %copy-done.3, f32[1997]{0:T(1024)S(1)} %copy-done, f32[7808,128]{1,0:T(8,128)} %bitcast.17, f32[7808,128]{1,0:T(8,128)} %bitcast.18, ...), custom_call_target="tpu_custom_call" | custom-call | tf_op jit(solution)/shard_map/prepare/pallas_call | solution.py:251
  20.1 1.8 %collective-permute-done.2.refs_1_ = f32[8,64,128]{2,1,0:T(8,128)S(1)} collective-permute-done((f32[8,64,128]{2,1,0:T(8,128)S(1)}, f32[8,64,128]{2,1,0:T(8,128)S(1)}, u32[]{:S(2)}, u32[]{:S(2)}) %collective-permute-start.2) | collective-permute-done | bytes 262176 | tf_op jit(solution)/shard_map/ppermute | solution.py:409
  21.9 0.0 copy-done.1
  21.9 3.7 %blocks.1 = (f32[16,8,128]{2,1,0:T(8,128)}, f32[32,8,128]{2,1,0:T(8,128)}) custom-call(f32[40,128]{1,0:T(8,128)S(1)} %get-tuple-element.11.aux_ref, s32[8,128]{1,0:T(8,128)S(1)} %bitcast.14, bf16[8,2,128,2048]{3,2,1,0:T(8,128)(2,1)S(1)} %get-tuple-element.12.operand_ref, f32[8,64,128]{2,1,0:T(8,128)S(1)} %get-tuple-element.13.refs_0_, ...), custom_call_target="tpu_custom_call" | custom-call | tf_op jit(solution)/shard_map/blocks/pallas_call | solution.py:328
  25.6 6.1 %all-to-all-start = ((f32[32,8,128]{2,1,0:T(8,128)}), f32[32,8,128]{2,1,0:T(8,128)S(1)}, u32[]{:S(2)}, u32[]{:S(2)}) async-start(f32[32,8,128]{2,1,0:T(8,128)} %get-tuple-element.16), calls=%async_computation | async-start | bytes 262144 | tf_op jit(solution)/shard_map/all_to_all | solution.py:445
  31.6 8.2 %all-to-all-done = f32[32,8,128]{2,1,0:T(8,128)S(1)} async-done(((f32[32,8,128]{2,1,0:T(8,128)}), f32[32,8,128]{2,1,0:T(8,128)S(1)}, u32[]{:S(2)}, u32[]{:S(2)}) %all-to-all-start) | async-done | bytes 131104 | tf_op jit(solution)/shard_map/all_to_all | solution.py:445
  39.8 1.0 %sums.1 = (f32[32,64]{1,0:T(8,128)}, f32[16,128]{1,0:T(8,128)}) custom-call(f32[40,128]{1,0:T(8,128)S(1)} %get-tuple-element.11.aux_ref, s32[16,128]{1,0:T(8,128)S(1)} %get-tuple-element.15.map_ref, f32[16,128]{1,0:T(8,128)S(1)} %pad_bitcast_fusion.lengths_ref, f32[256,128]{1,0:T(8,128)S(1)} %bitcast.13), custom_call_target="tpu_custom_call" | custom-call | tf_op jit(solution)/shard_map/sums/pallas_call | solution.py:372
  (1 shorter events, 0.0 us)
Async XLA Ops:
  0.6 6.8 %copy-start.2 = (s32[1,8]{1,0:T(1,128)S(1)}, s32[1,8]{1,0:T(1,128)}, u32[]{:S(2)}) copy-start(s32[1,8]{1,0:T(1,128)} %param.20) | copy-start | bytes 100
  6.9 4.7 %collective-permute-start = (f32[64,64,128]{2,1,0:T(8,128)S(1)}, f32[64,64,128]{2,1,0:T(8,128)S(1)}, u32[]{:S(2)}, u32[]{:S(2)}) collective-permute-start(f32[64,64,128]{2,1,0:T(8,128)S(1)} %pack.1.own_ref), channel_id=1, source_target_pairs={{0,1},{1,0},{2,3},{3,2},{4,5},{5,4},{6,7},{7,6},{8,9},{9,8},{10,11... | collective-permute-start | bytes 6291464 | tf_op jit(solution)/shard_map/ppermute | solution.py:415
  7.4 7.8 %copy-start = (f32[1997]{0:T(1024)S(1)}, f32[1997]{0:T(1024)}, u32[]{:S(2)}) copy-start(f32[1997]{0:T(1024)} %lengths_ref.1) | copy-start | bytes 23968
  7.4 7.8 %copy-start.3 = (s32[16]{0:T(128)S(1)}, s32[16]{0:T(128)}, u32[]{:S(2)}) copy-start(s32[16]{0:T(128)} %chosen_ref.1) | copy-start | bytes 196
  7.4 4.2 %collective-permute-start.1 = (s32[8]{0:T(128)S(1)}, s32[8]{0:T(128)S(1)}, u32[]{:S(2)}, u32[]{:S(2)}) collective-permute-start(s32[8]{0:T(128)S(1)} %bitcast.15), channel_id=1, source_target_pairs={{0,2},{1,3},{2,0},{3,1},{4,6},{5,7},{6,4},{7,5},{8,10},{9,11},{10,... | collective-permute-start | bytes 104 | tf_op jit(solution)/shard_map/ppermute | solution.py:409
  12.7 9.2 %collective-permute-start.2 = (f32[8,64,128]{2,1,0:T(8,128)S(1)}, f32[8,64,128]{2,1,0:T(8,128)S(1)}, u32[]{:S(2)}, u32[]{:S(2)}) collective-permute-start(f32[8,64,128]{2,1,0:T(8,128)S(1)} %pick.1), channel_id=1, source_target_pairs={{0,2},{1,3},{2,0},{3,1},{4,6},{5,7},{6,4},{7,5},{8,10},{9,11},{10,... | collective-permute-start | bytes 786440 | tf_op jit(solution)/shard_map/ppermute | solution.py:409
  15.3 6.6 %copy-start.1 = (s32[1,1024]{1,0:T(1,128)S(1)}, s32[1,1024]{1,0:T(1,128)}, u32[]{:S(2)}) copy-start(s32[1,1024]{1,0:T(1,128)} %param.19) | copy-start | bytes 12292
  25.6 14.3 %all-to-all-start = ((f32[32,8,128]{2,1,0:T(8,128)}), f32[32,8,128]{2,1,0:T(8,128)S(1)}, u32[]{:S(2)}, u32[]{:S(2)}) async-start(f32[32,8,128]{2,1,0:T(8,128)} %get-tuple-element.16), calls=%async_computation | async-start | bytes 262144 | tf_op jit(solution)/shard_map/all_to_all | solution.py:445

commit v3 on v2

v3 whole, which is shorter than its diff:
```python
import functools

import jax
import jax.numpy as jnp
from jax import lax
from jax.experimental import pallas as pl
from jax.experimental.pallas import tpu as pltpu
from jax.sharding import PartitionSpec as P

BLK = 128
HALF = 64
SUB = 8
LOG2_E = 1.4426950408889634
F32 = jnp.float32
BF16 = jnp.bfloat16
LIMITS = pltpu.CompilerParams(vmem_limit_bytes=24 * 1024 * 1024)


def in_hbm(x):
    return pltpu.with_memory_space_constraint(x, pltpu.HBM)


def pack_kernel(
    rate_hbm,
    left_hbm,
    right_hbm,
    decay_hbm,
    weight_hbm,
    out_ref,
    rate_ref,
    left_ref,
    right_ref,
    decay_ref,
    weight_ref,
    small_sems,
    sems,
):
    chunks, states, group, _ = left_ref.shape
    small = [
        pltpu.make_async_copy(src, dst, small_sems.at[i])
        for i, (src, dst) in enumerate(
            ((rate_hbm, rate_ref), (decay_hbm, decay_ref), (weight_hbm, weight_ref))
        )
    ]
    for copy in small:
        copy.start()

    def copies(g):
        rows = pl.ds(g * group, group)
        return [
            pltpu.make_async_copy(src.at[:, rows, :], dst.at[g], sems.at[i, g])
            for i, (src, dst) in enumerate(((left_hbm, left_ref), (right_hbm, right_ref)))
        ]

    for g in range(chunks):
        for copy in copies(g):
            copy.start()
    for copy in small:
        copy.wait()
    left = left_ref.reshape(chunks * states * group, states)
    right = right_ref.reshape(chunks * states * group, states)
    for g in range(chunks):
        for copy in copies(g):
            copy.wait()
        for q in range(g * group, (g + 1) * group):
            rows_of = pl.ds(g * states * group + q - g * group, states, stride=group)
            table = left[rows_of, :]
            decay = decay_ref[pl.ds(q, 1), :]
            rows = jnp.concatenate(
                [table, decay, jnp.zeros((HALF - states - 1, states), F32)], axis=0
            )
            scale = jnp.concatenate(
                [
                    weight_ref[pl.ds(q, 1), :],
                    jnp.full((1, 1), -rate_ref[q], F32),
                    jnp.zeros((1, HALF - states - 1), F32),
                ],
                axis=1,
            )
            scaled = rows.T * scale
            other = right[rows_of, :]
            tile = jnp.concatenate(
                [scaled, other, jnp.zeros((states, HALF - states), F32)], axis=1
            )
            out_ref[q] = jnp.concatenate(
                [tile, jnp.zeros((HALF - states, 2 * HALF), F32)], axis=0
            )


def pack_tables(left, right, decay, weight, rate):
    parts, states, _ = left.shape
    group = 8
    chunks = parts // group
    hbm = pl.BlockSpec(memory_space=pltpu.HBM)
    table = pltpu.VMEM((chunks, states, group, states), F32)
    row = pltpu.VMEM((parts, states), F32)
    return pl.pallas_call(
        pack_kernel,
        in_specs=[hbm] * 5,
        out_specs=pl.BlockSpec(memory_space=pltpu.VMEM),
        out_shape=jax.ShapeDtypeStruct((parts, HALF, 2 * HALF), F32),
        scratch_shapes=[
            pltpu.SMEM((parts,), F32),
            table,
            table,
            row,
            row,
            pltpu.SemaphoreType.DMA((3,)),
            pltpu.SemaphoreType.DMA((2, chunks)),
        ],
        name="pack",
        compiler_params=LIMITS,
    )(
        in_hbm(rate),
        in_hbm(jnp.transpose(left, (1, 0, 2))),
        in_hbm(jnp.transpose(right, (1, 0, 2))),
        in_hbm(decay),
        in_hbm(weight),
    )


def copy_tiles(wanted_ref, own_ref, partner_ref, *out_refs):
    owned = own_ref.shape[0]
    base = lax.axis_index("dom") * owned
    place = 0
    for out_ref in out_refs:
        for n in range(out_ref.shape[0]):
            part = wanted_ref[place]
            row = lax.rem(part, owned)
            mine = part - row == base
            chosen = jnp.full((1, own_ref.shape[2]), mine.astype(jnp.int32))
            out_ref[n] = jnp.where(chosen == 1, own_ref[row], partner_ref[row])
            place += 1


def pick_tiles(wanted, own, partner, pieces):
    vmem = pl.BlockSpec(memory_space=pltpu.VMEM)
    count = wanted.shape[0] // pieces
    return pl.pallas_call(
        copy_tiles,
        in_specs=[pl.BlockSpec(memory_space=pltpu.SMEM), vmem, vmem],
        out_specs=[vmem] * pieces,
        out_shape=[jax.ShapeDtypeStruct((count,) + own.shape[1:], F32)] * pieces,
        name="pick",
        compiler_params=LIMITS,
    )(wanted, own, partner)


def prepare_kernel(
    pair,
    rounds,
    blocks_ref,
    chosen_ref,
    lengths_ref,
    padded_ref,
    top_hbm,
    bottom_hbm,
    own_ref,
    partner_ref,
    out_ref,
    tiles_ref,
    aux_ref,
    map_ref,
    rows_ref,
    top_ref,
    bottom_ref,
    sems,
):
    nblocks = out_ref.shape[0]
    chunks = sems.shape[1]
    chunk = top_ref.shape[0] // chunks
    columns = out_ref.shape[3] // chunks
    fused = columns // BLK
    states = chunk // (fused * nblocks)
    branches = chosen_ref.shape[0]

    def copies(g):
        rows = pl.ds(g * chunk, chunk)
        return [
            pltpu.make_async_copy(src.at[rows], dst.at[rows], sems.at[i, g])
            for i, (src, dst) in enumerate(((top_hbm, top_ref), (bottom_hbm, bottom_ref)))
        ]

    for g in range(chunks):
        for copy in copies(g):
            copy.start()
    copy_tiles(blocks_ref, own_ref, partner_ref, tiles_ref)
    owned = own_ref.shape[0]
    my_pair = lax.axis_index("dom") // pair
    lane = lax.broadcasted_iota(jnp.int32, (1, BLK), 1)
    flat = lax.broadcasted_iota(jnp.int32, map_ref.shape, 0) * BLK
    flat = flat + lax.broadcasted_iota(jnp.int32, map_ref.shape, 1)
    for n in range(nblocks):
        part = blocks_ref[n]
        distance = lax.rem(lax.div(part, owned * pair) - my_pair + rounds, rounds)
        aux_ref[pl.ds(n, 1), :] = jnp.full((1, BLK), distance.astype(F32), F32)
        aux_ref[pl.ds(nblocks + n, 1), :] = jnp.full((1, BLK), part.astype(F32), F32)
    along = jnp.zeros((1, BLK), F32)
    update = jnp.zeros(map_ref.shape, jnp.int32)
    for b in range(branches):
        place = chosen_ref[b]
        time = lengths_ref[place]
        aux_ref[pl.ds(2 * nblocks + 8 + b, 1), :] = jnp.full((1, BLK), time, F32)
        along = jnp.where(lane == b, time, along)
        update = jnp.where(flat == place, b + 1, update)
    aux_ref[pl.ds(2 * nblocks, 1), :] = along
    map_ref[...] = update
    rows_ref[...] = padded_ref[...]
    pad = jnp.zeros((HALF - states, BLK), F32)

    def step(g, carry):
        for copy in copies(g):
            copy.wait()
        for b in range(fused):
            for n in range(nblocks):
                for side, ref in enumerate((top_ref, bottom_ref)):
                    first = g * chunk + b * states * nblocks + n
                    rows = ref[pl.ds(first, states, stride=nblocks), :]
                    full = jnp.concatenate([rows, pad], axis=0)
                    high = full.astype(BF16)
                    low = (full - high.astype(F32)).astype(BF16)
                    lanes = pl.ds(pl.multiple_of(g * columns + b * BLK, BLK), BLK)
                    out_ref[n, side, pl.ds(0, HALF), lanes] = high
                    out_ref[n, side, pl.ds(HALF, HALF), lanes] = low
        return carry

    lax.fori_loop(0, chunks, step, 0)


def prepare(blocks, chosen, lengths, padded, top, bottom, own, partner, states, pair, rounds):
    nblocks = blocks.shape[0]
    branches = chosen.shape[0]
    chunks = branches // 2
    smem = pl.BlockSpec(memory_space=pltpu.SMEM)
    hbm = pl.BlockSpec(memory_space=pltpu.HBM)
    vmem = pl.BlockSpec(memory_space=pltpu.VMEM)
    return pl.pallas_call(
        functools.partial(prepare_kernel, pair, rounds),
        in_specs=[smem, smem, smem, vmem, hbm, hbm, vmem, vmem],
        out_specs=[vmem] * 5,
        out_shape=[
            jax.ShapeDtypeStruct((nblocks, 2, 2 * HALF, branches * BLK), BF16),
            jax.ShapeDtypeStruct((nblocks,) + own.shape[1:], F32),
            jax.ShapeDtypeStruct((2 * nblocks + 8 + branches, BLK), F32),
            jax.ShapeDtypeStruct(padded.shape, jnp.int32),
            jax.ShapeDtypeStruct(padded.shape, F32),
        ],
        scratch_shapes=[
            pltpu.VMEM(top.shape, F32),
            pltpu.VMEM(top.shape, F32),
            pltpu.SemaphoreType.DMA((2, chunks)),
        ],
        name="prepare",
        compiler_params=LIMITS,
    )(blocks, chosen, lengths, padded, in_hbm(top), in_hbm(bottom), own, partner)


def block_kernel(rounds, states, pieces, piece, aux_ref, weight_ref, operand_ref, own_ref, *refs):
    tiles = refs[: rounds - 1]
    earlier = refs[rounds - 1 : rounds - 1 + (piece if piece == pieces - 1 else 0)]
    like_ref, terms_ref, partial_ref = refs[-3:]
    branches, count, _ = like_ref.shape
    nblocks = operand_ref.shape[0]
    start = piece * count
    wide = 2 * BLK
    lane = lax.broadcasted_iota(jnp.int32, (HALF, 2 * HALF), 1)
    is_left = lane < HALF
    for m in range(count):
        n = start + m
        distance = aux_ref[pl.ds(n, 1), :]
        tile = own_ref[n]
        for r in range(1, rounds):
            tile = jnp.where(distance == float(r), tiles[r - 1][m], tile)
        turned = pltpu.roll(tile, HALF, 1)
        sides = []
        for double in (jnp.where(is_left, tile, turned), jnp.where(is_left, turned, tile)):
            high = double.astype(BF16)
            low = (double - high.astype(F32)).astype(BF16)
            sides.append(jnp.concatenate([high, low[:, :HALF]], axis=1))
        expo = jnp.broadcast_to(tile[:, states : states + 1], (HALF, BLK))
        scaled = expo * LOG2_E
        for c in range(branches * BLK // wide):
            columns = pl.ds(c * wide, wide)
            prods = []
            for side, lhs in enumerate(sides):
                part = operand_ref[n, side, :, columns]
                rhs = jnp.concatenate([part, part[:HALF]], axis=0)
                prods.append(jnp.dot(lhs, rhs, preferred_element_type=F32))
            joint = prods[0] * prods[1]
            for h in range(wide // BLK):
                b = c * (wide // BLK) + h
                time = aux_ref[pl.ds(2 * nblocks + 8 + b, 1), :]
                zeroth = joint[:, h * BLK : (h + 1) * BLK] * jnp.exp2(scaled * time)
                first = zeroth * expo
                second = first * expo
                for i, term in enumerate((zeroth, first, second)):
                    total = term[:SUB]
                    for k in range(SUB, HALF, SUB):
                        total = total + term[k : k + SUB]
                    partial_ref[i, b, pl.ds(m * SUB, SUB), :] = total

    weight = weight_ref[pl.ds(start, count), :].astype(F32)
    lanes = lax.broadcasted_iota(jnp.int32, (count, BLK), 1)
    terms = jnp.where(lanes == 2 * branches, aux_ref[pl.ds(nblocks + start, count), :], 0.0)
    for b in range(branches):
        sums = []
        for i in range(3):
            total = partial_ref[i, b, pl.ds(0, count, stride=SUB), :]
            for j in range(1, SUB):
                total = total + partial_ref[i, b, pl.ds(j, count, stride=SUB), :]
            sums.append(total)
        like_ref[b] = sums[0]
        inverse = 1.0 / sums[0]
        first = sums[1] * inverse
        second = sums[2] * inverse - first * first
        one = jnp.sum(weight * first, axis=1, keepdims=True)
        two = jnp.sum(weight * second, axis=1, keepdims=True)
        terms = jnp.where(lanes == b, one, terms)
        terms = jnp.where(lanes == branches + b, two, terms)
    if piece < pieces - 1:
        terms_ref[...] = terms
    else:
        for ref in earlier:
            terms = ref[...] + pltpu.roll(terms, HALF, 1)
        for d in range(terms_ref.shape[0]):
            terms_ref[d] = terms


def block_likelihoods(
    aux, weight, operand, own_tiles, tiles, earlier, branches, states, devices, pieces, piece
):
    nblocks = operand.shape[0]
    count = nblocks // pieces
    vmem = pl.BlockSpec(memory_space=pltpu.VMEM)
    last = piece == pieces - 1
    return pl.pallas_call(
        functools.partial(block_kernel, len(tiles) + 1, states, pieces, piece),
        in_specs=[vmem] * (4 + len(tiles) + len(earlier)),
        out_specs=[vmem] * 2,
        out_shape=[
            jax.ShapeDtypeStruct((branches, count, BLK), F32),
            jax.ShapeDtypeStruct(((devices,) if last else ()) + (count, BLK), F32),
        ],
        scratch_shapes=[pltpu.VMEM((3, branches, count * SUB, BLK), F32)],
        name="blocks",
        compiler_params=LIMITS,
    )(aux, weight, operand, own_tiles, *tiles, *earlier)


def sum_kernel(aux_ref, map_ref, lengths_ref, weight_ref, share_ref, *refs):
    like_refs = refs[:-3]
    part_ref, new_ref, loglik_ref = refs[-3:]
    branches, count, _ = like_refs[0].shape
    nblocks = count * len(like_refs)
    owned = part_ref.shape[1]
    terms = part_ref.shape[0]
    share = share_ref[...]
    if len(like_refs) > 1:
        share = jnp.concatenate([share, pltpu.roll(share, HALF, 1)], axis=0)
    share = share[:, :HALF]
    parts = lax.broadcasted_iota(jnp.int32, (share.shape[0], owned), 1)
    parts = parts + lax.axis_index("dom") * owned
    ident = share[:, terms : terms + 1].astype(jnp.int32)
    onehot = (ident == parts).astype(F32)
    sums = lax.dot_general(
        share,
        onehot,
        (((0,), (0,)), ((), ())),
        precision=lax.Precision.HIGHEST,
        preferred_element_type=F32,
    )
    part_ref[...] = sums[:terms]
    total = jnp.sum(share, axis=0, keepdims=True)
    total = jnp.concatenate([total, total], axis=1)
    second = pltpu.roll(total, BLK - branches, 1)
    updated = aux_ref[pl.ds(2 * nblocks, 1), :] - total / second
    lane = lax.broadcasted_iota(jnp.int32, (1, BLK), 1)
    place = map_ref[...]
    new = lengths_ref[...]
    for b in range(branches):
        value = jnp.sum(jnp.where(lane == b, updated, 0.0), axis=1, keepdims=True)
        new = jnp.where(place == b + 1, value, new)
    new_ref[...] = new
    for i, like_ref in enumerate(like_refs):
        blocks = pl.ds(i * count, count)
        weight = weight_ref[blocks, :].astype(F32)
        for b in range(branches):
            loglik_ref[b, blocks, :] = weight * jnp.log(like_ref[b])


def add_up(aux, places, lengths, weight, share, likes, owned):
    vmem = pl.BlockSpec(memory_space=pltpu.VMEM)
    branches = likes[0].shape[0]
    nblocks = weight.shape[0]
    return pl.pallas_call(
        sum_kernel,
        in_specs=[vmem] * (5 + len(likes)),
        out_specs=[vmem] * 3,
        out_shape=[
            jax.ShapeDtypeStruct((2 * branches, owned), F32),
            jax.ShapeDtypeStruct(lengths.shape, F32),
            jax.ShapeDtypeStruct((branches, nblocks, BLK), F32),
        ],
        name="sums",
        compiler_params=LIMITS,
    )(aux, places, lengths, weight, share, *likes)


def on_device(
    top_partial,
    bottom_partial,
    left_vectors,
    right_vectors,
    decay_rates,
    state_weights,
    part_rates,
    branch_lengths,
    pattern_weights,
    block_partition,
    chosen_branches,
):
    branches, states, _, sites_here = top_partial.shape
    nblocks = sites_here // BLK
    owned = left_vectors.shape[0]
    groups = lax.axis_size("dom")
    pair = 2 if groups % 2 == 0 else 1
    rounds = groups // pair

    def shifted(value, r):
        step = [
            (d, ((d // pair + r) % rounds) * pair + d % pair) for d in range(groups)
        ]
        return lax.ppermute(value, "dom", step)

    blocks = block_partition[0]
    requests = [shifted(blocks, rounds - r) for r in range(1, rounds)]
    own = pack_tables(left_vectors, right_vectors, decay_rates, state_weights, part_rates)
    if pair == 2:
        partner = lax.ppermute(own, "dom", [(d, d ^ 1) for d in range(groups)])
    else:
        partner = own
    pieces = 2 if nblocks % 2 == 0 else 1
    answers = []
    for r, request in zip(range(1, rounds), requests):
        answers.append([shifted(t, r) for t in pick_tiles(request, own, partner, pieces)])
    count = branch_lengths.shape[0]
    rows = -(-count // BLK)
    padded = jnp.pad(branch_lengths, (0, rows * BLK - count)).reshape(rows, BLK)
    operand, tiles, aux, places, lengths = prepare(
        blocks,
        chosen_branches,
        branch_lengths,
        padded,
        top_partial.reshape(branches * states * nblocks, BLK),
        bottom_partial.reshape(branches * states * nblocks, BLK),
        own,
        partner,
        states,
        pair,
        rounds,
    )
    answers = answers[::-1]
    devices = lax.axis_size("site") * groups
    weight = pattern_weights.reshape(nblocks, BLK)
    likes, earlier = [], []
    for piece in range(pieces):
        like, terms = block_likelihoods(
            aux,
            weight,
            operand,
            tiles,
            [answer[piece] for answer in answers],
            earlier,
            branches,
            states,
            devices,
            pieces,
            piece,
        )
        likes.append(like)
        earlier = [terms]
    everything = lax.all_to_all(
        terms, ("site", "dom"), split_axis=0, concat_axis=0, tiled=True
    )
    parts, new_lengths, loglik = add_up(
        aux, places, lengths, weight, everything.reshape(-1, BLK), likes, owned
    )
    new_lengths = new_lengths.reshape(rows * BLK)[:count]
    return (
        loglik.reshape(branches, 1, sites_here),
        parts.reshape(2, branches, owned),
        new_lengths,
    )


def solution(mesh):
    return jax.shard_map(
        on_device,
        mesh=mesh,
        in_specs=(
            P(None, None, "dom", "site"),
            P(None, None, "dom", "site"),
            P("dom", None, None),
            P("dom", None, None),
            P("dom", None),
            P("dom", None),
            P("dom"),
            P(),
            P("dom", "site"),
            P("dom", "site"),
            P(),
        ),
        out_specs=(P(None, "dom", "site"), P(None, None, "dom"), P()),
        check_vma=False,
    )
```

time: 41 us -> 35.5 us (0.87)
  blocking collectives: 0 us -> 13.3 us
  waiting for transfers between devices: 11.6 us -> 1.77 us
  starting transfers between devices: 11.8 us -> 5.8 us
  Pallas kernels: 16.7 us -> 13.7 us
    all_to_all x0 -> x1, blocking collectives: none -> 13.3 us  [on_device(): lax.all_to_all(terms, ('site', 'dom'), split_axis=0, concat_axis=0, tiled...]
    all_to_all x1 -> x0, waiting for transfers between devices: 8.19 us -> none  [on_device(): lax.all_to_all(share, ('site', 'dom'), split_axis=0, concat_axis=0, tiled...]
    all_to_all x1 -> x0, starting transfers between devices: 6.08 us -> none  [on_device(): lax.all_to_all(share, ('site', 'dom'), split_axis=0, concat_axis=0, tiled...]
    pallas_call x1, Pallas kernels: 6.23 us -> 4.21 us  [pack_tables(): pl.pallas_call(pack_kernel, in_specs=[hbm] * 5, out_specs=pl.BlockSpec(me...]
    ppermute x2 -> x3, waiting for transfers between devices: 3.38 us -> 1.77 us  [shifted(): return lax.ppermute(value, 'dom', step)]
    pallas_call x3 -> x4, Pallas kernels: 5.72 us -> 4.85 us  [the longest x2 3.22 us: block_likelihoods(): pl.pallas_call(functools.partial(block_kernel, len(tiles) + 1, states, pi...]
    ppermute x2 -> x3, starting transfers between devices: 5.17 us -> 5.25 us  [shifted(): return lax.ppermute(value, 'dom', step)]
  transfers between devices with their start and end apart: 4 -> 4, of which waited for: 3 -> 2; matrix products, arithmetic and copies ran while one was open for 0% -> 0% of each run, Pallas kernels for 12% -> 18%
where the time goes in v3:
time: 35.5 us; the launch traced here: 35.3 us
  Pallas kernels  13.7 us (39%)
  blocking collectives  13.3 us (37%)
  starting transfers between devices  5.8 us (16%)
  waiting for transfers between devices  1.77 us (5%)
  between operations  0.7 us (2%)
    all_to_all x1, blocking collectives, on_device(): lax.all_to_all(terms, ('site', 'dom'), split_axis=0, concat_axis=0, tiled...  13.3 us
    ppermute x3, starting transfers between devices, shifted(): return lax.ppermute(value, 'dom', step)  5.25 us
    pallas_call x1, Pallas kernels, prepare(): pl.pallas_call(functools.partial(prepare_kernel, pair, rounds), in_specs=...  4.68 us
    pallas_call x1, Pallas kernels, pack_tables(): pl.pallas_call(pack_kernel, in_specs=[hbm] * 5, out_specs=pl.BlockSpec(me...  4.21 us
    pallas_call x2, Pallas kernels, block_likelihoods(): pl.pallas_call(functools.partial(block_kernel, len(tiles) + 1, states, pi...  3.22 us
    ppermute x3, waiting for transfers between devices, shifted(): return lax.ppermute(value, 'dom', step)  1.77 us
    pallas_call x1, Pallas kernels, add_up(): pl.pallas_call(sum_kernel, in_specs=[vmem] * (5 + len(likes)), out_specs=...  1.05 us
  transfers between devices with their start and end apart: 4, of which 2 were waited for; matrix products, arithmetic and copies ran while one was open for 0% of the time, Pallas kernels for 18%

profile of v3, /device:TPU:0, one launch (start us, length us, event | category | flops | bytes accessed | tf_op | source)
XLA Modules:
  0.0 35.3 jit_solution(3291569520430756743)
XLA Ops:
  0.6 0.0 copy-start.2
  0.6 4.2 %pack.1.own_ref = f32[64,64,128]{2,1,0:T(8,128)S(1)} custom-call(f32[64]{0:T(128)} %rate_hbm.1, f32[61,64,61]{2,1,0:T(8,128)} %bitcast.21, f32[61,64,61]{2,1,0:T(8,128)} %bitcast.22, f32[64,61]{1,0:T(8,128)} %decay_hbm.1, f32[64,61]{1,0:T(8,128)} %weight_hbm.1), custom_call_target="tpu_custom_call" | custom-call | tf_op jit(solution)/shard_map/pack/pallas_call | solution.py:97
  4.9 0.6 %collective-permute-start = (f32[64,64,128]{2,1,0:T(8,128)S(1)}, f32[64,64,128]{2,1,0:T(8,128)S(1)}, u32[]{:S(2)}, u32[]{:S(2)}) collective-permute-start(f32[64,64,128]{2,1,0:T(8,128)S(1)} %pack.1.own_ref), channel_id=1, source_target_pairs={{0,1},{1,0},{2,3},{3,2},{4,5},{5,4},{6,7},{7,6},{8,9},{9,8},{10,11... | collective-permute-start | bytes 6291464 | tf_op jit(solution)/shard_map/ppermute | solution.py:439
  5.4 0.0 copy-done.2
  5.4 0.0 copy-start.1
  5.4 0.0 copy-start.3
  5.4 2.6 %collective-permute-start.1 = (s32[8]{0:T(128)S(1)}, s32[8]{0:T(128)S(1)}, u32[]{:S(2)}, u32[]{:S(2)}) collective-permute-start(s32[8]{0:T(128)S(1)} %bitcast.17), channel_id=1, source_target_pairs={{0,2},{1,3},{2,0},{3,1},{4,6},{5,7},{6,4},{7,5},{8,10},{9,11},{10,... | collective-permute-start | bytes 104 | tf_op jit(solution)/shard_map/ppermute | solution.py:433
  8.0 1.5 %collective-permute-done.1.wanted_ref = s32[8]{0:T(128)S(1)} collective-permute-done((s32[8]{0:T(128)S(1)}, s32[8]{0:T(128)S(1)}, u32[]{:S(2)}, u32[]{:S(2)}) %collective-permute-start.1) | collective-permute-done | bytes 64 | tf_op jit(solution)/shard_map/ppermute | solution.py:433
  9.6 0.0 collective-permute-done.partner_ref
  9.6 0.6 %pick.1 = (f32[4,64,128]{2,1,0:T(8,128)S(1)}, f32[4,64,128]{2,1,0:T(8,128)S(1)}) custom-call(s32[8]{0:T(128)S(1)} %collective-permute-done.1.wanted_ref, f32[64,64,128]{2,1,0:T(8,128)S(1)} %pack.1.own_ref, f32[64,64,128]{2,1,0:T(8,128)S(1)} %collective-permute-done.partner_ref), custom_call_target="tpu_custom_call" | custom-call | tf_op jit(solution)/shard_map/pick/pallas_call | solution.py:139
  10.2 2.6 %collective-permute-start.3 = (f32[4,64,128]{2,1,0:T(8,128)S(1)}, f32[4,64,128]{2,1,0:T(8,128)S(1)}, u32[]{:S(2)}, u32[]{:S(2)}) collective-permute-start(f32[4,64,128]{2,1,0:T(8,128)S(1)} %get-tuple-element.23), channel_id=1, source_target_pairs={{0,2},{1,3},{2,0},{3,1},{4,6},{5,7},{6,4},{7,5},{8,10},{9,11},{10,... | collective-permute-start | bytes 393224 | tf_op jit(solution)/shard_map/ppermute | solution.py:433
  12.7 0.1 collective-permute-start.2
  12.8 0.0 copy-done.1
  12.8 0.0 copy-done.3
  12.8 0.0 copy-start
  12.8 4.7 %prepare.1 = (bf16[8,2,128,2048]{3,2,1,0:T(8,128)(2,1)S(1)}, f32[8,64,128]{2,1,0:T(8,128)S(1)}, f32[40,128]{1,0:T(8,128)S(1)}, s32[16,128]{1,0:T(8,128)S(1)}, f32[16,128]{1,0:T(8,128)S(1)}) custom-call(s32[8]{0:T(128)S(1)} %bitcast.18, s32[16]{0:T(128)S(1)} %copy-done.3, f32[1997]{0:T(1024)S(1)} %copy-done.1, f32[16,128]{1,0:T(8,128)S(1)} %pad_bitcast_fusion.padded_ref, ...), custom_call_target="tpu_custom_call" | custom-call | tf_op jit(solution)/shard_map/prepare/pallas_call | solution.py:237
  17.5 0.0 collective-permute-done.3.refs_0_
  17.5 0.0 copy-done
  17.5 1.6 %blocks.2 = (f32[16,4,128]{2,1,0:T(4,128)S(1)}, f32[4,128]{1,0:T(4,128)S(1)}) custom-call(f32[40,128]{1,0:T(8,128)S(1)} %get-tuple-element.17.aux_ref, s32[8,128]{1,0:T(8,128)S(1)} %bitcast.14, bf16[8,2,128,2048]{3,2,1,0:T(8,128)(2,1)S(1)} %get-tuple-element.20.operand_ref, f32[8,64,128]{2,1,0:T(8,128)S(1)} %get-tuple-element.21.own_ref, ...), custom_call_target="tpu_custom_call" | custom-call | tf_op jit(solution)/shard_map/blocks/pallas_call | solution.py:336
  19.1 0.2 collective-permute-done.2.refs_0_
  19.3 1.6 %blocks.3 = (f32[16,4,128]{2,1,0:T(4,128)S(1)}, f32[32,4,128]{2,1,0:T(4,128)S(1)}) custom-call(f32[40,128]{1,0:T(8,128)S(1)} %get-tuple-element.17.aux_ref, s32[8,128]{1,0:T(8,128)S(1)} %bitcast.15, bf16[8,2,128,2048]{3,2,1,0:T(8,128)(2,1)S(1)} %get-tuple-element.20.operand_ref, f32[8,64,128]{2,1,0:T(8,128)S(1)} %get-tuple-element.21.own_ref, ...), custom_call_target="tpu_custom_call" | custom-call | tf_op jit(solution)/shard_map/blocks/pallas_call | solution.py:336
  21.0 13.3 %all_to_all.5 = f32[32,4,128]{2,1,0:T(4,128)S(1)} all-to-all(f32[32,4,128]{2,1,0:T(4,128)S(1)} %get-tuple-element.25), channel_id=1, replica_groups=mesh['site'=8,'dom'=4] {'site','dom'}, dimensions={0} | all-to-all | bytes 131072 | tf_op jit(solution)/shard_map/all_to_all | solution.py:482
  34.3 1.0 %sums.1 = (f32[32,64]{1,0:T(8,128)}, f32[16,128]{1,0:T(8,128)}, f32[16,8,128]{2,1,0:T(8,128)}) custom-call(f32[40,128]{1,0:T(8,128)S(1)} %get-tuple-element.17.aux_ref, s32[16,128]{1,0:T(8,128)S(1)} %get-tuple-element.18.map_ref, f32[16,128]{1,0:T(8,128)S(1)} %get-tuple-element.19.lengths_ref, s32[8,128]{1,0:T(8,128)S(1)} %bitcast.16, ...), custom_call_target="tpu_custom_call" | custom-call | tf_op jit(solution)/shard_map/sums/pallas_call | solution.py:395
  (1 shorter events, 0.0 us)
Async XLA Ops:
  0.6 4.8 %copy-start.2 = (s32[1,8]{1,0:T(1,128)S(1)}, s32[1,8]{1,0:T(1,128)}, u32[]{:S(2)}) copy-start(s32[1,8]{1,0:T(1,128)} %param.20) | copy-start | bytes 100
  4.9 4.7 %collective-permute-start = (f32[64,64,128]{2,1,0:T(8,128)S(1)}, f32[64,64,128]{2,1,0:T(8,128)S(1)}, u32[]{:S(2)}, u32[]{:S(2)}) collective-permute-start(f32[64,64,128]{2,1,0:T(8,128)S(1)} %pack.1.own_ref), channel_id=1, source_target_pairs={{0,1},{1,0},{2,3},{3,2},{4,5},{5,4},{6,7},{7,6},{8,9},{9,8},{10,11... | collective-permute-start | bytes 6291464 | tf_op jit(solution)/shard_map/ppermute | solution.py:439
  5.4 7.4 %copy-start.1 = (f32[1997]{0:T(1024)S(1)}, f32[1997]{0:T(1024)}, u32[]{:S(2)}) copy-start(f32[1997]{0:T(1024)} %lengths_ref.1) | copy-start | bytes 23968
  5.4 7.4 %copy-start.3 = (s32[16]{0:T(128)S(1)}, s32[16]{0:T(128)}, u32[]{:S(2)}) copy-start(s32[16]{0:T(128)} %chosen_ref.1) | copy-start | bytes 196
  5.4 4.2 %collective-permute-start.1 = (s32[8]{0:T(128)S(1)}, s32[8]{0:T(128)S(1)}, u32[]{:S(2)}, u32[]{:S(2)}) collective-permute-start(s32[8]{0:T(128)S(1)} %bitcast.17), channel_id=1, source_target_pairs={{0,2},{1,3},{2,0},{3,1},{4,6},{5,7},{6,4},{7,5},{8,10},{9,11},{10,... | collective-permute-start | bytes 104 | tf_op jit(solution)/shard_map/ppermute | solution.py:433
  10.2 7.4 %collective-permute-start.3 = (f32[4,64,128]{2,1,0:T(8,128)S(1)}, f32[4,64,128]{2,1,0:T(8,128)S(1)}, u32[]{:S(2)}, u32[]{:S(2)}) collective-permute-start(f32[4,64,128]{2,1,0:T(8,128)S(1)} %get-tuple-element.23), channel_id=1, source_target_pairs={{0,2},{1,3},{2,0},{3,1},{4,6},{5,7},{6,4},{7,5},{8,10},{9,11},{10,... | collective-permute-start | bytes 393224 | tf_op jit(solution)/shard_map/ppermute | solution.py:433
  12.7 6.6 %collective-permute-start.2 = (f32[4,64,128]{2,1,0:T(8,128)S(1)}, f32[4,64,128]{2,1,0:T(8,128)S(1)}, u32[]{:S(2)}, u32[]{:S(2)}) collective-permute-start(f32[4,64,128]{2,1,0:T(8,128)S(1)} %get-tuple-element.22), channel_id=1, source_target_pairs={{0,2},{1,3},{2,0},{3,1},{4,6},{5,7},{6,4},{7,5},{8,10},{9,11},{10,... | collective-permute-start | bytes 393224 | tf_op jit(solution)/shard_map/ppermute | solution.py:433
  12.8 4.7 %copy-start = (s32[1,1024]{1,0:T(1,128)S(1)}, s32[1,1024]{1,0:T(1,128)}, u32[]{:S(2)}) copy-start(s32[1,1024]{1,0:T(1,128)} %param.19) | copy-start | bytes 12292

commit v4 on v3

v4 whole, which is shorter than its diff:
```python
import functools

import jax
import jax.numpy as jnp
from jax import lax
from jax.experimental import pallas as pl
from jax.experimental.pallas import tpu as pltpu
from jax.sharding import PartitionSpec as P


BLK = 128
HALF = 64
SUB = 8
EARLY = 6
LOG2_E = 1.4426950408889634
F32 = jnp.float32
BF16 = jnp.bfloat16
LIMITS = pltpu.CompilerParams(vmem_limit_bytes=24 * 1024 * 1024)


def in_hbm(x):
    return pltpu.with_memory_space_constraint(x, pltpu.HBM)


def pack_kernel(
    rate_hbm,
    left_hbm,
    right_hbm,
    decay_hbm,
    weight_hbm,
    out_ref,
    right_ref,
    rate_ref,
    left_ref,
    decay_ref,
    weight_ref,
    small_sems,
    sems,
    right_sem,
):
    chunks, states, group, _ = left_ref.shape
    half = out_ref.shape[0]
    small = [
        pltpu.make_async_copy(src, dst, small_sems.at[i])
        for i, (src, dst) in enumerate(
            ((rate_hbm, rate_ref), (decay_hbm, decay_ref), (weight_hbm, weight_ref))
        )
    ]
    for copy in small:
        copy.start()

    def chunk_copy(g):
        rows = pl.ds(g * group, group)
        return pltpu.make_async_copy(left_hbm.at[:, rows, :], left_ref.at[g], sems.at[g])

    for g in range(chunks // 2):
        chunk_copy(g).start()
        chunk_copy(g + chunks // 2).start()
    right_copy = pltpu.make_async_copy(right_hbm, right_ref, right_sem)
    right_copy.start()
    for copy in small:
        copy.wait()
    left = left_ref.reshape(chunks * states * group, states)
    gap = jnp.zeros((states, HALF - states), F32)

    def beside(first, second):
        space = gap[: first.shape[0]]
        return jnp.concatenate([first, space, second, space], axis=1)

    def exponents(q):
        return -(decay_ref[pl.ds(q, 1), :] * rate_ref[q])

    for g in range(chunks // 2):
        chunk_copy(g).wait()
        chunk_copy(g + chunks // 2).wait()
        for i in range(group):
            q = g * group + i
            tables = [
                left[pl.ds(c * states * group + i, states, stride=group), :]
                for c in (g, g + chunks // 2)
            ]
            out_ref[q, pl.ds(0, states), :] = beside(*tables)
            out_ref[q, pl.ds(states, 1), :] = beside(exponents(q), exponents(q + half))
            out_ref[q, pl.ds(states + 1, 1), :] = beside(
                weight_ref[pl.ds(q, 1), :], weight_ref[pl.ds(q + half, 1), :]
            )
            rest = HALF - states - 2
            out_ref[q, pl.ds(states + 2, rest), :] = jnp.zeros((rest, 2 * HALF), F32)
    right_copy.wait()


def pack_tables(left, right, decay, weight, rate):
    states, parts, _ = left.shape
    group = 8
    chunks = parts // group
    hbm = pl.BlockSpec(memory_space=pltpu.HBM)
    row = pltpu.VMEM((parts, states), F32)
    return pl.pallas_call(
        pack_kernel,
        in_specs=[hbm] * 5,
        out_specs=[pl.BlockSpec(memory_space=pltpu.VMEM)] * 2,
        out_shape=[
            jax.ShapeDtypeStruct((parts // 2, HALF, 2 * HALF), F32),
            jax.ShapeDtypeStruct(right.shape, F32),
        ],
        scratch_shapes=[
            pltpu.SMEM((parts,), F32),
            pltpu.VMEM((chunks, states, group, states), F32),
            row,
            row,
            pltpu.SemaphoreType.DMA((3,)),
            pltpu.SemaphoreType.DMA((chunks,)),
            pltpu.SemaphoreType.DMA,
        ],
        name="pack",
        compiler_params=LIMITS,
    )(in_hbm(rate), in_hbm(left), in_hbm(right), in_hbm(decay), in_hbm(weight))


def copy_tiles(wanted_ref, own_left, own_right, partner_left, partner_right, *out_refs):
    states, owned, _ = own_right.shape
    half = own_left.shape[0]
    base = lax.axis_index("dom") * owned
    rights = [ref.reshape(states * owned, states) for ref in (own_right, partner_right)]
    lane = lax.broadcasted_iota(jnp.int32, (HALF, 2 * HALF), 1)
    is_left = lane < HALF
    gap = jnp.zeros((states, 2 * HALF - states), F32)
    below = jnp.zeros((HALF - states, 2 * HALF), F32)
    place = 0
    for out_ref in out_refs:
        for n in range(out_ref.shape[0]):
            part = wanted_ref[place]
            row = lax.rem(part, owned)
            mine = part - row == base

            def chosen(flag):
                return jnp.full((1, 2 * HALF), flag.astype(jnp.int32)) == 1

            second = row >= half
            at = jnp.where(second, row - half, row)
            left = jnp.where(chosen(mine), own_left[at], partner_left[at])
            left = jnp.where(chosen(second), pltpu.roll(left, HALF, 1), left)
            table = [ref[pl.ds(row, states, stride=owned), :] for ref in rights]
            right = jnp.where(chosen(mine)[:, :states], *table)
            right = jnp.concatenate([jnp.concatenate([right, gap], axis=1), below], axis=0)
            out_ref[n] = jnp.where(is_left, left, pltpu.roll(right, HALF, 1))
            place += 1


def pick_tiles(wanted, tables, pieces):
    vmem = pl.BlockSpec(memory_space=pltpu.VMEM)
    count = wanted.shape[0] // pieces
    return pl.pallas_call(
        copy_tiles,
        in_specs=[pl.BlockSpec(memory_space=pltpu.SMEM)] + [vmem] * 4,
        out_specs=[vmem] * pieces,
        out_shape=[jax.ShapeDtypeStruct((count, HALF, 2 * HALF), F32)] * pieces,
        name="pick",
        compiler_params=LIMITS,
    )(wanted, *tables)


def start_split(skip, top_hbm, bottom_hbm, top_ref, bottom_ref, sems):
    chunks = sems.shape[1]
    chunk = top_ref.shape[0] // chunks

    def copies(g):
        there = pl.ds(g * chunk, chunk)
        here = pl.ds((skip + g) * chunk, chunk)
        return [
            pltpu.make_async_copy(src.at[here], dst.at[there], sems.at[i, g])
            for i, (src, dst) in enumerate(((top_hbm, top_ref), (bottom_hbm, bottom_ref)))
        ]

    for g in range(chunks):
        for copy in copies(g):
            copy.start()
    return copies


def finish_split(copies, out_ref, top_ref, bottom_ref, sems):
    nblocks = out_ref.shape[0]
    chunks = sems.shape[1]
    chunk = top_ref.shape[0] // chunks
    columns = out_ref.shape[3] // chunks
    fused = columns // BLK
    states = chunk // (fused * nblocks)
    pad = jnp.zeros((HALF - states, BLK), F32)

    def step(g, carry):
        for copy in copies(g):
            copy.wait()
        for b in range(fused):
            for n in range(nblocks):
                for side, ref in enumerate((top_ref, bottom_ref)):
                    first = g * chunk + b * states * nblocks + n
                    rows = ref[pl.ds(first, states, stride=nblocks), :]
                    full = jnp.concatenate([rows, pad], axis=0)
                    high = full.astype(BF16)
                    low = (full - high.astype(F32)).astype(BF16)
                    lanes = pl.ds(pl.multiple_of(g * columns + b * BLK, BLK), BLK)
                    out_ref[n, side, pl.ds(0, HALF), lanes] = high
                    out_ref[n, side, pl.ds(HALF, HALF), lanes] = low
        return carry

    lax.fori_loop(0, chunks, step, 0)


def early_kernel(top_hbm, bottom_hbm, out_ref, top_ref, bottom_ref, sems):
    copies = start_split(0, top_hbm, bottom_hbm, top_ref, bottom_ref, sems)
    finish_split(copies, out_ref, top_ref, bottom_ref, sems)


def late_kernel(
    skip,
    pair,
    rounds,
    blocks_ref,
    chosen_ref,
    lengths_ref,
    padded_ref,
    top_hbm,
    bottom_hbm,
    own_left,
    own_right,
    partner_left,
    partner_right,
    out_ref,
    tiles_ref,
    aux_ref,
    map_ref,
    rows_ref,
    top_ref,
    bottom_ref,
    sems,
):
    nblocks = out_ref.shape[0]
    branches = chosen_ref.shape[0]
    owned = own_right.shape[1]
    copies = start_split(skip, top_hbm, bottom_hbm, top_ref, bottom_ref, sems)
    copy_tiles(blocks_ref, own_left, own_right, partner_left, partner_right, tiles_ref)
    my_pair = lax.axis_index("dom") // pair
    lane = lax.broadcasted_iota(jnp.int32, (1, BLK), 1)
    flat = lax.broadcasted_iota(jnp.int32, map_ref.shape, 0) * BLK
    flat = flat + lax.broadcasted_iota(jnp.int32, map_ref.shape, 1)
    for n in range(nblocks):
        part = blocks_ref[n]
        distance = lax.rem(lax.div(part, owned * pair) - my_pair + rounds, rounds)
        aux_ref[pl.ds(n, 1), :] = jnp.full((1, BLK), distance.astype(F32), F32)
        aux_ref[pl.ds(nblocks + n, 1), :] = jnp.full((1, BLK), part.astype(F32), F32)
    along = jnp.zeros((1, BLK), F32)
    update = jnp.zeros(map_ref.shape, jnp.int32)
    for b in range(branches):
        place = chosen_ref[b]
        time = lengths_ref[place]
        aux_ref[pl.ds(2 * nblocks + 8 + b, 1), :] = jnp.full((1, BLK), time, F32)
        along = jnp.where(lane == b, time, along)
        update = jnp.where(flat == place, b + 1, update)
    aux_ref[pl.ds(2 * nblocks, 1), :] = along
    map_ref[...] = update
    rows_ref[...] = padded_ref[...]
    finish_split(copies, out_ref, top_ref, bottom_ref, sems)


def split_scratch(top, branches, taken, fused):
    rows = top.shape[0] // branches * taken
    return [
        pltpu.VMEM((rows, BLK), F32),
        pltpu.VMEM((rows, BLK), F32),
        pltpu.SemaphoreType.DMA((2, taken // fused)),
    ]


def prepare_early(top, bottom, nblocks, branches, taken):
    hbm = pl.BlockSpec(memory_space=pltpu.HBM)
    return pl.pallas_call(
        early_kernel,
        in_specs=[hbm, hbm],
        out_specs=pl.BlockSpec(memory_space=pltpu.VMEM),
        out_shape=jax.ShapeDtypeStruct((nblocks, 2, 2 * HALF, taken * BLK), BF16),
        scratch_shapes=split_scratch(top, branches, taken, 2),
        name="early",
        compiler_params=LIMITS,
    )(in_hbm(top), in_hbm(bottom))


def prepare_late(
    blocks, chosen, lengths, padded, top, bottom, tables, skipped, pair, rounds
):
    nblocks = blocks.shape[0]
    branches = chosen.shape[0]
    taken = branches - skipped
    smem = pl.BlockSpec(memory_space=pltpu.SMEM)
    hbm = pl.BlockSpec(memory_space=pltpu.HBM)
    vmem = pl.BlockSpec(memory_space=pltpu.VMEM)
    return pl.pallas_call(
        functools.partial(late_kernel, skipped // 2, pair, rounds),
        in_specs=[smem, smem, smem, vmem, hbm, hbm] + [vmem] * 4,
        out_specs=[vmem] * 5,
        out_shape=[
            jax.ShapeDtypeStruct((nblocks, 2, 2 * HALF, taken * BLK), BF16),
            jax.ShapeDtypeStruct((nblocks, HALF, 2 * HALF), F32),
            jax.ShapeDtypeStruct((2 * nblocks + 8 + branches, BLK), F32),
            jax.ShapeDtypeStruct(padded.shape, jnp.int32),
            jax.ShapeDtypeStruct(padded.shape, F32),
        ],
        scratch_shapes=split_scratch(top, branches, taken, 2),
        name="late",
        compiler_params=LIMITS,
    )(blocks, chosen, lengths, padded, in_hbm(top), in_hbm(bottom), *tables)


def block_kernel(rounds, states, pieces, piece, aux_ref, weight_ref, early_ref, late_ref, own_ref, *refs):
    tiles = refs[: rounds - 1]
    earlier = refs[rounds - 1 : rounds - 1 + (piece if piece == pieces - 1 else 0)]
    like_ref, terms_ref, partial_ref = refs[-3:]
    branches, count, _ = like_ref.shape
    nblocks = early_ref.shape[0]
    split = early_ref.shape[3]
    start = piece * count
    wide = 2 * BLK
    lane = lax.broadcasted_iota(jnp.int32, (HALF, 2 * HALF), 1)
    is_left = lane < HALF
    for m in range(count):
        n = start + m
        distance = aux_ref[pl.ds(n, 1), :]
        tile = own_ref[n]
        for r in range(1, rounds):
            tile = jnp.where(distance == float(r), tiles[r - 1][m], tile)
        turned = pltpu.roll(tile, HALF, 1)
        flipped = tile[:, :HALF].T
        scaled = flipped * tile[states + 1 : states + 2, :HALF]
        left = jnp.concatenate([scaled, scaled], axis=1)
        sides = []
        for double in (left, jnp.where(is_left, turned, tile)):
            high = double.astype(BF16)
            low = (double - high.astype(F32)).astype(BF16)
            sides.append(jnp.concatenate([high, low[:, :HALF]], axis=1))
        expo = jnp.broadcast_to(flipped[:, states : states + 1], (HALF, BLK))
        powers = expo * LOG2_E
        for c in range(branches * BLK // wide):
            prods = []
            for side, lhs in enumerate(sides):
                if c * wide < split:
                    part = early_ref[n, side, :, pl.ds(c * wide, wide)]
                else:
                    part = late_ref[n, side, :, pl.ds(c * wide - split, wide)]
                rhs = jnp.concatenate([part, part[:HALF]], axis=0)
                prods.append(jnp.dot(lhs, rhs, preferred_element_type=F32))
            joint = prods[0] * prods[1]
            for h in range(wide // BLK):
                b = c * (wide // BLK) + h
                time = aux_ref[pl.ds(2 * nblocks + 8 + b, 1), :]
                zeroth = joint[:, h * BLK : (h + 1) * BLK] * jnp.exp2(powers * time)
                first = zeroth * expo
                second = first * expo
                for i, term in enumerate((zeroth, first, second)):
                    total = term[:SUB]
                    for k in range(SUB, HALF, SUB):
                        total = total + term[k : k + SUB]
                    partial_ref[i, b, pl.ds(m * SUB, SUB), :] = total

    weight = weight_ref[pl.ds(start, count), :].astype(F32)
    lanes = lax.broadcasted_iota(jnp.int32, (count, BLK), 1)
    terms = jnp.where(lanes == 2 * branches, aux_ref[pl.ds(nblocks + start, count), :], 0.0)
    for b in range(branches):
        sums = []
        for i in range(3):
            total = partial_ref[i, b, pl.ds(0, count, stride=SUB), :]
            for j in range(1, SUB):
                total = total + partial_ref[i, b, pl.ds(j, count, stride=SUB), :]
            sums.append(total)
        like_ref[b] = sums[0]
        inverse = 1.0 / sums[0]
        first = sums[1] * inverse
        second = sums[2] * inverse - first * first
        one = jnp.sum(weight * first, axis=1, keepdims=True)
        two = jnp.sum(weight * second, axis=1, keepdims=True)
        terms = jnp.where(lanes == b, one, terms)
        terms = jnp.where(lanes == branches + b, two, terms)
    if piece < pieces - 1:
        terms_ref[...] = terms
    else:
        terms = [ref[...] for ref in earlier] + [terms]
        for d in range(terms_ref.shape[0]):
            for i in range(0, pieces, 2):
                pair = terms[i] + pltpu.roll(terms[i + 1], HALF, 1)
                terms_ref[d, pl.ds(i // 2 * count, count), :] = pair


def block_likelihoods(
    aux, weight, operands, own_tiles, tiles, earlier, branches, states, devices, pieces, piece
):
    nblocks = operands[0].shape[0]
    count = nblocks // pieces
    vmem = pl.BlockSpec(memory_space=pltpu.VMEM)
    last = piece == pieces - 1
    return pl.pallas_call(
        functools.partial(block_kernel, len(tiles) + 1, states, pieces, piece),
        in_specs=[vmem] * (5 + len(tiles) + len(earlier)),
        out_specs=[vmem] * 2,
        out_shape=[
            jax.ShapeDtypeStruct((branches, count, BLK), F32),
            jax.ShapeDtypeStruct((devices, nblocks // 2, BLK) if last else (count, BLK), F32),
        ],
        scratch_shapes=[pltpu.VMEM((3, branches, count * SUB, BLK), F32)],
        name="blocks",
        compiler_params=LIMITS,
    )(aux, weight, *operands, own_tiles, *tiles, *earlier)


def sum_kernel(aux_ref, map_ref, lengths_ref, weight_ref, share_ref, *refs):
    like_refs = refs[:-3]
    part_ref, new_ref, loglik_ref = refs[-3:]
    branches, count, _ = like_refs[0].shape
    nblocks = count * len(like_refs)
    owned = part_ref.shape[1]
    terms = part_ref.shape[0]
    share = share_ref[...]
    share = jnp.concatenate([share, pltpu.roll(share, HALF, 1)], axis=0)
    share = share[:, :HALF]
    parts = lax.broadcasted_iota(jnp.int32, (share.shape[0], owned), 1)
    parts = parts + lax.axis_index("dom") * owned
    ident = share[:, terms : terms + 1].astype(jnp.int32)
    onehot = (ident == parts).astype(F32)
    sums = lax.dot_general(
        share,
        onehot,
        (((0,), (0,)), ((), ())),
        precision=lax.Precision.HIGHEST,
        preferred_element_type=F32,
    )
    part_ref[...] = sums[:terms]
    total = jnp.sum(share, axis=0, keepdims=True)
    total = jnp.concatenate([total, total], axis=1)
    second = pltpu.roll(total, BLK - branches, 1)
    updated = aux_ref[pl.ds(2 * nblocks, 1), :] - total / second
    lane = lax.broadcasted_iota(jnp.int32, (1, BLK), 1)
    place = map_ref[...]
    new = lengths_ref[...]
    for b in range(branches):
        value = jnp.sum(jnp.where(lane == b, updated, 0.0), axis=1, keepdims=True)
        new = jnp.where(place == b + 1, value, new)
    new_ref[...] = new
    for i, like_ref in enumerate(like_refs):
        blocks = pl.ds(i * count, count)
        weight = weight_ref[blocks, :].astype(F32)
        for b in range(branches):
            loglik_ref[b, blocks, :] = weight * jnp.log(like_ref[b])


def add_up(aux, places, lengths, weight, share, likes, owned):
    vmem = pl.BlockSpec(memory_space=pltpu.VMEM)
    branches = likes[0].shape[0]
    nblocks = weight.shape[0]
    return pl.pallas_call(
        sum_kernel,
        in_specs=[vmem] * (5 + len(likes)),
        out_specs=[vmem] * 3,
        out_shape=[
            jax.ShapeDtypeStruct((2 * branches, owned), F32),
            jax.ShapeDtypeStruct(lengths.shape, F32),
            jax.ShapeDtypeStruct((branches, nblocks, BLK), F32),
        ],
        name="sums",
        compiler_params=LIMITS,
    )(aux, places, lengths, weight, share, *likes)


def compute(
    top_partial,
    bottom_partial,
    left_vectors,
    right_vectors,
    decay_rates,
    state_weights,
    part_rates,
    branch_lengths,
    pattern_weights,
    block_partition,
    chosen_branches,
):
    branches, states, _, sites_here = top_partial.shape
    nblocks = sites_here // BLK
    owned = left_vectors.shape[0]
    groups = lax.axis_size("dom")
    pair = 2 if groups % 2 == 0 else 1
    rounds = groups // pair

    def shifted(value, r):
        step = [
            (d, ((d // pair + r) % rounds) * pair + d % pair) for d in range(groups)
        ]
        return lax.ppermute(value, "dom", step)

    blocks = block_partition[0]
    requests = [shifted(blocks, rounds - r) for r in range(1, rounds)]
    left_turned = jnp.transpose(left_vectors, (1, 0, 2))
    right_turned = jnp.transpose(right_vectors, (1, 0, 2))

    def swapped(value):
        if pair == 1:
            return value
        return lax.ppermute(value, "dom", [(d, d ^ 1) for d in range(groups)])

    partner_right = swapped(right_turned)
    own = pack_tables(left_turned, right_turned, decay_rates, state_weights, part_rates)
    partner_left = swapped(own[0])
    tables = [*own, partner_left, partner_right]
    pieces = 2
    answers = []
    for r, request in zip(range(1, rounds), requests):
        answers.append([shifted(t, r) for t in pick_tiles(request, tables, pieces)])
    count = branch_lengths.shape[0]
    rows = -(-count // BLK)
    padded = jnp.pad(branch_lengths, (0, rows * BLK - count)).reshape(rows, BLK)
    top = top_partial.reshape(branches * states * nblocks, BLK)
    bottom = bottom_partial.reshape(branches * states * nblocks, BLK)
    early = prepare_early(top, bottom, nblocks, branches, EARLY)
    late, tiles, aux, places, lengths = prepare_late(
        blocks,
        chosen_branches,
        branch_lengths,
        padded,
        top,
        bottom,
        tables,
        EARLY,
        pair,
        rounds,
    )
    operands = [early, late]
    answers = answers[::-1]
    devices = lax.axis_size("site") * groups
    weight = pattern_weights.reshape(nblocks, BLK)
    likes, earlier = [], []
    for piece in range(pieces):
        like, terms = block_likelihoods(
            aux,
            weight,
            operands,
            tiles,
            [answer[piece] for answer in answers],
            earlier,
            branches,
            states,
            devices,
            pieces,
            piece,
        )
        likes.append(like)
        earlier.append(terms)
    everything = lax.all_to_all(
        terms, ("site", "dom"), split_axis=0, concat_axis=0, tiled=True
    )
    parts, new_lengths, loglik = add_up(
        aux, places, lengths, weight, everything.reshape(-1, BLK), likes, owned
    )
    new_lengths = new_lengths.reshape(rows * BLK)[:count]
    return (
        loglik.reshape(branches, 1, sites_here),
        parts.reshape(2, branches, owned),
        new_lengths,
    )


def solution(mesh):
    return jax.shard_map(
        compute,
        mesh=mesh,
        in_specs=(
            P(None, None, "dom", "site"),
            P(None, None, "dom", "site"),
            P("dom", None, None),
            P("dom", None, None),
            P("dom", None),
            P("dom", None),
            P("dom"),
            P(),
            P("dom", "site"),
            P("dom", "site"),
            P(),
        ),
        out_specs=(P(None, "dom", "site"), P(None, None, "dom"), P()),
        check_vma=False,
    )
```

time: 35.5 us -> 37.3 us (1.051)
  starting transfers between devices: 5.8 us -> 6.56 us
  Pallas kernels: 13.7 us -> 14.1 us
    pallas_call x1, Pallas kernels: 0.58 us -> 1.17 us  [pick_tiles(): pl.pallas_call(copy_tiles, in_specs=[pl.BlockSpec(memory_space=pltpu.SMEM...]
    ppermute x1 -> x2, waiting for transfers between devices: 0.01 us -> 0.58 us  [swapped(): return lax.ppermute(value, 'dom', [(d, d ^ 1) for d in range(groups)])]
    ppermute x3, starting transfers between devices: 5.25 us -> 5.75 us  [shifted(): return lax.ppermute(value, 'dom', step)]
    ppermute x1 -> x2, starting transfers between devices: 0.56 us -> 0.82 us  [swapped(): return lax.ppermute(value, 'dom', [(d, d ^ 1) for d in range(groups)])]
    pallas_call x2 -> x3, Pallas kernels: 8.89 us -> 8.81 us  [the longest x1 4.08 us: prepare_late(): pl.pallas_call(functools.partial(late_kernel, skipped // 2, pair, rounds)...]
  transfers between devices with their start and end apart: 4 -> 5, of which waited for: 2 -> 2; matrix products, arithmetic and copies ran while one was open for 0% -> 0% of each run, Pallas kernels for 18% -> 21%
where the time goes in v4:
time: 37.3 us; the launch traced here: 37.1 us
  Pallas kernels  14.1 us (38%)
  blocking collectives  13.5 us (36%)
  starting transfers between devices  6.56 us (18%)
  waiting for transfers between devices  2.13 us (6%)
  between operations  0.73 us (2%)
    all_to_all x1, blocking collectives, compute(): lax.all_to_all(terms, ('site', 'dom'), split_axis=0, concat_axis=0, tiled...  13.5 us
    ppermute x3, starting transfers between devices, shifted(): return lax.ppermute(value, 'dom', step)  5.75 us
    pallas_call x1, Pallas kernels, prepare_late(): pl.pallas_call(functools.partial(late_kernel, skipped // 2, pair, rounds)...  4.08 us
    pallas_call x2, Pallas kernels, block_likelihoods(): pl.pallas_call(functools.partial(block_kernel, len(tiles) + 1, states, pi...  3.11 us
    pallas_call x1, Pallas kernels, pack_tables(): pl.pallas_call(pack_kernel, in_specs=[hbm] * 5, out_specs=[pl.BlockSpec(m...  2.59 us
    pallas_call x1, Pallas kernels, prepare_early(): pl.pallas_call(early_kernel, in_specs=[hbm, hbm], out_specs=pl.BlockSpec(...  2.14 us
    ppermute x3, waiting for transfers between devices, shifted(): return lax.ppermute(value, 'dom', step)  1.55 us
    pallas_call x1, Pallas kernels, pick_tiles(): pl.pallas_call(copy_tiles, in_specs=[pl.BlockSpec(memory_space=pltpu.SMEM...  1.17 us
  transfers between devices with their start and end apart: 5, of which 2 were waited for; matrix products, arithmetic and copies ran while one was open for 0% of the time, Pallas kernels for 21%

profile of v4, /device:TPU:0, one launch (start us, length us, event | category | flops | bytes accessed | tf_op | source)
XLA Modules:
  0.0 37.1 jit_solution(9716264909876129494)
XLA Ops:
  0.6 0.0 copy-start.4
  0.6 0.0 copy-start.2
  0.7 2.6 %pack.1 = (f32[32,64,128]{2,1,0:T(8,128)S(1)}, f32[61,64,61]{2,1,0:T(8,128)S(1)}) custom-call(f32[64]{0:T(128)} %rate_hbm.1, f32[61,64,61]{2,1,0:T(8,128)} %bitcast.23, f32[61,64,61]{2,1,0:T(8,128)} %bitcast.24, f32[64,61]{1,0:T(8,128)} %decay_hbm.1, f32[64,61]{1,0:T(8,128)} %weight_hbm.1), custom_call_target="tpu_custom_call" | custom-call | tf_op jit(solution)/shard_map/pack/pallas_call | solution.py:98
  3.2 0.6 %collective-permute-start = (f32[32,64,128]{2,1,0:T(8,128)S(1)}, f32[32,64,128]{2,1,0:T(8,128)S(1)}, u32[]{:S(2)}, u32[]{:S(2)}) collective-permute-start(f32[32,64,128]{2,1,0:T(8,128)S(1)} %get-tuple-element.19.own_left), channel_id=1, source_target_pairs={{0,1},{1,0},{2,3},{3,2},{4,5},{5,4},{6,7},{7,6},{8,9},{9,8},{10,11... | collective-permute-start | bytes 3145736 | tf_op jit(solution)/shard_map/ppermute | solution.py:504
  3.8 0.0 copy-done.4
  3.8 0.3 collective-permute-start.1
  4.1 0.0 copy-done.2
  4.1 2.8 %collective-permute-start.2 = (s32[8]{0:T(128)S(1)}, s32[8]{0:T(128)S(1)}, u32[]{:S(2)}, u32[]{:S(2)}) collective-permute-start(s32[8]{0:T(128)S(1)} %bitcast.17), channel_id=1, source_target_pairs={{0,2},{1,3},{2,0},{3,1},{4,6},{5,7},{6,4},{7,5},{8,10},{9,11},{10,... | collective-permute-start | bytes 104 | tf_op jit(solution)/shard_map/ppermute | solution.py:494
  6.8 1.5 %collective-permute-done.2.wanted_ref = s32[8]{0:T(128)S(1)} collective-permute-done((s32[8]{0:T(128)S(1)}, s32[8]{0:T(128)S(1)}, u32[]{:S(2)}, u32[]{:S(2)}) %collective-permute-start.2) | collective-permute-done | bytes 64 | tf_op jit(solution)/shard_map/ppermute | solution.py:494
  8.4 0.6 %collective-permute-done.1.partner_right = f32[61,64,61]{2,1,0:T(8,128)S(1)} collective-permute-done((f32[61,64,61]{2,1,0:T(8,128)S(1)}, f32[61,64,61]{2,1,0:T(8,128)S(1)}, u32[]{:S(2)}, u32[]{:S(2)}) %collective-permute-start.1) | collective-permute-done | bytes 952608 | tf_op jit(solution)/shard_map/ppermute | solution.py:504
  9.0 0.0 collective-permute-done.partner_left
  9.0 1.2 %pick.1 = (f32[4,64,128]{2,1,0:T(8,128)S(1)}, f32[4,64,128]{2,1,0:T(8,128)S(1)}) custom-call(s32[8]{0:T(128)S(1)} %collective-permute-done.2.wanted_ref, f32[32,64,128]{2,1,0:T(8,128)S(1)} %get-tuple-element.19.own_left, f32[61,64,61]{2,1,0:T(8,128)S(1)} %get-tuple-element.20.own_right, f32[32,64,128]{2,1,0:T(8,128)S(1)} %collective-permute-done.partner_left, ...), custom_call_target="tpu_custom_call" | custom-call | tf_op jit(solution)/shard_map/pick/pallas_call | solution.py:153
  10.1 2.9 %collective-permute-start.4 = (f32[4,64,128]{2,1,0:T(8,128)S(1)}, f32[4,64,128]{2,1,0:T(8,128)S(1)}, u32[]{:S(2)}, u32[]{:S(2)}) collective-permute-start(f32[4,64,128]{2,1,0:T(8,128)S(1)} %get-tuple-element.27), channel_id=1, source_target_pairs={{0,2},{1,3},{2,0},{3,1},{4,6},{5,7},{6,4},{7,5},{8,10},{9,11},{10,... | collective-permute-start | bytes 393224 | tf_op jit(solution)/shard_map/ppermute | solution.py:494
  13.0 0.1 collective-permute-start.3
  13.1 0.0 copy-start.1
  13.1 0.0 copy-start.3
  13.1 2.1 %early.1.early_ref = bf16[8,2,128,768]{3,2,1,0:T(8,128)(2,1)S(1)} custom-call(f32[7808,128]{1,0:T(8,128)} %bitcast.19, f32[7808,128]{1,0:T(8,128)} %bitcast.21), custom_call_target="tpu_custom_call" | custom-call | tf_op jit(solution)/shard_map/early/pallas_call | solution.py:276
  15.3 0.0 copy-done.1
  15.3 0.0 copy-done.3
  15.3 0.0 copy-start
  15.3 4.1 %late.1 = (bf16[8,2,128,1280]{3,2,1,0:T(8,128)(2,1)S(1)}, f32[8,64,128]{2,1,0:T(8,128)S(1)}, f32[40,128]{1,0:T(8,128)S(1)}, s32[16,128]{1,0:T(8,128)S(1)}, f32[16,128]{1,0:T(8,128)S(1)}) custom-call(s32[8]{0:T(128)S(1)} %bitcast.18, s32[16]{0:T(128)S(1)} %copy-done.3, f32[1997]{0:T(1024)S(1)} %copy-done.1, f32[16,128]{1,0:T(8,128)S(1)} %pad_bitcast_fusion.padded_ref, ...), custom_call_target="tpu_custom_call" | custom-call | tf_op jit(solution)/shard_map/late/pallas_call | solution.py:296
  19.4 0.0 collective-permute-done.4.refs_0_
  19.4 0.0 copy-done
  19.4 1.5 %blocks.2 = (f32[16,4,128]{2,1,0:T(4,128)S(1)}, f32[4,128]{1,0:T(4,128)S(1)}) custom-call(f32[40,128]{1,0:T(8,128)S(1)} %get-tuple-element.21.aux_ref, s32[8,128]{1,0:T(8,128)S(1)} %bitcast.14, bf16[8,2,128,768]{3,2,1,0:T(8,128)(2,1)S(1)} %early.1.early_ref, bf16[8,2,128,1280]{3,2,1,0:T(8,128)(2,1)S(1)} %get-tuple-element.24.late_ref, ...), custom_call_target="tpu_custom_call" | custom-call | tf_op jit(solution)/shard_map/blocks/pallas_call | solution.py:398
  20.9 0.0 collective-permute-done.3.refs_0_
  20.9 1.6 %blocks.3 = (f32[16,4,128]{2,1,0:T(4,128)S(1)}, f32[32,4,128]{2,1,0:T(4,128)S(1)}) custom-call(f32[40,128]{1,0:T(8,128)S(1)} %get-tuple-element.21.aux_ref, s32[8,128]{1,0:T(8,128)S(1)} %bitcast.15, bf16[8,2,128,768]{3,2,1,0:T(8,128)(2,1)S(1)} %early.1.early_ref, bf16[8,2,128,1280]{3,2,1,0:T(8,128)(2,1)S(1)} %get-tuple-element.24.late_ref, ...), custom_call_target="tpu_custom_call" | custom-call | tf_op jit(solution)/shard_map/blocks/pallas_call | solution.py:398
  22.5 13.5 %all_to_all.5 = f32[32,4,128]{2,1,0:T(4,128)S(1)} all-to-all(f32[32,4,128]{2,1,0:T(4,128)S(1)} %get-tuple-element.29), channel_id=1, replica_groups=mesh['site'=8,'dom'=4] {'site','dom'}, dimensions={0} | all-to-all | bytes 131072 | tf_op jit(solution)/shard_map/all_to_all | solution.py:553
  36.0 1.0 %sums.1 = (f32[32,64]{1,0:T(8,128)}, f32[16,128]{1,0:T(8,128)}, f32[16,8,128]{2,1,0:T(8,128)}) custom-call(f32[40,128]{1,0:T(8,128)S(1)} %get-tuple-element.21.aux_ref, s32[16,128]{1,0:T(8,128)S(1)} %get-tuple-element.22.map_ref, f32[16,128]{1,0:T(8,128)S(1)} %get-tuple-element.23.lengths_ref, s32[8,128]{1,0:T(8,128)S(1)} %bitcast.16, ...), custom_call_target="tpu_custom_call" | custom-call | tf_op jit(solution)/shard_map/sums/pallas_call | solution.py:456
  (1 shorter events, 0.0 us)
Async XLA Ops:
  0.6 3.2 %copy-start.4 = (f32[64,61,61]{2,0,1:T(8,128)S(1)}, f32[64,61,61]{2,0,1:T(8,128)}, u32[]{:S(2)}) copy-start(f32[64,61,61]{2,0,1:T(8,128)} %param.14) | copy-start | bytes 2857732
  0.6 3.4 %copy-start.2 = (s32[1,8]{1,0:T(1,128)S(1)}, s32[1,8]{1,0:T(1,128)}, u32[]{:S(2)}) copy-start(s32[1,8]{1,0:T(1,128)} %param.20) | copy-start | bytes 100
  3.2 5.7 %collective-permute-start = (f32[32,64,128]{2,1,0:T(8,128)S(1)}, f32[32,64,128]{2,1,0:T(8,128)S(1)}, u32[]{:S(2)}, u32[]{:S(2)}) collective-permute-start(f32[32,64,128]{2,1,0:T(8,128)S(1)} %get-tuple-element.19.own_left), channel_id=1, source_target_pairs={{0,1},{1,0},{2,3},{3,2},{4,5},{5,4},{6,7},{7,6},{8,9},{9,8},{10,11... | collective-permute-start | bytes 3145736 | tf_op jit(solution)/shard_map/ppermute | solution.py:504
  3.8 5.1 %collective-permute-start.1 = (f32[61,64,61]{2,1,0:T(8,128)S(1)}, f32[61,64,61]{2,1,0:T(8,128)S(1)}, u32[]{:S(2)}, u32[]{:S(2)}) collective-permute-start(f32[61,64,61]{2,1,0:T(8,128)S(1)} %bitcast.25), channel_id=1, source_target_pairs={{0,1},{1,0},{2,3},{3,2},{4,5},{5,4},{6,7},{7,6},{8,9},{9,8},{10,11... | collective-permute-start | bytes 2857736 | tf_op jit(solution)/shard_map/ppermute | solution.py:504
  4.1 4.3 %collective-permute-start.2 = (s32[8]{0:T(128)S(1)}, s32[8]{0:T(128)S(1)}, u32[]{:S(2)}, u32[]{:S(2)}) collective-permute-start(s32[8]{0:T(128)S(1)} %bitcast.17), channel_id=1, source_target_pairs={{0,2},{1,3},{2,0},{3,1},{4,6},{5,7},{6,4},{7,5},{8,10},{9,11},{10,... | collective-permute-start | bytes 104 | tf_op jit(solution)/shard_map/ppermute | solution.py:494
  10.1 9.3 %collective-permute-start.4 = (f32[4,64,128]{2,1,0:T(8,128)S(1)}, f32[4,64,128]{2,1,0:T(8,128)S(1)}, u32[]{:S(2)}, u32[]{:S(2)}) collective-permute-start(f32[4,64,128]{2,1,0:T(8,128)S(1)} %get-tuple-element.27), channel_id=1, source_target_pairs={{0,2},{1,3},{2,0},{3,1},{4,6},{5,7},{6,4},{7,5},{8,10},{9,11},{10,... | collective-permute-start | bytes 393224 | tf_op jit(solution)/shard_map/ppermute | solution.py:494
  13.0 7.9 %collective-permute-start.3 = (f32[4,64,128]{2,1,0:T(8,128)S(1)}, f32[4,64,128]{2,1,0:T(8,128)S(1)}, u32[]{:S(2)}, u32[]{:S(2)}) collective-permute-start(f32[4,64,128]{2,1,0:T(8,128)S(1)} %get-tuple-element.26), channel_id=1, source_target_pairs={{0,2},{1,3},{2,0},{3,1},{4,6},{5,7},{6,4},{7,5},{8,10},{9,11},{10,... | collective-permute-start | bytes 393224 | tf_op jit(solution)/shard_map/ppermute | solution.py:494
  13.1 2.2 %copy-start.1 = (f32[1997]{0:T(1024)S(1)}, f32[1997]{0:T(1024)}, u32[]{:S(2)}) copy-start(f32[1997]{0:T(1024)} %lengths_ref.1) | copy-start | bytes 23968
  13.1 2.2 %copy-start.3 = (s32[16]{0:T(128)S(1)}, s32[16]{0:T(128)}, u32[]{:S(2)}) copy-start(s32[16]{0:T(128)} %chosen_ref.1) | copy-start | bytes 196
  15.3 4.1 %copy-start = (s32[1,1024]{1,0:T(1,128)S(1)}, s32[1,1024]{1,0:T(1,128)}, u32[]{:S(2)}) copy-start(s32[1,1024]{1,0:T(1,128)} %param.19) | copy-start | bytes 12292

commit v5 on v4

--- a/solution.py
+++ b/solution.py
@@ -117,7 +117,8 @@
     )(in_hbm(rate), in_hbm(left), in_hbm(right), in_hbm(decay), in_hbm(weight))
 
 
-def copy_tiles(wanted_ref, own_left, own_right, partner_left, partner_right, *out_refs):
+def copy_tiles(wanted_ref, own_left, own_right, partner_left, partner_right, *refs):
+    out_refs, right_ref = refs[:-1], refs[-1]
     states, owned, _ = own_right.shape
     half = own_left.shape[0]
     base = lax.axis_index("dom") * owned
@@ -126,6 +127,19 @@
     is_left = lane < HALF
     gap = jnp.zeros((states, 2 * HALF - states), F32)
     below = jnp.zeros((HALF - states, 2 * HALF), F32)
+    for n in range(right_ref.shape[0]):
+        part = wanted_ref[n]
+        row = lax.rem(part, owned)
+        mine = part - row == base
+
+        @pl.when(mine)
+        def _():
+            right_ref[n] = rights[0][pl.ds(row, states, stride=owned), :]
+
+        @pl.when(jnp.logical_not(mine))
+        def _():
+            right_ref[n] = rights[1][pl.ds(row, states, stride=owned), :]
+
     place = 0
     for out_ref in out_refs:
         for n in range(out_ref.shape[0]):
@@ -140,8 +154,7 @@
             at = jnp.where(second, row - half, row)
             left = jnp.where(chosen(mine), own_left[at], partner_left[at])
             left = jnp.where(chosen(second), pltpu.roll(left, HALF, 1), left)
-            table = [ref[pl.ds(row, states, stride=owned), :] for ref in rights]
-            right = jnp.where(chosen(mine)[:, :states], *table)
+            right = right_ref[place]
             right = jnp.concatenate([jnp.concatenate([right, gap], axis=1), below], axis=0)
             out_ref[n] = jnp.where(is_left, left, pltpu.roll(right, HALF, 1))
             place += 1
@@ -155,6 +168,7 @@
         in_specs=[pl.BlockSpec(memory_space=pltpu.SMEM)] + [vmem] * 4,
         out_specs=[vmem] * pieces,
         out_shape=[jax.ShapeDtypeStruct((count, HALF, 2 * HALF), F32)] * pieces,
+        scratch_shapes=[pltpu.VMEM(wanted.shape + tables[1].shape[::2], F32)],
         name="pick",
         compiler_params=LIMITS,
     )(wanted, *tables)
@@ -215,9 +229,9 @@
     skip,
     pair,
     rounds,
-    blocks_ref,
-    chosen_ref,
-    lengths_ref,
+    blocks_hbm,
+    chosen_hbm,
+    lengths_hbm,
     padded_ref,
     top_hbm,
     bottom_hbm,
@@ -233,12 +247,31 @@
     top_ref,
     bottom_ref,
     sems,
+    right_ref,
+    blocks_ref,
+    chosen_ref,
+    lengths_ref,
+    small_sems,
 ):
     nblocks = out_ref.shape[0]
     branches = chosen_ref.shape[0]
     owned = own_right.shape[1]
+    small = [
+        pltpu.make_async_copy(src, dst, small_sems.at[i])
+        for i, (src, dst) in enumerate(
+            (
+                (blocks_hbm, blocks_ref),
+                (chosen_hbm, chosen_ref),
+                (lengths_hbm, lengths_ref),
+            )
+        )
+    ]
+    for copy in small:
+        copy.start()
     copies = start_split(skip, top_hbm, bottom_hbm, top_ref, bottom_ref, sems)
-    copy_tiles(blocks_ref, own_left, own_right, partner_left, partner_right, tiles_ref)
+    for copy in small:
+        copy.wait()
+    copy_tiles(blocks_ref, own_left, own_right, partner_left, partner_right, tiles_ref, right_ref)
     my_pair = lax.axis_index("dom") // pair
     lane = lax.broadcasted_iota(jnp.int32, (1, BLK), 1)
     flat = lax.broadcasted_iota(jnp.int32, map_ref.shape, 0) * BLK
@@ -290,12 +323,11 @@
     nblocks = blocks.shape[0]
     branches = chosen.shape[0]
     taken = branches - skipped
-    smem = pl.BlockSpec(memory_space=pltpu.SMEM)
     hbm = pl.BlockSpec(memory_space=pltpu.HBM)
     vmem = pl.BlockSpec(memory_space=pltpu.VMEM)
     return pl.pallas_call(
         functools.partial(late_kernel, skipped // 2, pair, rounds),
-        in_specs=[smem, smem, smem, vmem, hbm, hbm] + [vmem] * 4,
+        in_specs=[hbm, hbm, hbm, vmem, hbm, hbm] + [vmem] * 4,
         out_specs=[vmem] * 5,
         out_shape=[
             jax.ShapeDtypeStruct((nblocks, 2, 2 * HALF, taken * BLK), BF16),
@@ -304,10 +336,25 @@
             jax.ShapeDtypeStruct(padded.shape, jnp.int32),
             jax.ShapeDtypeStruct(padded.shape, F32),
         ],
-        scratch_shapes=split_scratch(top, branches, taken, 2),
+        scratch_shapes=split_scratch(top, branches, taken, 2)
+        + [
+            pltpu.VMEM((nblocks,) + tables[1].shape[::2], F32),
+            pltpu.SMEM(blocks.shape, jnp.int32),
+            pltpu.SMEM(chosen.shape, jnp.int32),
+            pltpu.SMEM(lengths.shape, F32),
+            pltpu.SemaphoreType.DMA((3,)),
+        ],
         name="late",
         compiler_params=LIMITS,
-    )(blocks, chosen, lengths, padded, in_hbm(top), in_hbm(bottom), *tables)
+    )(
+        in_hbm(blocks),
+        in_hbm(chosen),
+        in_hbm(lengths),
+        padded,
+        in_hbm(top),
+        in_hbm(bottom),
+        *tables,
+    )
 
 
 def block_kernel(rounds, states, pieces, piece, aux_ref, weight_ref, early_ref, late_ref, own_ref, *refs):

time: 37.3 us -> 36.2 us (0.971)
  Pallas kernels: 14.1 us -> 13 us
    pallas_call x1, Pallas kernels: 4.08 us -> 3.05 us  [prepare_late(): pl.pallas_call(functools.partial(late_kernel, skipped // 2, pair, rounds)...]
  transfers between devices with their start and end apart: 5 -> 5, of which waited for: 2 -> 2; matrix products, arithmetic and copies ran while one was open for 0% -> 0% of each run, Pallas kernels for 21% -> 19%
where the time goes in v5:
time: 36.2 us; the launch traced here: 36 us
  blocking collectives  13.5 us (37%)
  Pallas kernels  13 us (36%)
  starting transfers between devices  6.59 us (18%)
  waiting for transfers between devices  2.13 us (6%)
  between operations  0.73 us (2%)
    all_to_all x1, blocking collectives, compute(): lax.all_to_all(terms, ('site', 'dom'), split_axis=0, concat_axis=0, tiled...  13.5 us
    ppermute x3, starting transfers between devices, shifted(): return lax.ppermute(value, 'dom', step)  5.78 us
    pallas_call x2, Pallas kernels, block_likelihoods(): pl.pallas_call(functools.partial(block_kernel, len(tiles) + 1, states, pi...  3.11 us
    pallas_call x1, Pallas kernels, prepare_late(): pl.pallas_call(functools.partial(late_kernel, skipped // 2, pair, rounds)...  3.05 us
    pallas_call x1, Pallas kernels, pack_tables(): pl.pallas_call(pack_kernel, in_specs=[hbm] * 5, out_specs=[pl.BlockSpec(m...  2.59 us
    pallas_call x1, Pallas kernels, prepare_early(): pl.pallas_call(early_kernel, in_specs=[hbm, hbm], out_specs=pl.BlockSpec(...  2.12 us
    ppermute x3, waiting for transfers between devices, shifted(): return lax.ppermute(value, 'dom', step)  1.55 us
    pallas_call x1, Pallas kernels, pick_tiles(): pl.pallas_call(copy_tiles, in_specs=[pl.BlockSpec(memory_space=pltpu.SMEM...  1.12 us
  transfers between devices with their start and end apart: 5, of which 2 were waited for; matrix products, arithmetic and copies ran while one was open for 0% of the time, Pallas kernels for 19%

profile of v5, /device:TPU:0, one launch (start us, length us, event | category | flops | bytes accessed | tf_op | source)
XLA Modules:
  0.0 36.0 jit_solution(6786445782285096260)
XLA Ops:
  0.6 0.0 copy-start.1
  0.6 0.0 copy-start.3
  0.7 2.6 %pack.1 = (f32[32,64,128]{2,1,0:T(8,128)S(1)}, f32[61,64,61]{2,1,0:T(8,128)S(1)}) custom-call(f32[64]{0:T(128)} %rate_hbm.1, f32[61,64,61]{2,1,0:T(8,128)} %bitcast.21, f32[61,64,61]{2,1,0:T(8,128)} %bitcast.22, f32[64,61]{1,0:T(8,128)} %decay_hbm.1, f32[64,61]{1,0:T(8,128)} %weight_hbm.1), custom_call_target="tpu_custom_call" | custom-call | tf_op jit(solution)/shard_map/pack/pallas_call | solution.py:98
  3.3 0.6 %collective-permute-start = (f32[32,64,128]{2,1,0:T(8,128)S(1)}, f32[32,64,128]{2,1,0:T(8,128)S(1)}, u32[]{:S(2)}, u32[]{:S(2)}) collective-permute-start(f32[32,64,128]{2,1,0:T(8,128)S(1)} %get-tuple-element.19.own_left), channel_id=1, source_target_pairs={{0,1},{1,0},{2,3},{3,2},{4,5},{5,4},{6,7},{7,6},{8,9},{9,8},{10,11... | collective-permute-start | bytes 3145736 | tf_op jit(solution)/shard_map/ppermute | solution.py:551
  3.8 0.0 copy-done.1
  3.8 0.3 collective-permute-start.1
  4.1 0.0 copy-done.3
  4.1 2.8 %collective-permute-start.2 = (s32[8]{0:T(128)S(1)}, s32[8]{0:T(128)S(1)}, u32[]{:S(2)}, u32[]{:S(2)}) collective-permute-start(s32[8]{0:T(128)S(1)} %bitcast.25), channel_id=1, source_target_pairs={{0,2},{1,3},{2,0},{3,1},{4,6},{5,7},{6,4},{7,5},{8,10},{9,11},{10,... | collective-permute-start | bytes 104 | tf_op jit(solution)/shard_map/ppermute | solution.py:541
  6.8 1.5 %collective-permute-done.2.wanted_ref = s32[8]{0:T(128)S(1)} collective-permute-done((s32[8]{0:T(128)S(1)}, s32[8]{0:T(128)S(1)}, u32[]{:S(2)}, u32[]{:S(2)}) %collective-permute-start.2) | collective-permute-done | bytes 64 | tf_op jit(solution)/shard_map/ppermute | solution.py:541
  8.4 0.6 %collective-permute-done.1.partner_right = f32[61,64,61]{2,1,0:T(8,128)S(1)} collective-permute-done((f32[61,64,61]{2,1,0:T(8,128)S(1)}, f32[61,64,61]{2,1,0:T(8,128)S(1)}, u32[]{:S(2)}, u32[]{:S(2)}) %collective-permute-start.1) | collective-permute-done | bytes 952608 | tf_op jit(solution)/shard_map/ppermute | solution.py:551
  9.0 0.0 collective-permute-done.partner_left
  9.0 1.1 %pick.1 = (f32[4,64,128]{2,1,0:T(8,128)S(1)}, f32[4,64,128]{2,1,0:T(8,128)S(1)}) custom-call(s32[8]{0:T(128)S(1)} %collective-permute-done.2.wanted_ref, f32[32,64,128]{2,1,0:T(8,128)S(1)} %get-tuple-element.19.own_left, f32[61,64,61]{2,1,0:T(8,128)S(1)} %get-tuple-element.20.own_right, f32[32,64,128]{2,1,0:T(8,128)S(1)} %collective-permute-done.partner_left, ...), custom_call_target="tpu_custom_call" | custom-call | tf_op jit(solution)/shard_map/pick/pallas_call | solution.py:166
  10.1 2.9 %collective-permute-start.4 = (f32[4,64,128]{2,1,0:T(8,128)S(1)}, f32[4,64,128]{2,1,0:T(8,128)S(1)}, u32[]{:S(2)}, u32[]{:S(2)}) collective-permute-start(f32[4,64,128]{2,1,0:T(8,128)S(1)} %get-tuple-element.27), channel_id=1, source_target_pairs={{0,2},{1,3},{2,0},{3,1},{4,6},{5,7},{6,4},{7,5},{8,10},{9,11},{10,... | collective-permute-start | bytes 393224 | tf_op jit(solution)/shard_map/ppermute | solution.py:541
  13.0 0.1 collective-permute-start.3
  13.1 0.0 copy-start.2
  13.1 2.1 %early.1.early_ref = bf16[8,2,128,768]{3,2,1,0:T(8,128)(2,1)S(1)} custom-call(f32[7808,128]{1,0:T(8,128)} %bitcast.17, f32[7808,128]{1,0:T(8,128)} %bitcast.19), custom_call_target="tpu_custom_call" | custom-call | tf_op jit(solution)/shard_map/early/pallas_call | solution.py:309
  15.2 0.0 copy-done.2
  15.3 0.0 copy-start
  15.3 3.0 %late.1 = (bf16[8,2,128,1280]{3,2,1,0:T(8,128)(2,1)S(1)}, f32[8,64,128]{2,1,0:T(8,128)S(1)}, f32[40,128]{1,0:T(8,128)S(1)}, s32[16,128]{1,0:T(8,128)S(1)}, f32[16,128]{1,0:T(8,128)S(1)}) custom-call(s32[8]{0:T(128)} %bitcast.24, s32[16]{0:T(128)} %chosen_hbm.1, f32[1997]{0:T(1024)} %lengths_hbm.1, f32[16,128]{1,0:T(8,128)S(1)} %pad_bitcast_fusion.padded_ref, ...), custom_call_target="tpu_custom_call" | custom-call | tf_op jit(solution)/shard_map/late/pallas_call | solution.py:328
  18.3 0.0 collective-permute-done.4.refs_0_
  18.3 0.0 copy-done
  18.4 1.5 %blocks.2 = (f32[16,4,128]{2,1,0:T(4,128)S(1)}, f32[4,128]{1,0:T(4,128)S(1)}) custom-call(f32[40,128]{1,0:T(8,128)S(1)} %get-tuple-element.21.aux_ref, s32[8,128]{1,0:T(8,128)S(1)} %bitcast.14, bf16[8,2,128,768]{3,2,1,0:T(8,128)(2,1)S(1)} %early.1.early_ref, bf16[8,2,128,1280]{3,2,1,0:T(8,128)(2,1)S(1)} %get-tuple-element.24.late_ref, ...), custom_call_target="tpu_custom_call" | custom-call | tf_op jit(solution)/shard_map/blocks/pallas_call | solution.py:445
  19.9 0.0 collective-permute-done.3.refs_0_
  19.9 1.6 %blocks.3 = (f32[16,4,128]{2,1,0:T(4,128)S(1)}, f32[32,4,128]{2,1,0:T(4,128)S(1)}) custom-call(f32[40,128]{1,0:T(8,128)S(1)} %get-tuple-element.21.aux_ref, s32[8,128]{1,0:T(8,128)S(1)} %bitcast.15, bf16[8,2,128,768]{3,2,1,0:T(8,128)(2,1)S(1)} %early.1.early_ref, bf16[8,2,128,1280]{3,2,1,0:T(8,128)(2,1)S(1)} %get-tuple-element.24.late_ref, ...), custom_call_target="tpu_custom_call" | custom-call | tf_op jit(solution)/shard_map/blocks/pallas_call | solution.py:445
  21.5 13.5 %all_to_all.5 = f32[32,4,128]{2,1,0:T(4,128)S(1)} all-to-all(f32[32,4,128]{2,1,0:T(4,128)S(1)} %get-tuple-element.29), channel_id=1, replica_groups=mesh['site'=8,'dom'=4] {'site','dom'}, dimensions={0} | all-to-all | bytes 131072 | tf_op jit(solution)/shard_map/all_to_all | solution.py:600
  35.0 1.0 %sums.1 = (f32[32,64]{1,0:T(8,128)}, f32[16,128]{1,0:T(8,128)}, f32[16,8,128]{2,1,0:T(8,128)}) custom-call(f32[40,128]{1,0:T(8,128)S(1)} %get-tuple-element.21.aux_ref, s32[16,128]{1,0:T(8,128)S(1)} %get-tuple-element.22.map_ref, f32[16,128]{1,0:T(8,128)S(1)} %get-tuple-element.23.lengths_ref, s32[8,128]{1,0:T(8,128)S(1)} %bitcast.16, ...), custom_call_target="tpu_custom_call" | custom-call | tf_op jit(solution)/shard_map/sums/pallas_call | solution.py:503
  (1 shorter events, 0.0 us)
Async XLA Ops:
  0.6 3.2 %copy-start.1 = (f32[64,61,61]{2,0,1:T(8,128)S(1)}, f32[64,61,61]{2,0,1:T(8,128)}, u32[]{:S(2)}) copy-start(f32[64,61,61]{2,0,1:T(8,128)} %param.14) | copy-start | bytes 2857732
  0.6 3.4 %copy-start.3 = (s32[1,8]{1,0:T(1,128)S(1)}, s32[1,8]{1,0:T(1,128)}, u32[]{:S(2)}) copy-start(s32[1,8]{1,0:T(1,128)} %param.20) | copy-start | bytes 100
  3.3 5.7 %collective-permute-start = (f32[32,64,128]{2,1,0:T(8,128)S(1)}, f32[32,64,128]{2,1,0:T(8,128)S(1)}, u32[]{:S(2)}, u32[]{:S(2)}) collective-permute-start(f32[32,64,128]{2,1,0:T(8,128)S(1)} %get-tuple-element.19.own_left), channel_id=1, source_target_pairs={{0,1},{1,0},{2,3},{3,2},{4,5},{5,4},{6,7},{7,6},{8,9},{9,8},{10,11... | collective-permute-start | bytes 3145736 | tf_op jit(solution)/shard_map/ppermute | solution.py:551
  3.8 5.1 %collective-permute-start.1 = (f32[61,64,61]{2,1,0:T(8,128)S(1)}, f32[61,64,61]{2,1,0:T(8,128)S(1)}, u32[]{:S(2)}, u32[]{:S(2)}) collective-permute-start(f32[61,64,61]{2,1,0:T(8,128)S(1)} %bitcast.23), channel_id=1, source_target_pairs={{0,1},{1,0},{2,3},{3,2},{4,5},{5,4},{6,7},{7,6},{8,9},{9,8},{10,11... | collective-permute-start | bytes 2857736 | tf_op jit(solution)/shard_map/ppermute | solution.py:551
  4.1 4.3 %collective-permute-start.2 = (s32[8]{0:T(128)S(1)}, s32[8]{0:T(128)S(1)}, u32[]{:S(2)}, u32[]{:S(2)}) collective-permute-start(s32[8]{0:T(128)S(1)} %bitcast.25), channel_id=1, source_target_pairs={{0,2},{1,3},{2,0},{3,1},{4,6},{5,7},{6,4},{7,5},{8,10},{9,11},{10,... | collective-permute-start | bytes 104 | tf_op jit(solution)/shard_map/ppermute | solution.py:541
  10.1 8.2 %collective-permute-start.4 = (f32[4,64,128]{2,1,0:T(8,128)S(1)}, f32[4,64,128]{2,1,0:T(8,128)S(1)}, u32[]{:S(2)}, u32[]{:S(2)}) collective-permute-start(f32[4,64,128]{2,1,0:T(8,128)S(1)} %get-tuple-element.27), channel_id=1, source_target_pairs={{0,2},{1,3},{2,0},{3,1},{4,6},{5,7},{6,4},{7,5},{8,10},{9,11},{10,... | collective-permute-start | bytes 393224 | tf_op jit(solution)/shard_map/ppermute | solution.py:541
  13.0 6.8 %collective-permute-start.3 = (f32[4,64,128]{2,1,0:T(8,128)S(1)}, f32[4,64,128]{2,1,0:T(8,128)S(1)}, u32[]{:S(2)}, u32[]{:S(2)}) collective-permute-start(f32[4,64,128]{2,1,0:T(8,128)S(1)} %get-tuple-element.26), channel_id=1, source_target_pairs={{0,2},{1,3},{2,0},{3,1},{4,6},{5,7},{6,4},{7,5},{8,10},{9,11},{10,... | collective-permute-start | bytes 393224 | tf_op jit(solution)/shard_map/ppermute | solution.py:541
  13.1 2.1 %copy-start.2 = (f32[1997]{0:T(1024)S(1)}, f32[1997]{0:T(1024)}, u32[]{:S(2)}) copy-start(f32[1997]{0:T(1024)} %lengths_hbm.1) | copy-start | bytes 23968
  15.3 3.1 %copy-start = (s32[1,1024]{1,0:T(1,128)S(1)}, s32[1,1024]{1,0:T(1,128)}, u32[]{:S(2)}) copy-start(s32[1,1024]{1,0:T(1,128)} %param.19) | copy-start | bytes 12292

commit v6 on v5

--- a/solution.py
+++ b/solution.py
@@ -126,7 +126,7 @@
     lane = lax.broadcasted_iota(jnp.int32, (HALF, 2 * HALF), 1)
     is_left = lane < HALF
     gap = jnp.zeros((states, 2 * HALF - states), F32)
-    below = jnp.zeros((HALF - states, 2 * HALF), F32)
+    below = jnp.zeros((HALF - states - 1, 2 * HALF), F32)
     for n in range(right_ref.shape[0]):
         part = wanted_ref[n]
         row = lax.rem(part, owned)
@@ -142,7 +142,8 @@
 
     place = 0
     for out_ref in out_refs:
-        for n in range(out_ref.shape[0]):
+        tall = HALF if len(out_ref.shape) == 3 else states + 1
+        for n in range(out_ref.size // (tall * 2 * HALF)):
             part = wanted_ref[place]
             row = lax.rem(part, owned)
             mine = part - row == base
@@ -155,19 +156,27 @@
             left = jnp.where(chosen(mine), own_left[at], partner_left[at])
             left = jnp.where(chosen(second), pltpu.roll(left, HALF, 1), left)
             right = right_ref[place]
-            right = jnp.concatenate([jnp.concatenate([right, gap], axis=1), below], axis=0)
-            out_ref[n] = jnp.where(is_left, left, pltpu.roll(right, HALF, 1))
+            right = jnp.concatenate(
+                [jnp.concatenate([right, gap], axis=1), left[states + 1 : states + 2], below],
+                axis=0,
+            )
+            tile = jnp.where(is_left, left, pltpu.roll(right, HALF, 1))
+            if len(out_ref.shape) == 3:
+                out_ref[n] = tile
+            else:
+                out_ref[pl.ds(n * (states + 1), states + 1), :] = tile[: states + 1]
             place += 1
 
 
 def pick_tiles(wanted, tables, pieces):
     vmem = pl.BlockSpec(memory_space=pltpu.VMEM)
     count = wanted.shape[0] // pieces
+    rows = tables[1].shape[0] + 1
     return pl.pallas_call(
         copy_tiles,
         in_specs=[pl.BlockSpec(memory_space=pltpu.SMEM)] + [vmem] * 4,
         out_specs=[vmem] * pieces,
-        out_shape=[jax.ShapeDtypeStruct((count, HALF, 2 * HALF), F32)] * pieces,
+        out_shape=[jax.ShapeDtypeStruct((count * rows, 2 * HALF), F32)] * pieces,
         scratch_shapes=[pltpu.VMEM(wanted.shape + tables[1].shape[::2], F32)],
         name="pick",
         compiler_params=LIMITS,
@@ -373,10 +382,12 @@
         distance = aux_ref[pl.ds(n, 1), :]
         tile = own_ref[n]
         for r in range(1, rounds):
-            tile = jnp.where(distance == float(r), tiles[r - 1][m], tile)
+            sent = tiles[r - 1][pl.ds(m * (states + 1), states + 1), :]
+            sent = jnp.concatenate([sent, jnp.zeros((HALF - states - 1, 2 * HALF), F32)], axis=0)
+            tile = jnp.where(distance == float(r), sent, tile)
         turned = pltpu.roll(tile, HALF, 1)
         flipped = tile[:, :HALF].T
-        scaled = flipped * tile[states + 1 : states + 2, :HALF]
+        scaled = flipped * turned[states : states + 1, :HALF]
         left = jnp.concatenate([scaled, scaled], axis=1)
         sides = []
         for double in (left, jnp.where(is_left, turned, tile)):

time: 36.2 us -> 36.2 us (level)
  no operation moved by 1% of the time
where the time goes in v6:
time: 36.2 us; the launch traced here: 36 us
  blocking collectives  13.5 us (37%)
  Pallas kernels  13.1 us (36%)
  starting transfers between devices  6.59 us (18%)
  waiting for transfers between devices  2.13 us (6%)
  between operations  0.73 us (2%)
    all_to_all x1, blocking collectives, compute(): lax.all_to_all(terms, ('site', 'dom'), split_axis=0, concat_axis=0, tiled...  13.5 us
    ppermute x3, starting transfers between devices, shifted(): return lax.ppermute(value, 'dom', step)  5.78 us
    pallas_call x1, Pallas kernels, prepare_late(): pl.pallas_call(functools.partial(late_kernel, skipped // 2, pair, rounds)...  3.09 us
    pallas_call x2, Pallas kernels, block_likelihoods(): pl.pallas_call(functools.partial(block_kernel, len(tiles) + 1, states, pi...  3.05 us
    pallas_call x1, Pallas kernels, pack_tables(): pl.pallas_call(pack_kernel, in_specs=[hbm] * 5, out_specs=[pl.BlockSpec(m...  2.59 us
    pallas_call x1, Pallas kernels, prepare_early(): pl.pallas_call(early_kernel, in_specs=[hbm, hbm], out_specs=pl.BlockSpec(...  2.12 us
    ppermute x3, waiting for transfers between devices, shifted(): return lax.ppermute(value, 'dom', step)  1.55 us
    pallas_call x1, Pallas kernels, pick_tiles(): pl.pallas_call(copy_tiles, in_specs=[pl.BlockSpec(memory_space=pltpu.SMEM...  1.17 us
  transfers between devices with their start and end apart: 5, of which 2 were waited for; matrix products, arithmetic and copies ran while one was open for 0% of the time, Pallas kernels for 19%

profile of v6, /device:TPU:0, one launch (start us, length us, event | category | flops | bytes accessed | tf_op | source)
XLA Modules:
  0.0 36.0 jit_solution(12986091711962382587)
XLA Ops:
  0.6 0.0 copy-start.1
  0.6 0.0 copy-start.3
  0.7 2.6 %pack.1 = (f32[32,64,128]{2,1,0:T(8,128)S(1)}, f32[61,64,61]{2,1,0:T(8,128)S(1)}) custom-call(f32[64]{0:T(128)} %rate_hbm.1, f32[61,64,61]{2,1,0:T(8,128)} %bitcast.21, f32[61,64,61]{2,1,0:T(8,128)} %bitcast.22, f32[64,61]{1,0:T(8,128)} %decay_hbm.1, f32[64,61]{1,0:T(8,128)} %weight_hbm.1), custom_call_target="tpu_custom_call" | custom-call | tf_op jit(solution)/shard_map/pack/pallas_call | solution.py:98
  3.3 0.6 %collective-permute-start = (f32[32,64,128]{2,1,0:T(8,128)S(1)}, f32[32,64,128]{2,1,0:T(8,128)S(1)}, u32[]{:S(2)}, u32[]{:S(2)}) collective-permute-start(f32[32,64,128]{2,1,0:T(8,128)S(1)} %get-tuple-element.19.own_left), channel_id=1, source_target_pairs={{0,1},{1,0},{2,3},{3,2},{4,5},{5,4},{6,7},{7,6},{8,9},{9,8},{10,11... | collective-permute-start | bytes 3145736 | tf_op jit(solution)/shard_map/ppermute | solution.py:562
  3.8 0.0 copy-done.1
  3.8 0.3 collective-permute-start.1
  4.1 0.0 copy-done.3
  4.1 2.8 %collective-permute-start.2 = (s32[8]{0:T(128)S(1)}, s32[8]{0:T(128)S(1)}, u32[]{:S(2)}, u32[]{:S(2)}) collective-permute-start(s32[8]{0:T(128)S(1)} %bitcast.25), channel_id=1, source_target_pairs={{0,2},{1,3},{2,0},{3,1},{4,6},{5,7},{6,4},{7,5},{8,10},{9,11},{10,... | collective-permute-start | bytes 104 | tf_op jit(solution)/shard_map/ppermute | solution.py:552
  6.8 1.5 %collective-permute-done.2.wanted_ref = s32[8]{0:T(128)S(1)} collective-permute-done((s32[8]{0:T(128)S(1)}, s32[8]{0:T(128)S(1)}, u32[]{:S(2)}, u32[]{:S(2)}) %collective-permute-start.2) | collective-permute-done | bytes 64 | tf_op jit(solution)/shard_map/ppermute | solution.py:552
  8.4 0.6 %collective-permute-done.1.partner_right = f32[61,64,61]{2,1,0:T(8,128)S(1)} collective-permute-done((f32[61,64,61]{2,1,0:T(8,128)S(1)}, f32[61,64,61]{2,1,0:T(8,128)S(1)}, u32[]{:S(2)}, u32[]{:S(2)}) %collective-permute-start.1) | collective-permute-done | bytes 952608 | tf_op jit(solution)/shard_map/ppermute | solution.py:562
  9.0 0.0 collective-permute-done.partner_left
  9.0 1.2 %pick.1 = (f32[248,128]{1,0:T(8,128)S(1)}, f32[248,128]{1,0:T(8,128)S(1)}) custom-call(s32[8]{0:T(128)S(1)} %collective-permute-done.2.wanted_ref, f32[32,64,128]{2,1,0:T(8,128)S(1)} %get-tuple-element.19.own_left, f32[61,64,61]{2,1,0:T(8,128)S(1)} %get-tuple-element.20.own_right, f32[32,64,128]{2,1,0:T(8,128)S(1)} %collective-permute-done.partner_left, ...), custom_call_target="tpu_custom_call" | custom-call | tf_op jit(solution)/shard_map/pick/pallas_call | solution.py:175
  10.1 2.9 %collective-permute-start.4 = (f32[248,128]{1,0:T(8,128)S(1)}, f32[248,128]{1,0:T(8,128)S(1)}, u32[]{:S(2)}, u32[]{:S(2)}) collective-permute-start(f32[248,128]{1,0:T(8,128)S(1)} %get-tuple-element.27), channel_id=1, source_target_pairs={{0,2},{1,3},{2,0},{3,1},{4,6},{5,7},{6,4},{7,5},{8,10},{9,11},{10,... | collective-permute-start | bytes 380936 | tf_op jit(solution)/shard_map/ppermute | solution.py:552
  13.1 0.1 collective-permute-start.3
  13.2 0.0 copy-start.2
  13.2 2.1 %early.1.early_ref = bf16[8,2,128,768]{3,2,1,0:T(8,128)(2,1)S(1)} custom-call(f32[7808,128]{1,0:T(8,128)} %bitcast.17, f32[7808,128]{1,0:T(8,128)} %bitcast.19), custom_call_target="tpu_custom_call" | custom-call | tf_op jit(solution)/shard_map/early/pallas_call | solution.py:318
  15.3 0.0 copy-done.2
  15.3 0.0 copy-start
  15.3 3.1 %late.1 = (bf16[8,2,128,1280]{3,2,1,0:T(8,128)(2,1)S(1)}, f32[8,64,128]{2,1,0:T(8,128)S(1)}, f32[40,128]{1,0:T(8,128)S(1)}, s32[16,128]{1,0:T(8,128)S(1)}, f32[16,128]{1,0:T(8,128)S(1)}) custom-call(s32[8]{0:T(128)} %bitcast.24, s32[16]{0:T(128)} %chosen_hbm.1, f32[1997]{0:T(1024)} %lengths_hbm.1, f32[16,128]{1,0:T(8,128)S(1)} %pad_bitcast_fusion.padded_ref, ...), custom_call_target="tpu_custom_call" | custom-call | tf_op jit(solution)/shard_map/late/pallas_call | solution.py:337
  18.4 0.0 collective-permute-done.4.refs_0_
  18.4 0.0 copy-done
  18.4 1.5 %blocks.2 = (f32[16,4,128]{2,1,0:T(4,128)S(1)}, f32[4,128]{1,0:T(4,128)S(1)}) custom-call(f32[40,128]{1,0:T(8,128)S(1)} %get-tuple-element.21.aux_ref, s32[8,128]{1,0:T(8,128)S(1)} %bitcast.14, bf16[8,2,128,768]{3,2,1,0:T(8,128)(2,1)S(1)} %early.1.early_ref, bf16[8,2,128,1280]{3,2,1,0:T(8,128)(2,1)S(1)} %get-tuple-element.24.late_ref, ...), custom_call_target="tpu_custom_call" | custom-call | tf_op jit(solution)/shard_map/blocks/pallas_call | solution.py:456
  19.9 0.0 collective-permute-done.3.refs_0_
  19.9 1.6 %blocks.3 = (f32[16,4,128]{2,1,0:T(4,128)S(1)}, f32[32,4,128]{2,1,0:T(4,128)S(1)}) custom-call(f32[40,128]{1,0:T(8,128)S(1)} %get-tuple-element.21.aux_ref, s32[8,128]{1,0:T(8,128)S(1)} %bitcast.15, bf16[8,2,128,768]{3,2,1,0:T(8,128)(2,1)S(1)} %early.1.early_ref, bf16[8,2,128,1280]{3,2,1,0:T(8,128)(2,1)S(1)} %get-tuple-element.24.late_ref, ...), custom_call_target="tpu_custom_call" | custom-call | tf_op jit(solution)/shard_map/blocks/pallas_call | solution.py:456
  21.5 13.5 %all_to_all.5 = f32[32,4,128]{2,1,0:T(4,128)S(1)} all-to-all(f32[32,4,128]{2,1,0:T(4,128)S(1)} %get-tuple-element.29), channel_id=1, replica_groups=mesh['site'=8,'dom'=4] {'site','dom'}, dimensions={0} | all-to-all | bytes 131072 | tf_op jit(solution)/shard_map/all_to_all | solution.py:611
  35.0 1.0 %sums.1 = (f32[32,64]{1,0:T(8,128)}, f32[16,128]{1,0:T(8,128)}, f32[16,8,128]{2,1,0:T(8,128)}) custom-call(f32[40,128]{1,0:T(8,128)S(1)} %get-tuple-element.21.aux_ref, s32[16,128]{1,0:T(8,128)S(1)} %get-tuple-element.22.map_ref, f32[16,128]{1,0:T(8,128)S(1)} %get-tuple-element.23.lengths_ref, s32[8,128]{1,0:T(8,128)S(1)} %bitcast.16, ...), custom_call_target="tpu_custom_call" | custom-call | tf_op jit(solution)/shard_map/sums/pallas_call | solution.py:514
  (1 shorter events, 0.0 us)
Async XLA Ops:
  0.6 3.2 %copy-start.1 = (f32[64,61,61]{2,0,1:T(8,128)S(1)}, f32[64,61,61]{2,0,1:T(8,128)}, u32[]{:S(2)}) copy-start(f32[64,61,61]{2,0,1:T(8,128)} %param.14) | copy-start | bytes 2857732
  0.6 3.4 %copy-start.3 = (s32[1,8]{1,0:T(1,128)S(1)}, s32[1,8]{1,0:T(1,128)}, u32[]{:S(2)}) copy-start(s32[1,8]{1,0:T(1,128)} %param.20) | copy-start | bytes 100
  3.3 5.7 %collective-permute-start = (f32[32,64,128]{2,1,0:T(8,128)S(1)}, f32[32,64,128]{2,1,0:T(8,128)S(1)}, u32[]{:S(2)}, u32[]{:S(2)}) collective-permute-start(f32[32,64,128]{2,1,0:T(8,128)S(1)} %get-tuple-element.19.own_left), channel_id=1, source_target_pairs={{0,1},{1,0},{2,3},{3,2},{4,5},{5,4},{6,7},{7,6},{8,9},{9,8},{10,11... | collective-permute-start | bytes 3145736 | tf_op jit(solution)/shard_map/ppermute | solution.py:562
  3.8 5.1 %collective-permute-start.1 = (f32[61,64,61]{2,1,0:T(8,128)S(1)}, f32[61,64,61]{2,1,0:T(8,128)S(1)}, u32[]{:S(2)}, u32[]{:S(2)}) collective-permute-start(f32[61,64,61]{2,1,0:T(8,128)S(1)} %bitcast.23), channel_id=1, source_target_pairs={{0,1},{1,0},{2,3},{3,2},{4,5},{5,4},{6,7},{7,6},{8,9},{9,8},{10,11... | collective-permute-start | bytes 2857736 | tf_op jit(solution)/shard_map/ppermute | solution.py:562
  4.1 4.3 %collective-permute-start.2 = (s32[8]{0:T(128)S(1)}, s32[8]{0:T(128)S(1)}, u32[]{:S(2)}, u32[]{:S(2)}) collective-permute-start(s32[8]{0:T(128)S(1)} %bitcast.25), channel_id=1, source_target_pairs={{0,2},{1,3},{2,0},{3,1},{4,6},{5,7},{6,4},{7,5},{8,10},{9,11},{10,... | collective-permute-start | bytes 104 | tf_op jit(solution)/shard_map/ppermute | solution.py:552
  10.1 8.3 %collective-permute-start.4 = (f32[248,128]{1,0:T(8,128)S(1)}, f32[248,128]{1,0:T(8,128)S(1)}, u32[]{:S(2)}, u32[]{:S(2)}) collective-permute-start(f32[248,128]{1,0:T(8,128)S(1)} %get-tuple-element.27), channel_id=1, source_target_pairs={{0,2},{1,3},{2,0},{3,1},{4,6},{5,7},{6,4},{7,5},{8,10},{9,11},{10,... | collective-permute-start | bytes 380936 | tf_op jit(solution)/shard_map/ppermute | solution.py:552
  13.1 6.9 %collective-permute-start.3 = (f32[248,128]{1,0:T(8,128)S(1)}, f32[248,128]{1,0:T(8,128)S(1)}, u32[]{:S(2)}, u32[]{:S(2)}) collective-permute-start(f32[248,128]{1,0:T(8,128)S(1)} %get-tuple-element.26), channel_id=1, source_target_pairs={{0,2},{1,3},{2,0},{3,1},{4,6},{5,7},{6,4},{7,5},{8,10},{9,11},{10,... | collective-permute-start | bytes 380936 | tf_op jit(solution)/shard_map/ppermute | solution.py:552
  13.2 2.1 %copy-start.2 = (f32[1997]{0:T(1024)S(1)}, f32[1997]{0:T(1024)}, u32[]{:S(2)}) copy-start(f32[1997]{0:T(1024)} %lengths_hbm.1) | copy-start | bytes 23968
  15.3 3.1 %copy-start = (s32[1,1024]{1,0:T(1,128)S(1)}, s32[1,1024]{1,0:T(1,128)}, u32[]{:S(2)}) copy-start(s32[1,1024]{1,0:T(1,128)} %param.19) | copy-start | bytes 12292

commit v7 on v6

--- a/solution.py
+++ b/solution.py
@@ -11,7 +11,7 @@
 BLK = 128
 HALF = 64
 SUB = 8
-EARLY = 6
+EARLY = 2
 LOG2_E = 1.4426950408889634
 F32 = jnp.float32
 BF16 = jnp.bfloat16
@@ -118,28 +118,37 @@
 
 
 def copy_tiles(wanted_ref, own_left, own_right, partner_left, partner_right, *refs):
-    out_refs, right_ref = refs[:-1], refs[-1]
+    copy_rights(wanted_ref, own_right, partner_right, refs[-1])
+    join_tiles(wanted_ref, own_left, partner_left, refs[-1], *refs[:-1])
+
+
+def copy_rights(wanted_ref, own_right, partner_right, right_ref):
     states, owned, _ = own_right.shape
-    half = own_left.shape[0]
     base = lax.axis_index("dom") * owned
     rights = [ref.reshape(states * owned, states) for ref in (own_right, partner_right)]
+    for n in range(right_ref.shape[0]):
+        part = wanted_ref[n]
+        row = lax.rem(part, owned)
+        mine = part - row == base
+
+        @pl.when(mine)
+        def _():
+            right_ref[n] = rights[0][pl.ds(row, states, stride=owned), :]
+
+        @pl.when(jnp.logical_not(mine))
+        def _():
+            right_ref[n] = rights[1][pl.ds(row, states, stride=owned), :]
+
+
+def join_tiles(wanted_ref, own_left, partner_left, right_ref, *out_refs):
+    states = right_ref.shape[1]
+    half = own_left.shape[0]
+    owned = 2 * half
+    base = lax.axis_index("dom") * owned
     lane = lax.broadcasted_iota(jnp.int32, (HALF, 2 * HALF), 1)
     is_left = lane < HALF
     gap = jnp.zeros((states, 2 * HALF - states), F32)
     below = jnp.zeros((HALF - states - 1, 2 * HALF), F32)
-    for n in range(right_ref.shape[0]):
-        part = wanted_ref[n]
-        row = lax.rem(part, owned)
-        mine = part - row == base
-
-        @pl.when(mine)
-        def _():
-            right_ref[n] = rights[0][pl.ds(row, states, stride=owned), :]
-
-        @pl.when(jnp.logical_not(mine))
-        def _():
-            right_ref[n] = rights[1][pl.ds(row, states, stride=owned), :]
-
     place = 0
     for out_ref in out_refs:
         tall = HALF if len(out_ref.shape) == 3 else states + 1
@@ -172,15 +181,23 @@
     vmem = pl.BlockSpec(memory_space=pltpu.VMEM)
     count = wanted.shape[0] // pieces
     rows = tables[1].shape[0] + 1
+    smem = pl.BlockSpec(memory_space=pltpu.SMEM)
+    right = pl.pallas_call(
+        copy_rights,
+        in_specs=[smem, vmem, vmem],
+        out_specs=vmem,
+        out_shape=jax.ShapeDtypeStruct(wanted.shape + tables[1].shape[::2], F32),
+        name="rights",
+        compiler_params=LIMITS,
+    )(wanted, tables[1], tables[3])
     return pl.pallas_call(
-        copy_tiles,
-        in_specs=[pl.BlockSpec(memory_space=pltpu.SMEM)] + [vmem] * 4,
+        join_tiles,
+        in_specs=[smem] + [vmem] * 3,
         out_specs=[vmem] * pieces,
         out_shape=[jax.ShapeDtypeStruct((count * rows, 2 * HALF), F32)] * pieces,
-        scratch_shapes=[pltpu.VMEM(wanted.shape + tables[1].shape[::2], F32)],
         name="pick",
         compiler_params=LIMITS,
-    )(wanted, *tables)
+    )(wanted, tables[0], tables[2], right)
 
 
 def start_split(skip, top_hbm, bottom_hbm, top_ref, bottom_ref, sems):

time: 36.2 us -> 36.7 us (1.014)
  Pallas kernels: 13.1 us -> 13.6 us
    pallas_call x1, Pallas kernels: 2.12 us -> 1.49 us  [prepare_early(): pl.pallas_call(early_kernel, in_specs=[hbm, hbm], out_specs=pl.BlockSpec(...]
    pallas_call x1, Pallas kernels: 3.09 us -> 3.69 us  [prepare_late(): pl.pallas_call(functools.partial(late_kernel, skipped // 2, pair, rounds)...]
    pallas_call x1 -> x2, Pallas kernels: 1.17 us -> 1.71 us  [the longest x1 0.92 us: pick_tiles(): pl.pallas_call(copy_rights, in_specs=[smem, vmem, vmem], out_specs=vmem,...]
  transfers between devices with their start and end apart: 5 -> 5, of which waited for: 2 -> 2; matrix products, arithmetic and copies ran while one was open for 0% -> 0% of each run, Pallas kernels for 19% -> 21%
where the time goes in v7:
time: 36.7 us; the launch traced here: 36.6 us
  Pallas kernels  13.6 us (37%)
  blocking collectives  13.5 us (37%)
  starting transfers between devices  6.59 us (18%)
  waiting for transfers between devices  2.13 us (6%)
  between operations  0.74 us (2%)
    all_to_all x1, blocking collectives, compute(): lax.all_to_all(terms, ('site', 'dom'), split_axis=0, concat_axis=0, tiled...  13.5 us
    ppermute x3, starting transfers between devices, shifted(): return lax.ppermute(value, 'dom', step)  5.78 us
    pallas_call x1, Pallas kernels, prepare_late(): pl.pallas_call(functools.partial(late_kernel, skipped // 2, pair, rounds)...  3.69 us
    pallas_call x2, Pallas kernels, block_likelihoods(): pl.pallas_call(functools.partial(block_kernel, len(tiles) + 1, states, pi...  3.06 us
    pallas_call x1, Pallas kernels, pack_tables(): pl.pallas_call(pack_kernel, in_specs=[hbm] * 5, out_specs=[pl.BlockSpec(m...  2.59 us
    ppermute x3, waiting for transfers between devices, shifted(): return lax.ppermute(value, 'dom', step)  1.55 us
    pallas_call x1, Pallas kernels, prepare_early(): pl.pallas_call(early_kernel, in_specs=[hbm, hbm], out_specs=pl.BlockSpec(...  1.49 us
    pallas_call x1, Pallas kernels, add_up(): pl.pallas_call(sum_kernel, in_specs=[vmem] * (5 + len(likes)), out_specs=...  1.05 us
  transfers between devices with their start and end apart: 5, of which 2 were waited for; matrix products, arithmetic and copies ran while one was open for 0% of the time, Pallas kernels for 21%

profile of v7, /device:TPU:0, one launch (start us, length us, event | category | flops | bytes accessed | tf_op | source)
XLA Modules:
  0.0 36.6 jit_solution(15572092129606330744)
XLA Ops:
  0.6 0.0 copy-start.1
  0.6 0.0 copy-start.3
  0.7 2.6 %pack.1 = (f32[32,64,128]{2,1,0:T(8,128)S(1)}, f32[61,64,61]{2,1,0:T(8,128)S(1)}) custom-call(f32[64]{0:T(128)} %rate_hbm.1, f32[61,64,61]{2,1,0:T(8,128)} %bitcast.21, f32[61,64,61]{2,1,0:T(8,128)} %bitcast.22, f32[64,61]{1,0:T(8,128)} %decay_hbm.1, f32[64,61]{1,0:T(8,128)} %weight_hbm.1), custom_call_target="tpu_custom_call" | custom-call | tf_op jit(solution)/shard_map/pack/pallas_call | solution.py:98
  3.3 0.6 %collective-permute-start = (f32[32,64,128]{2,1,0:T(8,128)S(1)}, f32[32,64,128]{2,1,0:T(8,128)S(1)}, u32[]{:S(2)}, u32[]{:S(2)}) collective-permute-start(f32[32,64,128]{2,1,0:T(8,128)S(1)} %get-tuple-element.19.own_left), channel_id=1, source_target_pairs={{0,1},{1,0},{2,3},{3,2},{4,5},{5,4},{6,7},{7,6},{8,9},{9,8},{10,11... | collective-permute-start | bytes 3145736 | tf_op jit(solution)/shard_map/ppermute | solution.py:579
  3.8 0.0 copy-done.1
  3.8 0.3 collective-permute-start.1
  4.1 0.0 copy-done.3
  4.1 2.8 %collective-permute-start.2 = (s32[8]{0:T(128)S(1)}, s32[8]{0:T(128)S(1)}, u32[]{:S(2)}, u32[]{:S(2)}) collective-permute-start(s32[8]{0:T(128)S(1)} %bitcast.25), channel_id=1, source_target_pairs={{0,2},{1,3},{2,0},{3,1},{4,6},{5,7},{6,4},{7,5},{8,10},{9,11},{10,... | collective-permute-start | bytes 104 | tf_op jit(solution)/shard_map/ppermute | solution.py:569
  6.8 1.5 %collective-permute-done.2.wanted_ref = s32[8]{0:T(128)S(1)} collective-permute-done((s32[8]{0:T(128)S(1)}, s32[8]{0:T(128)S(1)}, u32[]{:S(2)}, u32[]{:S(2)}) %collective-permute-start.2) | collective-permute-done | bytes 64 | tf_op jit(solution)/shard_map/ppermute | solution.py:569
  8.4 0.6 %collective-permute-done.1.partner_right = f32[61,64,61]{2,1,0:T(8,128)S(1)} collective-permute-done((f32[61,64,61]{2,1,0:T(8,128)S(1)}, f32[61,64,61]{2,1,0:T(8,128)S(1)}, u32[]{:S(2)}, u32[]{:S(2)}) %collective-permute-start.1) | collective-permute-done | bytes 952608 | tf_op jit(solution)/shard_map/ppermute | solution.py:579
  9.0 0.9 %rights.1.right_ref = f32[8,61,61]{2,1,0:T(8,128)S(1)} custom-call(s32[8]{0:T(128)S(1)} %collective-permute-done.2.wanted_ref, f32[61,64,61]{2,1,0:T(8,128)S(1)} %get-tuple-element.20.own_right, f32[61,64,61]{2,1,0:T(8,128)S(1)} %collective-permute-done.1.partner_right), custom_call_target="tpu_custom_call" | custom-call | tf_op jit(solution)/shard_map/rights/pallas_call | solution.py:185
  9.9 0.0 collective-permute-done.partner_left
  9.9 0.8 %pick.1 = (f32[248,128]{1,0:T(8,128)S(1)}, f32[248,128]{1,0:T(8,128)S(1)}) custom-call(s32[8]{0:T(128)S(1)} %collective-permute-done.2.wanted_ref, f32[32,64,128]{2,1,0:T(8,128)S(1)} %get-tuple-element.19.own_left, f32[32,64,128]{2,1,0:T(8,128)S(1)} %collective-permute-done.partner_left, f32[8,61,61]{2,1,0:T(8,128)S(1)} %rights.1.right_ref), custom_call_target="tpu_custom_call" | custom-call | tf_op jit(solution)/shard_map/pick/pallas_call | solution.py:193
  10.7 2.9 %collective-permute-start.4 = (f32[248,128]{1,0:T(8,128)S(1)}, f32[248,128]{1,0:T(8,128)S(1)}, u32[]{:S(2)}, u32[]{:S(2)}) collective-permute-start(f32[248,128]{1,0:T(8,128)S(1)} %get-tuple-element.27), channel_id=1, source_target_pairs={{0,2},{1,3},{2,0},{3,1},{4,6},{5,7},{6,4},{7,5},{8,10},{9,11},{10,... | collective-permute-start | bytes 380936 | tf_op jit(solution)/shard_map/ppermute | solution.py:569
  13.6 0.1 collective-permute-start.3
  13.7 0.0 copy-start.2
  13.7 1.5 %early.1.early_ref = bf16[8,2,128,256]{3,2,1,0:T(8,128)(2,1)S(1)} custom-call(f32[7808,128]{1,0:T(8,128)} %bitcast.17, f32[7808,128]{1,0:T(8,128)} %bitcast.19), custom_call_target="tpu_custom_call" | custom-call | tf_op jit(solution)/shard_map/early/pallas_call | solution.py:335
  15.2 0.0 copy-done.2
  15.2 0.0 copy-start
  15.2 3.7 %late.1 = (bf16[8,2,128,1792]{3,2,1,0:T(8,128)(2,1)S(1)}, f32[8,64,128]{2,1,0:T(8,128)S(1)}, f32[40,128]{1,0:T(8,128)S(1)}, s32[16,128]{1,0:T(8,128)S(1)}, f32[16,128]{1,0:T(8,128)S(1)}) custom-call(s32[8]{0:T(128)} %bitcast.24, s32[16]{0:T(128)} %chosen_hbm.1, f32[1997]{0:T(1024)} %lengths_hbm.1, f32[16,128]{1,0:T(8,128)S(1)} %pad_bitcast_fusion.padded_ref, ...), custom_call_target="tpu_custom_call" | custom-call | tf_op jit(solution)/shard_map/late/pallas_call | solution.py:354
  18.9 0.0 collective-permute-done.4.refs_0_
  19.0 0.0 copy-done
  19.0 1.5 %blocks.2 = (f32[16,4,128]{2,1,0:T(4,128)S(1)}, f32[4,128]{1,0:T(4,128)S(1)}) custom-call(f32[40,128]{1,0:T(8,128)S(1)} %get-tuple-element.21.aux_ref, s32[8,128]{1,0:T(8,128)S(1)} %bitcast.14, bf16[8,2,128,256]{3,2,1,0:T(8,128)(2,1)S(1)} %early.1.early_ref, bf16[8,2,128,1792]{3,2,1,0:T(8,128)(2,1)S(1)} %get-tuple-element.24.late_ref, ...), custom_call_target="tpu_custom_call" | custom-call | tf_op jit(solution)/shard_map/blocks/pallas_call | solution.py:473
  20.5 0.0 collective-permute-done.3.refs_0_
  20.5 1.6 %blocks.3 = (f32[16,4,128]{2,1,0:T(4,128)S(1)}, f32[32,4,128]{2,1,0:T(4,128)S(1)}) custom-call(f32[40,128]{1,0:T(8,128)S(1)} %get-tuple-element.21.aux_ref, s32[8,128]{1,0:T(8,128)S(1)} %bitcast.15, bf16[8,2,128,256]{3,2,1,0:T(8,128)(2,1)S(1)} %early.1.early_ref, bf16[8,2,128,1792]{3,2,1,0:T(8,128)(2,1)S(1)} %get-tuple-element.24.late_ref, ...), custom_call_target="tpu_custom_call" | custom-call | tf_op jit(solution)/shard_map/blocks/pallas_call | solution.py:473
  22.0 13.5 %all_to_all.5 = f32[32,4,128]{2,1,0:T(4,128)S(1)} all-to-all(f32[32,4,128]{2,1,0:T(4,128)S(1)} %get-tuple-element.29), channel_id=1, replica_groups=mesh['site'=8,'dom'=4] {'site','dom'}, dimensions={0} | all-to-all | bytes 131072 | tf_op jit(solution)/shard_map/all_to_all | solution.py:628
  35.5 1.0 %sums.1 = (f32[32,64]{1,0:T(8,128)}, f32[16,128]{1,0:T(8,128)}, f32[16,8,128]{2,1,0:T(8,128)}) custom-call(f32[40,128]{1,0:T(8,128)S(1)} %get-tuple-element.21.aux_ref, s32[16,128]{1,0:T(8,128)S(1)} %get-tuple-element.22.map_ref, f32[16,128]{1,0:T(8,128)S(1)} %get-tuple-element.23.lengths_ref, s32[8,128]{1,0:T(8,128)S(1)} %bitcast.16, ...), custom_call_target="tpu_custom_call" | custom-call | tf_op jit(solution)/shard_map/sums/pallas_call | solution.py:531
  (1 shorter events, 0.0 us)
Async XLA Ops:
  0.6 3.2 %copy-start.1 = (f32[64,61,61]{2,0,1:T(8,128)S(1)}, f32[64,61,61]{2,0,1:T(8,128)}, u32[]{:S(2)}) copy-start(f32[64,61,61]{2,0,1:T(8,128)} %param.14) | copy-start | bytes 2857732
  0.6 3.4 %copy-start.3 = (s32[1,8]{1,0:T(1,128)S(1)}, s32[1,8]{1,0:T(1,128)}, u32[]{:S(2)}) copy-start(s32[1,8]{1,0:T(1,128)} %param.20) | copy-start | bytes 100
  3.3 6.6 %collective-permute-start = (f32[32,64,128]{2,1,0:T(8,128)S(1)}, f32[32,64,128]{2,1,0:T(8,128)S(1)}, u32[]{:S(2)}, u32[]{:S(2)}) collective-permute-start(f32[32,64,128]{2,1,0:T(8,128)S(1)} %get-tuple-element.19.own_left), channel_id=1, source_target_pairs={{0,1},{1,0},{2,3},{3,2},{4,5},{5,4},{6,7},{7,6},{8,9},{9,8},{10,11... | collective-permute-start | bytes 3145736 | tf_op jit(solution)/shard_map/ppermute | solution.py:579
  3.8 5.1 %collective-permute-start.1 = (f32[61,64,61]{2,1,0:T(8,128)S(1)}, f32[61,64,61]{2,1,0:T(8,128)S(1)}, u32[]{:S(2)}, u32[]{:S(2)}) collective-permute-start(f32[61,64,61]{2,1,0:T(8,128)S(1)} %bitcast.23), channel_id=1, source_target_pairs={{0,1},{1,0},{2,3},{3,2},{4,5},{5,4},{6,7},{7,6},{8,9},{9,8},{10,11... | collective-permute-start | bytes 2857736 | tf_op jit(solution)/shard_map/ppermute | solution.py:579
  4.1 4.3 %collective-permute-start.2 = (s32[8]{0:T(128)S(1)}, s32[8]{0:T(128)S(1)}, u32[]{:S(2)}, u32[]{:S(2)}) collective-permute-start(s32[8]{0:T(128)S(1)} %bitcast.25), channel_id=1, source_target_pairs={{0,2},{1,3},{2,0},{3,1},{4,6},{5,7},{6,4},{7,5},{8,10},{9,11},{10,... | collective-permute-start | bytes 104 | tf_op jit(solution)/shard_map/ppermute | solution.py:569
  10.7 8.3 %collective-permute-start.4 = (f32[248,128]{1,0:T(8,128)S(1)}, f32[248,128]{1,0:T(8,128)S(1)}, u32[]{:S(2)}, u32[]{:S(2)}) collective-permute-start(f32[248,128]{1,0:T(8,128)S(1)} %get-tuple-element.27), channel_id=1, source_target_pairs={{0,2},{1,3},{2,0},{3,1},{4,6},{5,7},{6,4},{7,5},{8,10},{9,11},{10,... | collective-permute-start | bytes 380936 | tf_op jit(solution)/shard_map/ppermute | solution.py:569
  13.6 6.8 %collective-permute-start.3 = (f32[248,128]{1,0:T(8,128)S(1)}, f32[248,128]{1,0:T(8,128)S(1)}, u32[]{:S(2)}, u32[]{:S(2)}) collective-permute-start(f32[248,128]{1,0:T(8,128)S(1)} %get-tuple-element.26), channel_id=1, source_target_pairs={{0,2},{1,3},{2,0},{3,1},{4,6},{5,7},{6,4},{7,5},{8,10},{9,11},{10,... | collective-permute-start | bytes 380936 | tf_op jit(solution)/shard_map/ppermute | solution.py:569
  13.7 1.5 %copy-start.2 = (f32[1997]{0:T(1024)S(1)}, f32[1997]{0:T(1024)}, u32[]{:S(2)}) copy-start(f32[1997]{0:T(1024)} %lengths_hbm.1) | copy-start | bytes 23968
  15.2 3.7 %copy-start = (s32[1,1024]{1,0:T(1,128)S(1)}, s32[1,1024]{1,0:T(1,128)}, u32[]{:S(2)}) copy-start(s32[1,1024]{1,0:T(1,128)} %param.19) | copy-start | bytes 12292
